TPU v7x, 128 devices: a whole 4x4x4 slice. The times are simulated.
128 devices in a mesh: dp: 32 (over x, y, core), mp: 4 (over z).
Axes of the slice: x: 4, y: 4, z: 4, core: 2. Of those that a mesh axis runs over, the one named last changes fastest.
Arguments:
- slab_values: bfloat16 [128, 128, 2048], P(('dp', 'mp')), may hold values from -6 to 6
- row_ids: int32 [128, 128, 32], P(('dp', 'mp')), may hold values from 0 to 4095, as said below
- peer_counts: int32 [128, 128], P(('dp', 'mp')), may hold values from 1 to 32, as said below
- lookup_slots: int32 [32768, 16], P(('dp', 'mp')), may hold values from 0 to 4095, as said below
- labels: int32 [32768], P('dp'), may hold values 0 or 1
- sample_weight: float32 [32768], P('dp'), may hold values from 0.3 to 9
- weight_in: bfloat16 [1024, 8192], P(None, 'mp'), may hold values from -0.1875 to 0.1875
- bias_in: float32 [8192], P('mp'), may hold values from -3 to 3
- weight_out: bfloat16 [8192], P('mp'), may hold values from -0.0625 to 0.0625
- dense_accum: float32 [1024, 8192], P('dp', 'mp'), may hold values from 1e-08 to 1e-06
- table_rows: float32 [524288, 64], P(('dp', 'mp')), may hold values from -0.12 to 0.12
- table_accum: float32 [524288], P(('dp', 'mp')), may hold values from 1e-12 to 1e-05
Outputs:
- weight_new: bfloat16 [1024, 8192], P(None, 'mp')
- accum_new: float32 [1024, 8192], P('dp', 'mp')
- table_new: float32 [524288, 64], P(('dp', 'mp'))
- table_accum_new: float32 [524288], P(('dp', 'mp'))
Inputs may be any that keep to these rules, and one draw needn't show every extreme that they name: `row_ids`: the first peer_counts entries of each device's list for an owner are distinct rows of that owner's shard. `peer_counts`: some owner has 32 touched rows on every device, and some device has 32 touched rows of every owner. `lookup_slots`: below the sum of that device's peer_counts; every device has a lookup of its last touched row.
All inputs are finite; a program needn't handle non-finite values. No bound on the sum of `labels` on one device may be relied on, other than what follows from the above.
Results may differ from a plain program's by a relative error of at most 0.0034.
Values may be sent and summed in bfloat16 or wider, within the bound.
No kernel may reach another device: no remote copies, remote signals or barrier semaphores. Data moves between devices by JAX's collectives and lax.ppermute only.
A program may use at most 128 MiB of HBM per device.

v0:
```python
import functools
import math

import jax
import jax.numpy as jnp
from jax import lax
from jax.experimental import pallas as pl
from jax.experimental.pallas import tpu as pltpu
from jax.sharding import Mesh
from jax.sharding import PartitionSpec as P


DP = ("dp_0", "dp_1", "dp_2")
DP_MP = ("dp_0", "dp_1", "dp_2", "mp")

clip_norm = 1.0
dense_rate = 0.02
table_rate = 0.5
adagrad_eps = 1e-10

F32 = jnp.float32
BF16 = jnp.bfloat16
VM = pl.BlockSpec(memory_space=pltpu.VMEM)


def iota(shape, dim):
    return lax.broadcasted_iota(jnp.int32, shape, dim)


def dot_f32(a, b, dims=(((1,), (0,)), ((), ()))):
    return lax.dot_general(a, b, dims, preferred_element_type=F32)


def hot_rows(counts_ref, lookups_ref):
    owners = counts_ref.shape[1]
    features = lookups_ref.shape[0]
    spread = jnp.broadcast_to(counts_ref[...].astype(F32), (owners, owners))
    at, of = iota((owners, owners), 0), iota((owners, owners), 1)
    ends = jnp.sum(jnp.where(of <= at, spread, 0.0), axis=1, keepdims=True)
    starts = ends - jnp.sum(jnp.where(of == at, spread, 0.0), axis=1, keepdims=True)
    hots, slots = [], []
    for f in range(features):
        q = lookups_ref[f : f + 1, :].astype(F32)
        match = (q >= starts) & (q < ends)
        hots.append(jnp.where(match, 1.0, 0.0))
        slots.append(q - jnp.sum(jnp.where(match, starts, 0.0), axis=0, keepdims=True))
    return hots, slots


def gather_kernel(counts_ref, lookups_ref, slab_ref, out_ref):
    features, batch = lookups_ref.shape
    halfway = slab_ref.shape[1] // 2
    hots, slots = hot_rows(counts_ref, lookups_ref)
    inner = jnp.concatenate([jnp.where(s >= 16.0, s - 16.0, s) for s in slots], axis=0).T
    halves = jnp.concatenate([slab_ref[:, :halfway], slab_ref[:, halfway:]], axis=0)
    low_lane = iota((batch, 128), 1) < 64
    for pair in range(features // 2):
        both = []
        for parity in range(2):
            f = 2 * pair + parity
            upper = slots[f] >= 16.0
            hot = jnp.concatenate(
                [jnp.where(upper, 0.0, hots[f]), jnp.where(upper, hots[f], 0.0)], axis=0
            ).astype(BF16)
            rows = dot_f32(hot, halves, (((0,), (0,)), ((), ())))
            place = jnp.broadcast_to(inner[:, f : f + 1], (batch, 128))
            block = jnp.floor(place * 0.5)
            found = rows[:, :128]
            for k in range(1, 8):
                found = jnp.where(block == float(k), rows[:, 128 * k : 128 * (k + 1)], found)
            swap = place - 2.0 * block != float(parity)
            both.append(jnp.where(swap, pltpu.roll(found, 64, 1), found))
        out_ref[:, 128 * pair : 128 * (pair + 1)] = jnp.where(low_lane, both[0], both[1]).astype(BF16)


def gather_rows(counts, lookups_t, slab):
    features, batch = lookups_t.shape
    return pl.pallas_call(
        gather_kernel,
        out_shape=jax.ShapeDtypeStruct((batch, features * 64), BF16),
        in_specs=[VM, VM, VM],
        out_specs=VM,
        name="gather_rows",
        compiler_params=pltpu.CompilerParams(vmem_limit_bytes=16 * 2**20),
        cost_estimate=pl.CostEstimate(flops=6 * 10**9, transcendentals=0, bytes_accessed=2 * 10**6),
    )(counts, lookups_t, slab)


def slot_kernel(
    counts_ref, lookups_ref, ids_ref, own_ref, a_ref, b_ref, c_ref, dense_ref, out_ref, value_ref, at_ref
):
    owners = counts_ref.shape[1]
    capacity = ids_ref.shape[1]
    features, batch = lookups_ref.shape
    spread = jnp.broadcast_to(counts_ref[...].astype(F32), (owners, owners))
    at, of = iota((owners, owners), 0), iota((owners, owners), 1)
    ends = jnp.sum(jnp.where(of <= at, spread, 0.0), axis=1, keepdims=True)
    starts = ends - jnp.sum(jnp.where(of == at, spread, 0.0), axis=1, keepdims=True)
    moves = iota((owners, 1), 0).astype(F32) * float(capacity) - starts
    indices = []
    for f in range(features):
        q = lookups_ref[f : f + 1, :].astype(F32)
        match = (q >= starts) & (q < ends)
        indices.append(q + jnp.sum(jnp.where(match, moves, 0.0), axis=0, keepdims=True))
        at_ref[0:1, batch * f : batch * (f + 1)] = jnp.floor(indices[f] * 0.5)
    index = jnp.concatenate(indices, axis=0)
    odd = (index - 2.0 * jnp.floor(index * 0.5)).T
    low_lane = iota((batch, 128), 1) < 64
    lane_odd = jnp.where(low_lane, 0.0, 1.0)
    for pair in range(features // 2):
        cols = slice(128 * pair, 128 * (pair + 1))
        total = own_ref[:, cols]
        for piece_ref in (a_ref, b_ref, c_ref):
            total = total + piece_ref[:, cols].astype(F32)
        turned = pltpu.roll(total, 64, 1)
        for parity in range(2):
            f = 2 * pair + parity
            rows = jnp.where(low_lane, total, turned) if parity == 0 else jnp.where(low_lane, turned, total)
            rows = jnp.where(jnp.broadcast_to(odd[:, f : f + 1], (batch, 128)) == lane_odd, rows, 0.0)
            high = rows.astype(BF16)
            value_ref[batch * f : batch * (f + 1), 0:128] = high
            value_ref[batch * f : batch * (f + 1), 128:256] = (rows - high.astype(F32)).astype(BF16)
    block = 512
    each = block * 2 // capacity
    where = jnp.broadcast_to(at_ref[...], (block, features * batch))
    lines = iota((block, features * batch), 0).astype(F32)

    def part(m, square):
        hot = jnp.where(lines == where - (m * block).astype(F32), 1.0, 0.0).astype(BF16)
        both = dot_f32(hot, value_ref[...])
        sums = both[:, 0:128] + both[:, 128:256]
        first = pl.multiple_of(m * each, each)
        out_ref[pl.ds(first, each), 0 : capacity // 2, :] = sums.astype(BF16).reshape(each, capacity // 2, 128)
        return square + jnp.sum(jnp.sum(sums * sums, axis=1, keepdims=True), axis=0, keepdims=True)

    square = lax.fori_loop(0, owners // each, part, dense_ref[0:1, 0:1])
    top = square.astype(BF16).astype(F32)
    mid = (square - top).astype(BF16).astype(F32)
    end = square - top - mid
    ids = ids_ref[...]
    lane = iota((owners, 128 - 2 * capacity), 1)
    tail = jnp.where(lane == 0, top, jnp.where(lane == 1, mid, jnp.where(lane == 2, end, 0.0)))
    info = jnp.concatenate([(ids >> 8).astype(F32), (ids & 255).astype(F32), tail], axis=1)
    out_ref[:, capacity // 2 :, :] = jnp.broadcast_to(info[:, None, :], (owners, 8, 128)).astype(BF16)


def table_kernel(rate, eps, clip, arrived_ref, table_ref, accum_ref, table_out, accum_out, scale_out, acc_ref):
    sources, lines, _ = arrived_ref.shape
    half = lines - 8
    capacity = 2 * half
    rows = table_ref.shape[1]
    blocks = rows // 256
    every = sources * half
    info = arrived_ref[:, half:, :].reshape(sources * 8, 128)
    squares = jnp.sum(info.astype(F32)[:, 2 * capacity : 2 * capacity + 3], axis=0, keepdims=True)
    total = jnp.sum(squares, axis=1, keepdims=True) * 0.125
    scale = clip / jnp.maximum(jnp.sqrt(total), clip)
    scale_out[...] = jnp.broadcast_to(scale, scale_out.shape)
    share = jnp.where(iota((sources * 8, every), 0) >> 3 == iota((sources * 8, every), 1) // half, 0.125, 0.0)
    spread_info = dot_f32(info, share.astype(BF16), (((0,), (0,)), ((), ())))
    slot = iota((capacity, every), 0)
    line = iota((capacity, every), 1) & (half - 1)
    inside_at = iota((256, every), 0).astype(F32)
    turned = arrived_ref[:, :half, :].reshape(every, 128).astype(F32).T
    acc = None
    for parity in range(2):
        mine = slot == 2 * line + parity
        block = jnp.sum(jnp.where(mine, spread_info[0:capacity], 0.0), axis=0, keepdims=True)
        inside = jnp.sum(jnp.where(mine, spread_info[capacity : 2 * capacity], 0.0), axis=0, keepdims=True)
        piece = turned[64 * parity : 64 * (parity + 1), :]
        hot = jnp.where(inside_at == inside, 1.0, 0.0).astype(BF16)
        spread = jnp.concatenate([jnp.where(block == float(k), piece, 0.0).astype(BF16) for k in range(blocks)], axis=0)
        part = dot_f32(spread, hot, (((1,), (1,)), ((), ())))
        acc = part if acc is None else acc + part
    acc_ref[...] = acc
    for k in range(blocks):
        received = scale * acc_ref[64 * k : 64 * (k + 1), :]
        cols = slice(256 * k, 256 * (k + 1))
        accum = accum_ref[:, cols] + jnp.sum(received * received, axis=0, keepdims=True) * (1.0 / 64.0)
        accum_out[:, cols] = accum
        table_out[:, cols] = table_ref[:, cols] - rate * received / (jnp.sqrt(accum) + eps)


def footprint(shapes):
    return sum(math.prod(s.shape) * jnp.dtype(s.dtype).itemsize for s in shapes)


def call(kernel, outs, flops, args, scratch=(), spare=8):
    shapes = tuple(jax.ShapeDtypeStruct(s, t) for s, t in outs)
    held = footprint(args) + footprint(shapes) + footprint(scratch)
    res = pl.pallas_call(
        kernel,
        out_shape=shapes,
        in_specs=[VM] * len(args),
        out_specs=tuple(VM for _ in shapes),
        scratch_shapes=list(scratch),
        compiler_params=pltpu.CompilerParams(vmem_limit_bytes=held + spare * 2**20),
        cost_estimate=pl.CostEstimate(flops=flops, transcendentals=0, bytes_accessed=2 * 10**6),
    )(*args)
    return res


SHIFTS = (1, 3, 2)


def spot(axis, shift):
    return lax.rem(lax.axis_index(axis) + shift, 4)


def sigmoid(x):
    return 0.5 * jnp.tanh(0.5 * x) + 0.5


def forward_kernel(chunks, *refs):
    ins, (w_ref, bias_ref, out_w_ref) = refs[:chunks], refs[chunks : chunks + 3]
    slope_ref, hidden_ref, logit_ref, turned_ref = refs[chunks + 3 :]
    rows = ins[0].shape[0]
    width = w_ref.shape[1]
    for k in range(chunks):
        turned_ref[:, rows * k : rows * (k + 1)] = ins[k][...].T

    def columns(n, carry):
        cols = pl.ds(pl.multiple_of(n * 256, 256), 256)
        w = w_ref[:, cols]
        out_w = out_w_ref[:, cols].astype(F32)
        for k in range(chunks):
            act = dot_f32(ins[k][...], w) + bias_ref[:, cols]
            sigma = sigmoid(act)
            hidden_ref[rows * k : rows * (k + 1), cols] = (act * sigma).astype(BF16)
            slope_ref[rows * k : rows * (k + 1), cols] = out_w * sigma * (1.0 + act * (1.0 - sigma))
        return carry

    lax.fori_loop(0, width // 256, columns, 0)
    out_w = jnp.broadcast_to(out_w_ref[...], (16, width))
    for k in range(chunks):
        part = dot_f32(out_w, hidden_ref[rows * k : rows * (k + 1), :], (((1,), (1,)), ((), ())))
        at = rows * k
        logit_ref[at // 256 : at // 256 + 1, at % 256 : at % 256 + rows] = part[0:1, :]


def forward(chunks, w, bias, out_w):
    rows, depth = chunks[0].shape
    width = w.shape[1]
    n = len(chunks)
    total = n * rows
    outs = [((total, width), F32), ((total, width), BF16), ((total // 256, 256), F32), ((depth, total), BF16)]
    return call(functools.partial(forward_kernel, n), outs, total * 10**7, (*chunks, w, bias, out_w))


ORDER = (0, 3, 1, 2)
PARTNERS = ((0, 1, 2, 3), (2, 0, 3, 1), (1, 3, 0, 2), (3, 2, 1, 0))


def slope_kernel(*refs):
    slopes, hiddens = refs[0:3], refs[3:6]
    own_ref, prev_ref, next_ref, far_ref, labels_ref, weight_ref = refs[6:12]
    dact_ref, other_ref, sums_ref = refs[12:]
    rows, width = slopes[0].shape
    spans = ((0, 0), (1, 0), (1, rows), (2, 0))
    half = width // 2
    core = lax.axis_index("dp_2")
    dlogits = []
    for k in range(4):
        at = spot("mp", ORDER[k])
        logit = (own_ref[k : k + 1, :] + far_ref[PARTNERS[3][k] : PARTNERS[3][k] + 1, :]) + (
            prev_ref[PARTNERS[1][k] : PARTNERS[1][k] + 1, :] + next_ref[PARTNERS[2][k] : PARTNERS[2][k] + 1, :]
        )
        label = labels_ref[pl.ds(at, 1), :].astype(F32)
        dlogits.append(weight_ref[pl.ds(at, 1), :] * (sigmoid(logit) - label))
    rows_form = jnp.concatenate(dlogits + [jnp.zeros((4, rows), F32)], axis=0)
    cols_form = rows_form.T
    for k in range(4):
        which, start = spans[k]
        col = cols_form[:, k : k + 1]
        dact_ref[rows * k : rows * (k + 1), :] = (slopes[which][start : start + rows, :] * col).astype(BF16)
    other_ref[...] = dact_ref[:, pl.ds(pl.multiple_of((1 - core) * half, half), half)]
    ones = jnp.ones((16, rows), BF16)
    bias_sum = jnp.zeros((16, width), F32)
    out_sum = jnp.zeros((16, width), F32)
    for k in range(4):
        bias_sum = bias_sum + dot_f32(ones, dact_ref[rows * k : rows * (k + 1), :])
        d = dlogits[k]
        top = d.astype(BF16)
        rest = (d - top.astype(F32)).astype(BF16)
        pick = iota((16, rows), 0)
        left = jnp.where(pick == 0, top.astype(F32), jnp.where(pick == 1, rest.astype(F32), 0.0)).astype(BF16)
        which, start = spans[k]
        out_sum = out_sum + dot_f32(left, hiddens[which][start : start + rows, :])
    total = jnp.sum(out_sum, axis=0, keepdims=True)
    sums_ref[...] = jnp.concatenate([bias_sum[0:1, :], total], axis=0)


def back_kernel(dact_ref, w_ref, own_ref, *outs):
    rows = own_ref.shape[0]
    for k, target in enumerate((own_ref, *outs)):
        part = dot_f32(dact_ref[rows * k : rows * (k + 1), :], w_ref[...], (((1,), (1,)), ((), ())))
        target[...] = part.astype(target.dtype)


def spot_on(first, core, shift):
    x, y = lax.axis_index("dp_0"), lax.axis_index("dp_1")
    along = x * (1 - core) + y * core if first else y * (1 - core) + x * core
    return lax.rem(along + shift, 4)


def chip_rows(core, outer, inner, size):
    return pl.multiple_of((outer * (4 - 3 * core) + inner * (1 + 3 * core)) * size, size)


def grad_kernel(*refs):
    turned, (dact_ref, far_dact_ref) = refs[0:6], refs[6:8]
    outs, acc_ref = refs[8:12], refs[12]
    depth = turned[0].shape[0]
    half = far_dact_ref.shape[1]
    spans = ((0, 256), (256, 512), (768, 256))
    core = lax.axis_index("dp_2")
    local = pl.ds(pl.multiple_of(core * half, half), half)

    def rows(x, carry):
        at = pl.ds(pl.multiple_of(x * 256, 256), 256)
        part = None
        for i, (s, n) in enumerate(spans):
            p = dot_f32(turned[i][at, :], dact_ref[s : s + n, local])
            p = p + dot_f32(turned[i + 3][at, :], far_dact_ref[s : s + n, :])
            part = p if part is None else part + p
        acc_ref[at, :] = part
        return carry

    lax.fori_loop(0, depth // 256, rows, 0)
    size = depth // 16
    for target, shift in zip(outs, (0, *SHIFTS)):
        for t in range(4):
            at = chip_rows(core, spot_on(True, core, shift), t, size)
            target[size * t : size * (t + 1), :] = acc_ref[pl.ds(at, size), :].astype(target.dtype)


def middle_kernel(own_ref, a_ref, b_ref, c_ref, *refs):
    outs, acc_ref = refs[:4], refs[4]
    size = outs[0].shape[0]
    core = lax.axis_index("dp_2")
    acc_ref[...] = own_ref[...] + a_ref[...].astype(F32) + b_ref[...].astype(F32) + c_ref[...].astype(F32)
    for target, shift in zip(outs, (0, *SHIFTS)):
        at = pl.multiple_of(spot_on(False, core, shift) * size, size)
        target[...] = acc_ref[pl.ds(at, size), :].astype(target.dtype)


def last_kernel(own_ref, a_ref, b_ref, c_ref, sums_ref, narrow_ref, mine_ref, other_ref, square_ref, full_ref):
    core = lax.axis_index("dp_2")
    total = own_ref[...] + a_ref[...].astype(F32) + b_ref[...].astype(F32) + c_ref[...].astype(F32)
    extra = jnp.sum(sums_ref[...], axis=0, keepdims=True)
    square = jnp.sum(jnp.sum(total * total, axis=1, keepdims=True), axis=0, keepdims=True)
    square = square + jnp.sum(extra * extra, axis=1, keepdims=True)
    square_ref[...] = jnp.broadcast_to(square, square_ref.shape)
    full_ref[...] = total
    narrow_ref[...] = total.astype(BF16)
    per = total.shape[0] // 2
    mine_ref[...] = full_ref[pl.ds(pl.multiple_of(core * per, per), per), :]
    other_ref[...] = full_ref[pl.ds(pl.multiple_of((1 - core) * per, per), per), :]


def pack_kernel(*refs):
    rows = refs[0].shape[0]
    for k in range(4):
        refs[4][rows * k : rows * (k + 1), :] = refs[k][...]


def weight_kernel(scale_ref, w_ref, near_ref, far_ref, rows_ref, mine_ref, theirs_ref, *refs):
    stacks, (w_out_ref, accum_ref) = refs[:8], refs[8:]
    core = lax.axis_index("dp_2")
    scale = scale_ref[0:1, 0:1]
    _, per, _ = near_ref.shape
    half = stacks[0].shape[1]
    for side, c in ((0, core), (1, 1 - core)):
        cols = pl.ds(pl.multiple_of(c * half, half), half)
        for i in range(4):
            outer = spot_on(True, c, (4 - i) % 4)

            def chip(j, carry, stack=stacks[4 * side + i], outer=outer, c=c, cols=cols):
                inner = spot_on(False, c, lax.rem(4 - j, 4))
                at = chip_rows(c, outer, inner, 1)
                for held_ref, r in ((near_ref, core), (far_ref, 1 - core)):
                    rows = pl.ds(pl.multiple_of((at * 2 + r) * per, per), per)
                    grad = scale * stack[pl.ds(pl.multiple_of((j * 2 + r) * per, per), per), :].astype(F32)
                    accum = held_ref[at, :, cols].astype(F32) + grad * grad
                    w = w_ref[rows, cols].astype(F32)
                    w_out_ref[rows, cols] = (w - dense_rate * grad / (jnp.sqrt(accum) + adagrad_eps)).astype(BF16)
                return carry

            lax.fori_loop(0, 4, chip, 0)
        grad = scale * (mine_ref, theirs_ref)[side][...]
        accum_ref[:, cols] = rows_ref[:, cols] + grad * grad


def cross(x, first, shift):
    moves = []
    for i in range(32):
        a, b, c = i // 8, i // 2 % 4, i % 2
        a, b = ((a + shift) % 4, b) if (c == 0) == first else (a, (b + shift) % 4)
        moves.append((i, a * 8 + b * 2 + c))
    return lax.ppermute(x, DP, moves)


def send(x, axis, shift):
    n = lax.axis_size(axis)
    return lax.ppermute(x, axis, [(i, (i + shift) % n) for i in range(n)])


def around(x, axis):
    return [send(x, axis, s) for s in SHIFTS]


def inner(
    slab_values,
    row_ids,
    peer_counts,
    lookup_slots,
    labels,
    sample_weight,
    weight_in,
    bias_in,
    weight_out,
    dense_accum,
    table_rows,
    table_accum,
):
    batch, features = lookup_slots.shape
    depth, width = weight_in.shape
    half = width // 2
    lookups_t = lookup_slots.T
    pooled = gather_rows(peer_counts, lookups_t, slab_values[0])
    before, after = send(pooled, "mp", 1), send(pooled, "mp", 3)
    chips = ("dp_0", "dp_1")
    narrow = dense_accum.astype(BF16)
    near = lax.all_to_all(jnp.broadcast_to(narrow[None], (16, *narrow.shape)), chips, 0, 0, tiled=True)
    distant = send(near, "dp_2", 1)
    bias = bias_in.reshape(1, width)
    out_w = weight_out.reshape(1, width)
    far_low, far_high = send(before[: batch // 2], "mp", 1), send(after[batch // 2 :], "mp", 3)
    slope_0, hidden_0, logit_0, turned_0 = forward([pooled], weight_in, bias, out_w)
    slope_1, hidden_1, logit_1, turned_1 = forward([before, after], weight_in, bias, out_w)
    slope_2, hidden_2, logit_2, turned_2 = forward([far_low, far_high], weight_in, bias, out_w)
    turned = [turned_0, turned_1, turned_2]
    turned = turned + [send(t, "dp_2", 1) for t in turned]
    logits = jnp.concatenate([logit_0, logit_1, logit_2], axis=0)
    logit_before, logit_after, logit_far = around(logits, "mp")
    dact, other, sums = call(
        slope_kernel,
        [((4 * batch, width), BF16), ((4 * batch, half), BF16), ((2, width), F32)],
        2 * 10**9,
        (
            slope_0,
            slope_1,
            slope_2,
            hidden_0,
            hidden_1,
            hidden_2,
            logits,
            logit_before,
            logit_after,
            logit_far,
            labels.reshape(4, batch),
            sample_weight.reshape(4, batch),
        ),
    )
    far_dact = send(other, "dp_2", 1)
    own, to_before, to_after, to_far = call(
        back_kernel, [((batch, depth), F32)] + [((batch, depth), BF16)] * 3, 4 * 10**9, (dact, weight_in)
    )
    from_after, from_before, from_far = send(to_before, "mp", 3), send(to_after, "mp", 1), send(to_far, "mp", 2)
    stage = [((depth // 4, half), F32)] + [((depth // 4, half), BF16)] * 3
    keep, *give = call(grad_kernel, stage, 8 * 10**9, (*turned, dact, far_dact), [pltpu.VMEM((depth, half), F32)])
    got = [cross(g, True, s) for g, s in zip(give, SHIFTS)]
    stage = [((depth // 16, half), F32)] + [((depth // 16, half), BF16)] * 3
    keep, *give = call(middle_kernel, stage, 10**8, (keep, *got), [pltpu.VMEM((depth // 4, half), F32)])
    got = [cross(g, False, s) for g, s in zip(give, SHIFTS)]
    sums = lax.all_to_all(sums.reshape(32, 1, 2 * width // 32), DP, 0, 0, tiled=True).reshape(32, -1)
    narrow, mine, others, square = call(
        last_kernel,
        [((depth // 16, half), BF16)] + [((depth // 32, half), F32)] * 2 + [((8, 128), F32)],
        10**8,
        (keep, *got, sums),
        [pltpu.VMEM((depth // 16, half), F32)],
    )
    theirs = send(others, "dp_2", 1)
    parts = {s: cross(narrow, False, s) for s in SHIFTS}
    pack = call(pack_kernel, [((depth // 4, half), BF16)], 10**8, (narrow, parts[1], parts[2], parts[3]))[0]
    stacks = {s: cross(pack, True, s) for s in SHIFTS}
    stacks = [pack, stacks[1], stacks[2], stacks[3]]
    stacks = stacks + [send(g, "dp_2", 1) for g in stacks]
    peers, capacity = row_ids.shape[1:]
    outgoing = call(
        slot_kernel,
        [((peers, capacity // 2 + 8, 128), BF16)],
        8 * 10**9,
        (peer_counts, lookups_t, row_ids[0], own, from_before, from_after, from_far, square),
        [pltpu.VMEM((features * batch, 256), BF16), pltpu.VMEM((1, features * batch), F32)],
        24,
    )[0]
    arrived = lax.all_to_all(outgoing, DP_MP, 0, 0, tiled=True)
    table_t, accum_t, scale = call(
        functools.partial(table_kernel, table_rate, adagrad_eps, clip_norm),
        [(table_rows.shape[::-1], F32), ((1, table_rows.shape[0]), F32), ((8, 128), F32)],
        6 * 10**9,
        (arrived, table_rows.T, table_accum.reshape(1, -1)),
        [pltpu.VMEM((table_rows.shape[0] // 4, 256), F32)],
        32,
    )
    weight_new, accum_new = call(
        weight_kernel,
        [((depth, width), BF16), (dense_accum.shape, F32)],
        10**9,
        (scale, weight_in, near, distant, dense_accum, mine, theirs, *stacks),
    )
    return (weight_new, accum_new, table_t.T, accum_t.reshape(-1))


def solution(mesh):
    torus = Mesh(mesh.devices.reshape(4, 4, 2, mesh.shape["mp"]), ("dp_0", "dp_1", "dp_2", "mp"))
    placed = (
        P(DP_MP, None, None),
        P(DP_MP, None, None),
        P(DP_MP, None),
        P(DP_MP, None),
        P(DP),
        P(DP),
        P(None, "mp"),
        P("mp"),
        P("mp"),
        P(DP, "mp"),
        P(DP_MP, None),
        P(DP_MP),
    )
    return jax.shard_map(
        inner,
        mesh=torus,
        in_specs=placed,
        out_specs=(P(None, "mp"), P(DP, "mp"), P(DP_MP, None), P(DP_MP)),
        check_vma=False,
    )
```

profile of v0, /device:TPU:1, one launch (start us, length us, event | category | flops | bytes accessed | tf_op | source)
XLA Modules:
  0.0 198.7 jit_solution(2691838168410224596)
XLA Ops:
  0.6 1.0 copy-done.20
  1.7 0.7 copy-done.22
  3.1 3.3 %gather_rows.1.refs_0_ = bf16[256,1024]{1,0:T(8,128)(2,1)S(1)} custom-call(s32[1,128]{1,0:T(1,128)S(1)} %copy-done.26, s32[16,256]{1,0:T(8,128)S(1)} %bitcast.14, bf16[128,2048]{1,0:T(8,128)(2,1)S(1)} %bitcast.13), custom_call_target="tpu_custom_call" | custom-call | flops 6000000000 | bytes 2000000 | tf_op jit(solution)/shard_map/gather_rows/pallas_call | solution.py:78
  6.3 2.5 %collective-permute-start = (bf16[256,1024]{1,0:T(8,128)(2,1)S(1)}, bf16[256,1024]{1,0:T(8,128)(2,1)S(1)}, u32[]{:S(2)}, u32[]{:S(2)}) collective-permute-start(bf16[256,1024]{1,0:T(8,128)(2,1)S(1)} %gather_rows.1.refs_0_), channel_id=1, source_target_pairs={{0,1},{1,2},{2,3},{3,0},{4,5},{5,6},{6,7},{7,4},{8,9},{9,10},{10,1... | collective-permute-start | bytes 1572872 | tf_op jit(solution)/shard_map/ppermute | solution.py:405
  8.9 2.2 %collective-permute-start.1 = (bf16[256,1024]{1,0:T(8,128)(2,1)S(1)}, bf16[256,1024]{1,0:T(8,128)(2,1)S(1)}, u32[]{:S(2)}, u32[]{:S(2)}) collective-permute-start(bf16[256,1024]{1,0:T(8,128)(2,1)S(1)} %gather_rows.1.refs_0_), channel_id=1, source_target_pairs={{0,3},{1,0},{2,1},{3,2},{4,7},{5,4},{6,5},{7,6},{8,11},{9,8},{10,9... | collective-permute-start | bytes 1572872 | tf_op jit(solution)/shard_map/ppermute | solution.py:405
  11.1 3.5 %shard_map.147 = (f32[256,2048]{1,0:T(8,128)S(1)}, bf16[256,2048]{1,0:T(8,128)(2,1)S(1)}, f32[1,256]{1,0:T(1,128)S(1)}, bf16[1024,256]{1,0:T(8,128)(2,1)S(1)}) custom-call(bf16[256,1024]{1,0:T(8,128)(2,1)S(1)} %gather_rows.1.refs_0_, bf16[1024,2048]{1,0:T(8,128)(2,1)S(1)} %copy-done, f32[1,2048]{1,0:T(1,128)S(1)} %bitcast.17, ...), custom_call_target="tpu_custom_call" | custom-call | flops 2560000000 | bytes 2000000 | tf_op jit(solution)/shard_map/pallas_call | solution.py:191
  14.6 1.0 copy-done.10
  15.6 7.0 %collective-permute-done.refs_0_ = bf16[256,1024]{1,0:T(8,128)(2,1)S(1)} collective-permute-done((bf16[256,1024]{1,0:T(8,128)(2,1)S(1)}, bf16[256,1024]{1,0:T(8,128)(2,1)S(1)}, u32[]{:S(2)}, u32[]{:S(2)}) %collective-permute-start) | collective-permute-done | bytes 524320 | tf_op jit(solution)/shard_map/ppermute | solution.py:405
  22.7 2.7 %collective-permute-start.3 = (bf16[128,1024]{1,0:T(8,128)(2,1)S(1)}, bf16[128,1024]{1,0:T(8,128)(2,1)S(1)}, u32[]{:S(2)}, u32[]{:S(2)}) collective-permute-start(bf16[128,1024]{1,0:T(8,128)(2,1)S(1)} %slice.9), channel_id=1, source_target_pairs={{0,3},{1,0},{2,1},{3,2},{4,7},{5,4},{6,5},{7,6},{8,11},{9,8},{10,9... | collective-permute-start | bytes 786440 | tf_op jit(solution)/shard_map/ppermute | solution.py:405
  25.5 6.5 %shard_map.148 = (f32[512,2048]{1,0:T(8,128)S(1)}, bf16[512,2048]{1,0:T(8,128)(2,1)S(1)}, f32[2,256]{1,0:T(2,128)S(1)}, bf16[1024,512]{1,0:T(8,128)(2,1)}) custom-call(bf16[256,1024]{1,0:T(8,128)(2,1)S(1)} %collective-permute-done.refs_0_, bf16[256,1024]{1,0:T(8,128)(2,1)S(1)} %collective-permute-done.1.refs_1_, bf16[1024,2048]{1,0:T(8,128)(2,1)S(1)} %copy-done, ...), custom_call_target="tpu_custom_call" | custom-call | flops 5120000000 | bytes 2000000 | tf_op jit(solution)/shard_map/pallas_call | solution.py:191
  31.9 2.0 %copy-done.3 = f32[512,2048]{1,0:T(8,128)} copy-done((f32[512,2048]{1,0:T(8,128)}, f32[512,2048]{1,0:T(8,128)S(1)}, u32[]{:S(2)}) %copy-start.3) | copy-done | bytes 4194328
  34.0 3.7 %shard_map.149 = (f32[256,2048]{1,0:T(8,128)S(1)}, bf16[256,2048]{1,0:T(8,128)(2,1)S(1)}, f32[1,256]{1,0:T(1,128)S(1)}, bf16[1024,256]{1,0:T(8,128)(2,1)S(1)}) custom-call(bf16[128,1024]{1,0:T(8,128)(2,1)S(1)} %collective-permute-done.2.refs_0_, bf16[128,1024]{1,0:T(8,128)(2,1)S(1)} %collective-permute-done.3.refs_1_, bf16[1024,2048]{1,0:T(8,128)(2,1)S(1)} %copy-done, ...), custom_call_target="tpu_custom_call" | custom-call | flops 2560000000 | bytes 2000000 | tf_op jit(solution)/shard_map/pallas_call | solution.py:191
  37.7 1.3 copy-done.7
  39.0 1.0 copy-done.12
  40.1 2.7 %collective-permute-start.5 = (f32[4,256]{1,0:T(4,128)S(1)}, f32[4,256]{1,0:T(4,128)S(1)}, u32[]{:S(2)}, u32[]{:S(2)}) collective-permute-start(f32[4,256]{1,0:T(4,128)S(1)} %pad_maximum_fusion.refs_6_), channel_id=1, source_target_pairs={{0,3},{1,0},{2,1},{3,2},{4,7},{5,4},{6,5},{7,6},{8,11},{9,8},{10,9... | collective-permute-start | bytes 12296 | tf_op jit(solution)/shard_map/ppermute | solution.py:405
  42.8 1.0 collective-permute-done.4.refs_7_
  43.7 3.0 %collective-permute-done.6.refs_9_ = f32[4,256]{1,0:T(4,128)S(1)} collective-permute-done((f32[4,256]{1,0:T(4,128)S(1)}, f32[4,256]{1,0:T(4,128)S(1)}, u32[]{:S(2)}, u32[]{:S(2)}) %collective-permute-start.6) | collective-permute-done | bytes 4128 | tf_op jit(solution)/shard_map/ppermute | solution.py:405
  46.7 2.2 %copy-done.4 = f32[512,2048]{1,0:T(8,128)S(1)} copy-done((f32[512,2048]{1,0:T(8,128)S(1)}, f32[512,2048]{1,0:T(8,128)}, u32[]{:S(2)}) %copy-start.4) | copy-done | bytes 4194328
  48.9 1.6 copy-done.6
  50.5 1.6 copy-done.8
  52.1 1.2 copy-done.11
  53.3 1.2 copy-done.13
  54.5 3.2 %shard_map.150 = (bf16[1024,2048]{1,0:T(8,128)(2,1)S(1)}, bf16[1024,1024]{1,0:T(8,128)(2,1)}, f32[2,2048]{1,0:T(2,128)S(1)}) custom-call(f32[256,2048]{1,0:T(8,128)S(1)} %get-tuple-element.40.refs_0_, f32[512,2048]{1,0:T(8,128)S(1)} %copy-done.4, f32[256,2048]{1,0:T(8,128)S(1)} %copy-done.8, bf16[256,2048]{1,0:T(8,128)(2,1)S(1)} %copy-done.11, ...), custom_call_target="tpu_custom_call" | custom-call | flops 2000000000 | bytes 2000000 | tf_op jit(solution)/shard_map/pallas_call | solution.py:191
  57.8 2.0 %copy-done.16 = bf16[1024,2048]{1,0:T(8,128)(2,1)} copy-done((bf16[1024,2048]{1,0:T(8,128)(2,1)}, bf16[1024,2048]{1,0:T(8,128)(2,1)S(1)}, u32[]{:S(2)}) %copy-start.16) | copy-done | bytes 4194328
  59.8 3.5 %collective-permute-start.13 = (bf16[1024,1024]{1,0:T(8,128)(2,1)}, bf16[1024,1024]{1,0:T(8,128)(2,1)}, u32[]{:S(2)}, u32[]{:S(2)}) collective-permute-start(bf16[1024,1024]{1,0:T(8,128)(2,1)} %get-tuple-element.57), channel_id=1, source_target_pairs={{0,4},{4,0},{1,5},{5,1},{2,6},{6,2},{3,7},{7,3},{8,12},{12,8},{9,1... | collective-permute-start | bytes 6291464 | tf_op jit(solution)/shard_map/ppermute | solution.py:405
  63.8 1.6 broadcast_in_dim.2
  65.4 6.8 %all-to-all-start.2 = ((bf16[16,32,2048]{2,1,0:T(8,128)(2,1)}), bf16[16,32,2048]{2,1,0:T(8,128)(2,1)S(1)}, u32[]{:S(2)}, u32[]{:S(2)}) async-start(bf16[16,32,2048]{2,1,0:T(8,128)(2,1)} %broadcast_in_dim.2), calls=%async_computation.2 | async-start | bytes 4194304 | tf_op jit(solution)/shard_map/all_to_all | solution.py:434
  72.2 2.2 %copy-done.17 = bf16[1024,2048]{1,0:T(8,128)(2,1)S(1)} copy-done((bf16[1024,2048]{1,0:T(8,128)(2,1)S(1)}, bf16[1024,2048]{1,0:T(8,128)(2,1)}, u32[]{:S(2)}) %copy-start.17) | copy-done | bytes 4194328
  74.4 7.9 %shard_map.152 = (f32[256,1024]{1,0:T(8,128)S(1)}, bf16[256,1024]{1,0:T(8,128)(2,1)S(1)}, bf16[256,1024]{1,0:T(8,128)(2,1)S(1)}, bf16[256,1024]{1,0:T(8,128)(2,1)S(1)}) custom-call(bf16[1024,256]{1,0:T(8,128)(2,1)S(1)} %get-tuple-element.54.refs_0_, bf16[1024,512]{1,0:T(8,128)(2,1)} %get-tuple-element.55.refs_1_, ...), custom_call_target="tpu_custom_call" | custom-call | flops 8000000000 | bytes 2000000 | tf_op jit(solution)/shard_map/pallas_call | solution.py:191
  82.3 1.4 collective-permute-start.14
  83.7 1.3 collective-permute-start.15
  85.0 1.7 collective-permute-start.16
  86.7 5.3 %shard_map.151 = (f32[256,1024]{1,0:T(8,128)S(1)}, bf16[256,1024]{1,0:T(8,128)(2,1)}, bf16[256,1024]{1,0:T(8,128)(2,1)}, bf16[256,1024]{1,0:T(8,128)(2,1)}) custom-call(bf16[1024,2048]{1,0:T(8,128)(2,1)S(1)} %copy-done.18, bf16[1024,2048]{1,0:T(8,128)(2,1)S(1)} %copy-done.1), custom_call_target="tpu_custom_call" | custom-call | flops 4000000000 | bytes 2000000 | tf_op jit(solution)/shard_map/pallas_call | solution.py:191
  92.0 1.0 copy-done.28
  93.0 2.7 %collective-permute-start.8 = (bf16[256,1024]{1,0:T(8,128)(2,1)}, bf16[256,1024]{1,0:T(8,128)(2,1)}, u32[]{:S(2)}, u32[]{:S(2)}) collective-permute-start(bf16[256,1024]{1,0:T(8,128)(2,1)} %get-tuple-element.52), channel_id=1, source_target_pairs={{0,3},{1,0},{2,1},{3,2},{4,7},{5,4},{6,5},{7,6},{8,11},{9,8},{10,9... | collective-permute-start | bytes 1572872 | tf_op jit(solution)/shard_map/ppermute | solution.py:405
  95.7 8.7 %collective-permute-done.14.a_ref = bf16[256,1024]{1,0:T(8,128)(2,1)S(1)} collective-permute-done((bf16[256,1024]{1,0:T(8,128)(2,1)S(1)}, bf16[256,1024]{1,0:T(8,128)(2,1)S(1)}, u32[]{:S(2)}, u32[]{:S(2)}) %collective-permute-start.14) | collective-permute-done | bytes 524320 | tf_op jit(solution)/shard_map/ppermute | solution.py:400
  104.4 4.2 %collective-permute-done.15.b_ref = bf16[256,1024]{1,0:T(8,128)(2,1)S(1)} collective-permute-done((bf16[256,1024]{1,0:T(8,128)(2,1)S(1)}, bf16[256,1024]{1,0:T(8,128)(2,1)S(1)}, u32[]{:S(2)}, u32[]{:S(2)}) %collective-permute-start.15) | collective-permute-done | bytes 524320 | tf_op jit(solution)/shard_map/ppermute | solution.py:400
  108.6 1.7 collective-permute-done.16.c_ref
  110.7 0.9 collective-permute-start.17
  111.6 1.9 collective-permute-start.18
  113.5 2.8 %collective-permute-done.17.a_ref = bf16[64,1024]{1,0:T(8,128)(2,1)S(1)} collective-permute-done((bf16[64,1024]{1,0:T(8,128)(2,1)S(1)}, bf16[64,1024]{1,0:T(8,128)(2,1)S(1)}, u32[]{:S(2)}, u32[]{:S(2)}) %collective-permute-start.17) | collective-permute-done | bytes 131104 | tf_op jit(solution)/shard_map/ppermute | solution.py:400
  116.2 1.0 collective-permute-start.19
  117.8 8.2 %all-to-all-start = ((f32[32,1,128]{2,1,0:T(1,128)}), f32[32,1,128]{2,1,0:T(1,128)S(1)}, u32[]{:S(2)}, u32[]{:S(2)}) async-start(f32[32,1,128]{2,1,0:T(1,128)} %bitcast.4), calls=%async_computation | async-start | bytes 32768 | tf_op jit(solution)/shard_map/all_to_all | solution.py:476
  126.7 6.2 %all-to-all-done = f32[32,1,128]{2,1,0:T(1,128)S(1)} async-done(((f32[32,1,128]{2,1,0:T(1,128)}), f32[32,1,128]{2,1,0:T(1,128)S(1)}, u32[]{:S(2)}, u32[]{:S(2)}) %all-to-all-start) | async-done | bytes 16416 | tf_op jit(solution)/shard_map/all_to_all | solution.py:476
  133.8 1.2 copy-done.29
  135.0 9.4 %shard_map.155 = bf16[128,24,128]{2,1,0:T(8,128)(2,1)} custom-call(s32[1,128]{1,0:T(1,128)S(1)} %copy-done.27, s32[16,256]{1,0:T(8,128)S(1)} %bitcast.15, s32[128,32]{1,0:T(8,128)S(1)} %bitcast.10, f32[256,1024]{1,0:T(8,128)S(1)} %copy-done.29, bf16[256,1024]{1,0:T(8,128)(2,1)} %collective-permute-done.7.a_ref, ...), custom_call_target="tpu_custom_call" | custom-call | flops 8000000000 | bytes 2000000 | tf_op jit(solution)/shard_map/pallas_call | solution.py:191
  144.4 5.2 %all-to-all-start.1 = ((bf16[128,24,128]{2,1,0:T(8,128)(2,1)}), bf16[128,24,128]{2,1,0:T(8,128)(2,1)}, u32[]{:S(2)}, u32[]{:S(2)}) async-start(bf16[128,24,128]{2,1,0:T(8,128)(2,1)} %shard_map.155), calls=%async_computation.1 | async-start | bytes 1572864 | tf_op jit(solution)/shard_map/all_to_all | solution.py:499
  149.6 1.4 collective-permute-start.22
  151.0 2.4 %collective-permute-start.23 = (bf16[64,1024]{1,0:T(8,128)(2,1)S(1)}, bf16[64,1024]{1,0:T(8,128)(2,1)S(1)}, u32[]{:S(2)}, u32[]{:S(2)}) collective-permute-start(bf16[64,1024]{1,0:T(8,128)(2,1)S(1)} %get-tuple-element.71.refs_0_), channel_id=1, source_target_pairs={{0,16},{4,68},{8,24},{12,76},{16,0},{20,84},{24,8},{28,92},{32,48}... | collective-permute-start | bytes 393224 | tf_op jit(solution)/shard_map/ppermute | solution.py:400
  153.5 1.2 collective-permute-start.24
  154.6 7.7 %collective-permute-done.22.refs_1_ = bf16[64,1024]{1,0:T(8,128)(2,1)S(1)} collective-permute-done((bf16[64,1024]{1,0:T(8,128)(2,1)S(1)}, bf16[64,1024]{1,0:T(8,128)(2,1)S(1)}, u32[]{:S(2)}, u32[]{:S(2)}) %collective-permute-start.22) | collective-permute-done | bytes 131104 | tf_op jit(solution)/shard_map/ppermute | solution.py:400
  162.3 1.7 collective-permute-done.23.refs_2_
  164.0 1.3 collective-permute-start.25
  165.4 2.5 %collective-permute-start.26 = (bf16[256,1024]{1,0:T(8,128)(2,1)S(1)}, bf16[256,1024]{1,0:T(8,128)(2,1)}, u32[]{:S(2)}, u32[]{:S(2)}) collective-permute-start(bf16[256,1024]{1,0:T(8,128)(2,1)S(1)} %shard_map.157.refs_0_), channel_id=1, source_target_pairs={{0,64},{4,20},{8,72},{12,28},{16,80},{20,4},{24,88},{28,12},{32,96... | collective-permute-start | bytes 1572872 | tf_op jit(solution)/shard_map/ppermute | solution.py:400
  167.9 1.1 collective-permute-start.27
  169.0 1.1 collective-permute-start.21
  170.1 1.2 collective-permute-done.21.theirs_ref
  172.4 1.3 collective-permute-done.25.refs_1_
  173.6 1.3 collective-permute-start.29
  175.0 5.5 %collective-permute-done.26.refs_2_ = bf16[256,1024]{1,0:T(8,128)(2,1)} collective-permute-done((bf16[256,1024]{1,0:T(8,128)(2,1)S(1)}, bf16[256,1024]{1,0:T(8,128)(2,1)}, u32[]{:S(2)}, u32[]{:S(2)}) %collective-permute-start.26) | collective-permute-done | bytes 524320 | tf_op jit(solution)/shard_map/ppermute | solution.py:400
  180.5 1.1 collective-permute-start.30
  181.6 1.2 copy-done.19
  182.8 5.5 %shard_map.156 = (f32[64,4096]{1,0:T(8,128)}, f32[1,4096]{1,0:T(1,128)}, f32[8,128]{1,0:T(8,128)S(1)}) custom-call(bf16[128,24,128]{2,1,0:T(8,128)(2,1)} %all-to-all-done.1.arrived_ref, f32[64,4096]{1,0:T(8,128)S(1)} %bitcast.12, f32[1,4096]{1,0:T(1,128)S(1)} %bitcast.16), custom_call_target="tpu_custom_call" | custom-call | flops 6000000000 | bytes 2000000 | tf_op jit(solution)/shard_map/pallas_call | solution.py:191
  188.4 10.3 %shard_map.158 = (bf16[1024,2048]{1,0:T(8,128)(2,1)}, f32[32,2048]{1,0:T(8,128)}) custom-call(f32[8,128]{1,0:T(8,128)S(1)} %get-tuple-element.68.scale_ref, bf16[1024,2048]{1,0:T(8,128)(2,1)S(1)} %copy-done.2, bf16[16,32,2048]{2,1,0:T(8,128)(2,1)S(1)} %all-to-all-done.2.near_ref, bf16[16,32,2048]{2,1,0:T(8,128)(2,1)} %collective-permute-done.20.far_ref, ...), custom_call_target="tpu_custom_call" | custom-call | flops 1000000000 | bytes 2000000 | tf_op jit(solution)/shard_map/pallas_call | solution.py:191
  (97 shorter events, 5.1 us)
Async XLA Ops:
  0.6 1.0 copy-start.20
  3.0 8.0 %copy-start.31 = (bf16[2048]{0:T(1024)(128)(2,1)S(1)}, bf16[2048]{0:T(1024)(128)(2,1)}, u32[]{:S(2)}) copy-start(bf16[2048]{0:T(1024)(128)(2,1)} %param.20) | copy-start | bytes 12292
  3.0 8.0 %copy-start = (bf16[1024,2048]{1,0:T(8,128)(2,1)S(1)}, bf16[1024,2048]{1,0:T(8,128)(2,1)}, u32[]{:S(2)}) copy-start(bf16[1024,2048]{1,0:T(8,128)(2,1)} %w_ref.3) | copy-start | bytes 12582916
  3.1 8.0 %copy-start.25 = (f32[2048]{0:T(1024)S(1)}, f32[2048]{0:T(1024)}, u32[]{:S(2)}) copy-start(f32[2048]{0:T(1024)} %param.19) | copy-start | bytes 24580
  6.3 16.3 %collective-permute-start = (bf16[256,1024]{1,0:T(8,128)(2,1)S(1)}, bf16[256,1024]{1,0:T(8,128)(2,1)S(1)}, u32[]{:S(2)}, u32[]{:S(2)}) collective-permute-start(bf16[256,1024]{1,0:T(8,128)(2,1)S(1)} %gather_rows.1.refs_0_), channel_id=1, source_target_pairs={{0,1},{1,2},{2,3},{3,0},{4,5},{5,6},{6,7},{7,4},{8,9},{9,10},{10,1... | collective-permute-start | bytes 1572872 | tf_op jit(solution)/shard_map/ppermute | solution.py:405
  8.9 13.8 %collective-permute-start.1 = (bf16[256,1024]{1,0:T(8,128)(2,1)S(1)}, bf16[256,1024]{1,0:T(8,128)(2,1)S(1)}, u32[]{:S(2)}, u32[]{:S(2)}) collective-permute-start(bf16[256,1024]{1,0:T(8,128)(2,1)S(1)} %gather_rows.1.refs_0_), channel_id=1, source_target_pairs={{0,3},{1,0},{2,1},{3,2},{4,7},{5,4},{6,5},{7,6},{8,11},{9,8},{10,9... | collective-permute-start | bytes 1572872 | tf_op jit(solution)/shard_map/ppermute | solution.py:405
  14.6 1.0 copy-start.10
  22.6 11.3 %collective-permute-start.2 = (bf16[128,1024]{1,0:T(8,128)(2,1)S(1)}, bf16[128,1024]{1,0:T(8,128)(2,1)S(1)}, u32[]{:S(2)}, u32[]{:S(2)}) collective-permute-start(bf16[128,1024]{1,0:T(8,128)(2,1)S(1)} %slice.8), channel_id=1, source_target_pairs={{0,1},{1,2},{2,3},{3,0},{4,5},{5,6},{6,7},{7,4},{8,9},{9,10},{10,1... | collective-permute-start | bytes 786440 | tf_op jit(solution)/shard_map/ppermute | solution.py:405
  22.7 11.2 %collective-permute-start.3 = (bf16[128,1024]{1,0:T(8,128)(2,1)S(1)}, bf16[128,1024]{1,0:T(8,128)(2,1)S(1)}, u32[]{:S(2)}, u32[]{:S(2)}) collective-permute-start(bf16[128,1024]{1,0:T(8,128)(2,1)S(1)} %slice.9), channel_id=1, source_target_pairs={{0,3},{1,0},{2,1},{3,2},{4,7},{5,4},{6,5},{7,6},{8,11},{9,8},{10,9... | collective-permute-start | bytes 786440 | tf_op jit(solution)/shard_map/ppermute | solution.py:405
  31.9 2.0 %copy-start.3 = (f32[512,2048]{1,0:T(8,128)}, f32[512,2048]{1,0:T(8,128)S(1)}, u32[]{:S(2)}) copy-start(f32[512,2048]{1,0:T(8,128)S(1)} %get-tuple-element.41.refs_1_) | copy-start | bytes 12582916
  33.9 3.7 %copy-start.5 = (bf16[512,2048]{1,0:T(8,128)(2,1)}, bf16[512,2048]{1,0:T(8,128)(2,1)S(1)}, u32[]{:S(2)}) copy-start(bf16[512,2048]{1,0:T(8,128)(2,1)S(1)} %get-tuple-element.44.refs_4_) | copy-start | bytes 6291460
  33.9 8.8 %copy-start.32 = (s32[1024]{0:T(1024)S(1)}, s32[1024]{0:T(1024)}, u32[]{:S(2)}) copy-start(s32[1024]{0:T(1024)} %param.16) | copy-start | bytes 12292
  33.9 8.8 %copy-start.33 = (f32[1024]{0:T(1024)S(1)}, f32[1024]{0:T(1024)}, u32[]{:S(2)}) copy-start(f32[1024]{0:T(1024)} %param.17) | copy-start | bytes 12292
  37.7 1.3 copy-start.7
  39.0 1.0 copy-start.12
  40.0 3.7 %collective-permute-start.4 = (f32[4,256]{1,0:T(4,128)S(1)}, f32[4,256]{1,0:T(4,128)S(1)}, u32[]{:S(2)}, u32[]{:S(2)}) collective-permute-start(f32[4,256]{1,0:T(4,128)S(1)} %pad_maximum_fusion.refs_6_), channel_id=1, source_target_pairs={{0,1},{1,2},{2,3},{3,0},{4,5},{5,6},{6,7},{7,4},{8,9},{9,10},{10,1... | collective-permute-start | bytes 12296 | tf_op jit(solution)/shard_map/ppermute | solution.py:405
  40.1 3.7 %collective-permute-start.5 = (f32[4,256]{1,0:T(4,128)S(1)}, f32[4,256]{1,0:T(4,128)S(1)}, u32[]{:S(2)}, u32[]{:S(2)}) collective-permute-start(f32[4,256]{1,0:T(4,128)S(1)} %pad_maximum_fusion.refs_6_), channel_id=1, source_target_pairs={{0,3},{1,0},{2,1},{3,2},{4,7},{5,4},{6,5},{7,6},{8,11},{9,8},{10,9... | collective-permute-start | bytes 12296 | tf_op jit(solution)/shard_map/ppermute | solution.py:405
  42.7 4.0 %collective-permute-start.6 = (f32[4,256]{1,0:T(4,128)S(1)}, f32[4,256]{1,0:T(4,128)S(1)}, u32[]{:S(2)}, u32[]{:S(2)}) collective-permute-start(f32[4,256]{1,0:T(4,128)S(1)} %pad_maximum_fusion.refs_6_), channel_id=1, source_target_pairs={{0,2},{1,3},{2,0},{3,1},{4,6},{5,7},{6,4},{7,5},{8,10},{9,11},{10,... | collective-permute-start | bytes 12296 | tf_op jit(solution)/shard_map/ppermute | solution.py:405
  46.7 2.2 %copy-start.4 = (f32[512,2048]{1,0:T(8,128)S(1)}, f32[512,2048]{1,0:T(8,128)}, u32[]{:S(2)}) copy-start(f32[512,2048]{1,0:T(8,128)} %copy-done.3) | copy-start | bytes 12582916
  48.9 1.6 copy-start.6
  50.5 1.6 copy-start.8
  52.1 1.2 copy-start.11
  53.3 1.2 copy-start.13
  54.5 9.3 %copy-start.9 = (f32[32,2048]{1,0:T(8,128)S(1)}, f32[32,2048]{1,0:T(8,128)}, u32[]{:S(2)}) copy-start(f32[32,2048]{1,0:T(8,128)} %rows_ref.1) | copy-start | bytes 786436
  57.7 2.0 %copy-start.16 = (bf16[1024,2048]{1,0:T(8,128)(2,1)}, bf16[1024,2048]{1,0:T(8,128)(2,1)S(1)}, u32[]{:S(2)}) copy-start(bf16[1024,2048]{1,0:T(8,128)(2,1)S(1)} %get-tuple-element.49.dact_ref.refs_6_) | copy-start | bytes 12582916
  59.8 12.4 %collective-permute-start.13 = (bf16[1024,1024]{1,0:T(8,128)(2,1)}, bf16[1024,1024]{1,0:T(8,128)(2,1)}, u32[]{:S(2)}, u32[]{:S(2)}) collective-permute-start(bf16[1024,1024]{1,0:T(8,128)(2,1)} %get-tuple-element.57), channel_id=1, source_target_pairs={{0,4},{4,0},{1,5},{5,1},{2,6},{6,2},{3,7},{7,3},{8,12},{12,8},{9,1... | collective-permute-start | bytes 6291464 | tf_op jit(solution)/shard_map/ppermute | solution.py:405
  63.3 8.9 %collective-permute-start.11 = (bf16[1024,512]{1,0:T(8,128)(2,1)}, bf16[1024,512]{1,0:T(8,128)(2,1)}, u32[]{:S(2)}, u32[]{:S(2)}) collective-permute-start(bf16[1024,512]{1,0:T(8,128)(2,1)} %get-tuple-element.55.refs_1_), channel_id=1, source_target_pairs={{0,4},{4,0},{1,5},{5,1},{2,6},{6,2},{3,7},{7,3},{8,12},{12,8},{9,1... | collective-permute-start | bytes 3145736 | tf_op jit(solution)/shard_map/ppermute | solution.py:405
  63.3 8.9 %collective-permute-start.10 = (bf16[1024,256]{1,0:T(8,128)(2,1)S(1)}, bf16[1024,256]{1,0:T(8,128)(2,1)}, u32[]{:S(2)}, u32[]{:S(2)}) collective-permute-start(bf16[1024,256]{1,0:T(8,128)(2,1)S(1)} %get-tuple-element.54.refs_0_), channel_id=1, source_target_pairs={{0,4},{4,0},{1,5},{5,1},{2,6},{6,2},{3,7},{7,3},{8,12},{12,8},{9,1... | collective-permute-start | bytes 1572872 | tf_op jit(solution)/shard_map/ppermute | solution.py:405
  63.8 8.4 %collective-permute-start.12 = (bf16[1024,256]{1,0:T(8,128)(2,1)S(1)}, bf16[1024,256]{1,0:T(8,128)(2,1)}, u32[]{:S(2)}, u32[]{:S(2)}) collective-permute-start(bf16[1024,256]{1,0:T(8,128)(2,1)S(1)} %get-tuple-element.56.refs_2_), channel_id=1, source_target_pairs={{0,4},{4,0},{1,5},{5,1},{2,6},{6,2},{3,7},{7,3},{8,12},{12,8},{9,1... | collective-permute-start | bytes 1572872 | tf_op jit(solution)/shard_map/ppermute | solution.py:405
  65.4 52.5 %all-to-all-start.2 = ((bf16[16,32,2048]{2,1,0:T(8,128)(2,1)}), bf16[16,32,2048]{2,1,0:T(8,128)(2,1)S(1)}, u32[]{:S(2)}, u32[]{:S(2)}) async-start(bf16[16,32,2048]{2,1,0:T(8,128)(2,1)} %broadcast_in_dim.2), calls=%async_computation.2 | async-start | bytes 4194304 | tf_op jit(solution)/shard_map/all_to_all | solution.py:434
  72.2 2.2 %copy-start.17 = (bf16[1024,2048]{1,0:T(8,128)(2,1)S(1)}, bf16[1024,2048]{1,0:T(8,128)(2,1)}, u32[]{:S(2)}) copy-start(bf16[1024,2048]{1,0:T(8,128)(2,1)} %copy-done.16) | copy-start | bytes 12582916
  74.4 12.3 %copy-start.1 = (bf16[1024,2048]{1,0:T(8,128)(2,1)S(1)}, bf16[1024,2048]{1,0:T(8,128)(2,1)}, u32[]{:S(2)}) copy-start(bf16[1024,2048]{1,0:T(8,128)(2,1)} %w_ref.3) | copy-start | bytes 12582916
  74.4 12.3 %copy-start.18 = (bf16[1024,2048]{1,0:T(8,128)(2,1)S(1)}, bf16[1024,2048]{1,0:T(8,128)(2,1)}, u32[]{:S(2)}) copy-start(bf16[1024,2048]{1,0:T(8,128)(2,1)} %copy-done.16) | copy-start | bytes 12582916
  82.3 22.1 %collective-permute-start.14 = (bf16[256,1024]{1,0:T(8,128)(2,1)S(1)}, bf16[256,1024]{1,0:T(8,128)(2,1)S(1)}, u32[]{:S(2)}, u32[]{:S(2)}) collective-permute-start(bf16[256,1024]{1,0:T(8,128)(2,1)S(1)} %get-tuple-element.59), channel_id=1, source_target_pairs={{0,32},{4,12},{8,40},{12,20},{16,48},{20,28},{24,56},{28,4},{32,64... | collective-permute-start | bytes 1572872 | tf_op jit(solution)/shard_map/ppermute | solution.py:400
  83.7 24.9 %collective-permute-start.15 = (bf16[256,1024]{1,0:T(8,128)(2,1)S(1)}, bf16[256,1024]{1,0:T(8,128)(2,1)S(1)}, u32[]{:S(2)}, u32[]{:S(2)}) collective-permute-start(bf16[256,1024]{1,0:T(8,128)(2,1)S(1)} %get-tuple-element.60), channel_id=1, source_target_pairs={{0,96},{4,28},{8,104},{12,4},{16,112},{20,12},{24,120},{28,20},{32... | collective-permute-start | bytes 1572872 | tf_op jit(solution)/shard_map/ppermute | solution.py:400
  85.0 25.3 %collective-permute-start.16 = (bf16[256,1024]{1,0:T(8,128)(2,1)S(1)}, bf16[256,1024]{1,0:T(8,128)(2,1)S(1)}, u32[]{:S(2)}, u32[]{:S(2)}) collective-permute-start(bf16[256,1024]{1,0:T(8,128)(2,1)S(1)} %get-tuple-element.61), channel_id=1, source_target_pairs={{0,64},{4,20},{8,72},{12,28},{16,80},{20,4},{24,88},{28,12},{32,96... | collective-permute-start | bytes 1572872 | tf_op jit(solution)/shard_map/ppermute | solution.py:400
  93.0 33.0 %copy-start.30 = (s32[1,128,32]{1,2,0:T(8,128)S(1)}, s32[1,128,32]{1,2,0:T(8,128)}, u32[]{:S(2)}) copy-start(s32[1,128,32]{1,2,0:T(8,128)} %param.13) | copy-start | bytes 49156
  93.0 40.8 %copy-start.23 = (s32[256,16]{0,1:T(8,128)S(1)}, s32[256,16]{0,1:T(8,128)}, u32[]{:S(2)}) copy-start(s32[256,16]{0,1:T(8,128)} %param.15) | copy-start | bytes 49156
  93.0 40.8 %copy-start.27 = (s32[1,128]{1,0:T(1,128)S(1)}, s32[1,128]{1,0:T(1,128)}, u32[]{:S(2)}) copy-start(s32[1,128]{1,0:T(1,128)} %counts_ref.3) | copy-start | bytes 1540
  93.0 40.7 %collective-permute-start.7 = (bf16[256,1024]{1,0:T(8,128)(2,1)}, bf16[256,1024]{1,0:T(8,128)(2,1)}, u32[]{:S(2)}, u32[]{:S(2)}) collective-permute-start(bf16[256,1024]{1,0:T(8,128)(2,1)} %get-tuple-element.51), channel_id=1, source_target_pairs={{0,1},{1,2},{2,3},{3,0},{4,5},{5,6},{6,7},{7,4},{8,9},{9,10},{10,1... | collective-permute-start | bytes 1572872 | tf_op jit(solution)/shard_map/ppermute | solution.py:405
  93.0 40.7 %collective-permute-start.8 = (bf16[256,1024]{1,0:T(8,128)(2,1)}, bf16[256,1024]{1,0:T(8,128)(2,1)}, u32[]{:S(2)}, u32[]{:S(2)}) collective-permute-start(bf16[256,1024]{1,0:T(8,128)(2,1)} %get-tuple-element.52), channel_id=1, source_target_pairs={{0,3},{1,0},{2,1},{3,2},{4,7},{5,4},{6,5},{7,6},{8,11},{9,8},{10,9... | collective-permute-start | bytes 1572872 | tf_op jit(solution)/shard_map/ppermute | solution.py:405
  104.4 29.4 %collective-permute-start.9 = (bf16[256,1024]{1,0:T(8,128)(2,1)}, bf16[256,1024]{1,0:T(8,128)(2,1)}, u32[]{:S(2)}, u32[]{:S(2)}) collective-permute-start(bf16[256,1024]{1,0:T(8,128)(2,1)} %get-tuple-element.53), channel_id=1, source_target_pairs={{0,2},{1,3},{2,0},{3,1},{4,6},{5,7},{6,4},{7,5},{8,10},{9,11},{10,... | collective-permute-start | bytes 1572872 | tf_op jit(solution)/shard_map/ppermute | solution.py:405
  110.7 5.5 %collective-permute-start.17 = (bf16[64,1024]{1,0:T(8,128)(2,1)S(1)}, bf16[64,1024]{1,0:T(8,128)(2,1)S(1)}, u32[]{:S(2)}, u32[]{:S(2)}) collective-permute-start(bf16[64,1024]{1,0:T(8,128)(2,1)S(1)} %get-tuple-element.63), channel_id=1, source_target_pairs={{0,8},{4,36},{8,16},{12,44},{16,24},{20,52},{24,0},{28,60},{32,40}... | collective-permute-start | bytes 393224 | tf_op jit(solution)/shard_map/ppermute | solution.py:400
  111.6 14.5 %collective-permute-start.18 = (bf16[64,1024]{1,0:T(8,128)(2,1)S(1)}, bf16[64,1024]{1,0:T(8,128)(2,1)S(1)}, u32[]{:S(2)}, u32[]{:S(2)}) collective-permute-start(bf16[64,1024]{1,0:T(8,128)(2,1)S(1)} %get-tuple-element.64), channel_id=1, source_target_pairs={{0,24},{4,100},{8,0},{12,108},{16,8},{20,116},{24,16},{28,124},{32... | collective-permute-start | bytes 393224 | tf_op jit(solution)/shard_map/ppermute | solution.py:400
  116.2 16.7 %collective-permute-start.19 = (bf16[64,1024]{1,0:T(8,128)(2,1)S(1)}, bf16[64,1024]{1,0:T(8,128)(2,1)S(1)}, u32[]{:S(2)}, u32[]{:S(2)}) collective-permute-start(bf16[64,1024]{1,0:T(8,128)(2,1)S(1)} %get-tuple-element.65), channel_id=1, source_target_pairs={{0,16},{4,68},{8,24},{12,76},{16,0},{20,84},{24,8},{28,92},{32,48}... | collective-permute-start | bytes 393224 | tf_op jit(solution)/shard_map/ppermute | solution.py:400
  117.8 15.1 %all-to-all-start = ((f32[32,1,128]{2,1,0:T(1,128)}), f32[32,1,128]{2,1,0:T(1,128)S(1)}, u32[]{:S(2)}, u32[]{:S(2)}) async-start(f32[32,1,128]{2,1,0:T(1,128)} %bitcast.4), calls=%async_computation | async-start | bytes 32768 | tf_op jit(solution)/shard_map/all_to_all | solution.py:476
  126.1 62.2 %collective-permute-start.20 = (bf16[16,32,2048]{2,1,0:T(8,128)(2,1)S(1)}, bf16[16,32,2048]{2,1,0:T(8,128)(2,1)}, u32[]{:S(2)}, u32[]{:S(2)}) collective-permute-start(bf16[16,32,2048]{2,1,0:T(8,128)(2,1)S(1)} %all-to-all-done.2.near_ref), channel_id=1, source_target_pairs={{0,4},{4,0},{1,5},{5,1},{2,6},{6,2},{3,7},{7,3},{8,12},{12,8},{9,1... | collective-permute-start | bytes 6291464 | tf_op jit(solution)/shard_map/ppermute | solution.py:405
  133.8 1.2 copy-start.29
  144.4 37.2 %copy-start.24 = (f32[4096]{0:T(1024)S(1)}, f32[4096]{0:T(1024)}, u32[]{:S(2)}) copy-start(f32[4096]{0:T(1024)} %param.23) | copy-start | bytes 49156
  144.4 37.2 %all-to-all-start.1 = ((bf16[128,24,128]{2,1,0:T(8,128)(2,1)}), bf16[128,24,128]{2,1,0:T(8,128)(2,1)}, u32[]{:S(2)}, u32[]{:S(2)}) async-start(bf16[128,24,128]{2,1,0:T(8,128)(2,1)} %shard_map.155), calls=%async_computation.1 | async-start | bytes 1572864 | tf_op jit(solution)/shard_map/all_to_all | solution.py:499
  149.6 12.7 %collective-permute-start.22 = (bf16[64,1024]{1,0:T(8,128)(2,1)S(1)}, bf16[64,1024]{1,0:T(8,128)(2,1)S(1)}, u32[]{:S(2)}, u32[]{:S(2)}) collective-permute-start(bf16[64,1024]{1,0:T(8,128)(2,1)S(1)} %get-tuple-element.71.refs_0_), channel_id=1, source_target_pairs={{0,8},{4,36},{8,16},{12,44},{16,24},{20,52},{24,0},{28,60},{32,40}... | collective-permute-start | bytes 393224 | tf_op jit(solution)/shard_map/ppermute | solution.py:400
  151.0 13.0 %collective-permute-start.23 = (bf16[64,1024]{1,0:T(8,128)(2,1)S(1)}, bf16[64,1024]{1,0:T(8,128)(2,1)S(1)}, u32[]{:S(2)}, u32[]{:S(2)}) collective-permute-start(bf16[64,1024]{1,0:T(8,128)(2,1)S(1)} %get-tuple-element.71.refs_0_), channel_id=1, source_target_pairs={{0,16},{4,68},{8,24},{12,76},{16,0},{20,84},{24,8},{28,92},{32,48}... | collective-permute-start | bytes 393224 | tf_op jit(solution)/shard_map/ppermute | solution.py:400
  153.5 10.5 %collective-permute-start.24 = (bf16[64,1024]{1,0:T(8,128)(2,1)S(1)}, bf16[64,1024]{1,0:T(8,128)(2,1)S(1)}, u32[]{:S(2)}, u32[]{:S(2)}) collective-permute-start(bf16[64,1024]{1,0:T(8,128)(2,1)S(1)} %get-tuple-element.71.refs_0_), channel_id=1, source_target_pairs={{0,24},{4,100},{8,0},{12,108},{16,8},{20,116},{24,16},{28,124},{32... | collective-permute-start | bytes 393224 | tf_op jit(solution)/shard_map/ppermute | solution.py:400
  164.0 9.6 %collective-permute-start.25 = (bf16[256,1024]{1,0:T(8,128)(2,1)S(1)}, bf16[256,1024]{1,0:T(8,128)(2,1)S(1)}, u32[]{:S(2)}, u32[]{:S(2)}) collective-permute-start(bf16[256,1024]{1,0:T(8,128)(2,1)S(1)} %shard_map.157.refs_0_), channel_id=1, source_target_pairs={{0,32},{4,12},{8,40},{12,20},{16,48},{20,28},{24,56},{28,4},{32,64... | collective-permute-start | bytes 1572872 | tf_op jit(solution)/shard_map/ppermute | solution.py:400
  165.4 15.1 %collective-permute-start.26 = (bf16[256,1024]{1,0:T(8,128)(2,1)S(1)}, bf16[256,1024]{1,0:T(8,128)(2,1)}, u32[]{:S(2)}, u32[]{:S(2)}) collective-permute-start(bf16[256,1024]{1,0:T(8,128)(2,1)S(1)} %shard_map.157.refs_0_), channel_id=1, source_target_pairs={{0,64},{4,20},{8,72},{12,28},{16,80},{20,4},{24,88},{28,12},{32,96... | collective-permute-start | bytes 1572872 | tf_op jit(solution)/shard_map/ppermute | solution.py:400
  167.9 13.7 %collective-permute-start.27 = (bf16[256,1024]{1,0:T(8,128)(2,1)S(1)}, bf16[256,1024]{1,0:T(8,128)(2,1)}, u32[]{:S(2)}, u32[]{:S(2)}) collective-permute-start(bf16[256,1024]{1,0:T(8,128)(2,1)S(1)} %shard_map.157.refs_0_), channel_id=1, source_target_pairs={{0,96},{4,28},{8,104},{12,4},{16,112},{20,12},{24,120},{28,20},{32... | collective-permute-start | bytes 1572872 | tf_op jit(solution)/shard_map/ppermute | solution.py:400
  169.0 2.3 %collective-permute-start.21 = (f32[32,1024]{1,0:T(8,128)}, f32[32,1024]{1,0:T(8,128)S(1)}, u32[]{:S(2)}, u32[]{:S(2)}) collective-permute-start(f32[32,1024]{1,0:T(8,128)} %copy-done.21), channel_id=1, source_target_pairs={{0,4},{4,0},{1,5},{5,1},{2,6},{6,2},{3,7},{7,3},{8,12},{12,8},{9,1... | collective-permute-start | bytes 393224 | tf_op jit(solution)/shard_map/ppermute | solution.py:405
  172.0 16.3 %collective-permute-start.28 = (bf16[256,1024]{1,0:T(8,128)(2,1)S(1)}, bf16[256,1024]{1,0:T(8,128)(2,1)}, u32[]{:S(2)}, u32[]{:S(2)}) collective-permute-start(bf16[256,1024]{1,0:T(8,128)(2,1)S(1)} %shard_map.157.refs_0_), channel_id=1, source_target_pairs={{0,4},{4,0},{1,5},{5,1},{2,6},{6,2},{3,7},{7,3},{8,12},{12,8},{9,1... | collective-permute-start | bytes 1572872 | tf_op jit(solution)/shard_map/ppermute | solution.py:405
  173.6 14.7 %collective-permute-start.29 = (bf16[256,1024]{1,0:T(8,128)(2,1)S(1)}, bf16[256,1024]{1,0:T(8,128)(2,1)}, u32[]{:S(2)}, u32[]{:S(2)}) collective-permute-start(bf16[256,1024]{1,0:T(8,128)(2,1)S(1)} %collective-permute-done.25.refs_1_), channel_id=1, source_target_pairs={{0,4},{4,0},{1,5},{5,1},{2,6},{6,2},{3,7},{7,3},{8,12},{12,8},{9,1... | collective-permute-start | bytes 1572872 | tf_op jit(solution)/shard_map/ppermute | solution.py:405
  180.5 7.9 %collective-permute-start.30 = (bf16[256,1024]{1,0:T(8,128)(2,1)}, bf16[256,1024]{1,0:T(8,128)(2,1)}, u32[]{:S(2)}, u32[]{:S(2)}) collective-permute-start(bf16[256,1024]{1,0:T(8,128)(2,1)} %collective-permute-done.26.refs_2_), channel_id=1, source_target_pairs={{0,4},{4,0},{1,5},{5,1},{2,6},{6,2},{3,7},{7,3},{8,12},{12,8},{9,1... | collective-permute-start | bytes 1572872 | tf_op jit(solution)/shard_map/ppermute | solution.py:405
  181.6 6.8 %collective-permute-start.31 = (bf16[256,1024]{1,0:T(8,128)(2,1)}, bf16[256,1024]{1,0:T(8,128)(2,1)}, u32[]{:S(2)}, u32[]{:S(2)}) collective-permute-start(bf16[256,1024]{1,0:T(8,128)(2,1)} %collective-permute-done.27.refs_3_), channel_id=1, source_target_pairs={{0,4},{4,0},{1,5},{5,1},{2,6},{6,2},{3,7},{7,3},{8,12},{12,8},{9,1... | collective-permute-start | bytes 1572872 | tf_op jit(solution)/shard_map/ppermute | solution.py:405
  181.6 1.2 copy-start.19
  182.8 5.5 %copy-start.2 = (bf16[1024,2048]{1,0:T(8,128)(2,1)S(1)}, bf16[1024,2048]{1,0:T(8,128)(2,1)}, u32[]{:S(2)}) copy-start(bf16[1024,2048]{1,0:T(8,128)(2,1)} %w_ref.3) | copy-start | bytes 12582916
  182.8 5.5 %copy-start.15 = (f32[32,1024]{1,0:T(8,128)S(1)}, f32[32,1024]{1,0:T(8,128)}, u32[]{:S(2)}) copy-start(f32[32,1024]{1,0:T(8,128)} %copy-done.14) | copy-start | bytes 393220
  (5 other events, 3.7 us)
where the time goes:
time: 199 us
  starting transfers between devices  59.7 us (30%)
  Pallas kernels  59.2 us (30%)
  waiting for transfers between devices  51.9 us (26%)
  local copies, waits for them, and re-layouts  26.9 us (14%)
    pallas_call x12, Pallas kernels, call(): pl.pallas_call(kernel, out_shape=shapes, in_specs=[VM] * len(args), out_s...  55.9 us
    ppermute x12, waiting for transfers between devices, cross(): return lax.ppermute(x, DP, moves)  33.6 us
    unnamed x69, local copies, waits for them, and re-layouts  24.7 us
    ppermute x20, starting transfers between devices, send(): return lax.ppermute(x, axis, [(i, (i + shift) % n) for i in range(n)])  21.5 us
    ppermute x12, starting transfers between devices, cross(): return lax.ppermute(x, DP, moves)  18.1 us
    ppermute x20, waiting for transfers between devices, send(): return lax.ppermute(x, axis, [(i, (i + shift) % n) for i in range(n)])  12.1 us
    all_to_all x1, starting transfers between devices, inner(): lax.all_to_all(sums.reshape(32, 1, 2 * width // 32), DP, 0, 0, tiled=True)  8.18 us
    all_to_all x1, starting transfers between devices, inner(): lax.all_to_all(jnp.broadcast_to(narrow[None], (16, *narrow.shape)), chips...  6.75 us
  transfers between devices with their start and end apart: 35, of which 13 were waited for; matrix products, arithmetic and copies ran while one was open for 1% of the time, Pallas kernels for 19%

commit v1 on v0

--- a/solution.py
+++ b/solution.py
@@ -87,10 +87,9 @@
 
 
 def slot_kernel(
-    counts_ref, lookups_ref, ids_ref, own_ref, a_ref, b_ref, c_ref, dense_ref, out_ref, value_ref, at_ref
+    capacity, counts_ref, lookups_ref, own_ref, a_ref, b_ref, c_ref, out_ref, square_ref, value_ref, at_ref
 ):
     owners = counts_ref.shape[1]
-    capacity = ids_ref.shape[1]
     features, batch = lookups_ref.shape
     spread = jnp.broadcast_to(counts_ref[...].astype(F32), (owners, owners))
     at, of = iota((owners, owners), 0), iota((owners, owners), 1)
@@ -130,10 +129,18 @@
         both = dot_f32(hot, value_ref[...])
         sums = both[:, 0:128] + both[:, 128:256]
         first = pl.multiple_of(m * each, each)
-        out_ref[pl.ds(first, each), 0 : capacity // 2, :] = sums.astype(BF16).reshape(each, capacity // 2, 128)
+        out_ref[pl.ds(first, each), :, :] = sums.astype(BF16).reshape(each, capacity // 2, 128)
         return square + jnp.sum(jnp.sum(sums * sums, axis=1, keepdims=True), axis=0, keepdims=True)
 
-    square = lax.fori_loop(0, owners // each, part, dense_ref[0:1, 0:1])
+    square = lax.fori_loop(0, owners // each, part, jnp.zeros((1, 1), F32))
+    square_ref[...] = jnp.broadcast_to(square, square_ref.shape)
+
+
+def stamp_kernel(sums_ref, ids_ref, slot_square_ref, dense_square_ref, extra_ref, out_ref):
+    owners, capacity = ids_ref.shape
+    half = capacity // 2
+    extra = jnp.sum(extra_ref[...], axis=0, keepdims=True)
+    square = slot_square_ref[0:1, 0:1] + dense_square_ref[0:1, 0:1] + jnp.sum(extra * extra, axis=1, keepdims=True)
     top = square.astype(BF16).astype(F32)
     mid = (square - top).astype(BF16).astype(F32)
     end = square - top - mid
@@ -141,7 +148,8 @@
     lane = iota((owners, 128 - 2 * capacity), 1)
     tail = jnp.where(lane == 0, top, jnp.where(lane == 1, mid, jnp.where(lane == 2, end, 0.0)))
     info = jnp.concatenate([(ids >> 8).astype(F32), (ids & 255).astype(F32), tail], axis=1)
-    out_ref[:, capacity // 2 :, :] = jnp.broadcast_to(info[:, None, :], (owners, 8, 128)).astype(BF16)
+    out_ref[:, :half, :] = sums_ref[...]
+    out_ref[:, half:, :] = jnp.broadcast_to(info[:, None, :], (owners, 8, 128)).astype(BF16)
 
 
 def table_kernel(rate, eps, clip, arrived_ref, table_ref, accum_ref, table_out, accum_out, scale_out, acc_ref):
@@ -187,17 +195,15 @@
 
 def call(kernel, outs, flops, args, scratch=(), spare=8):
     shapes = tuple(jax.ShapeDtypeStruct(s, t) for s, t in outs)
-    held = footprint(args) + footprint(shapes) + footprint(scratch)
-    res = pl.pallas_call(
+    return pl.pallas_call(
         kernel,
         out_shape=shapes,
         in_specs=[VM] * len(args),
         out_specs=tuple(VM for _ in shapes),
         scratch_shapes=list(scratch),
-        compiler_params=pltpu.CompilerParams(vmem_limit_bytes=held + spare * 2**20),
+        compiler_params=pltpu.CompilerParams(vmem_limit_bytes=footprint(scratch) + spare * 2**20),
         cost_estimate=pl.CostEstimate(flops=flops, transcendentals=0, bytes_accessed=2 * 10**6),
     )(*args)
-    return res
 
 
 SHIFTS = (1, 3, 2)
@@ -213,29 +219,26 @@
 
 def forward_kernel(chunks, *refs):
     ins, (w_ref, bias_ref, out_w_ref) = refs[:chunks], refs[chunks : chunks + 3]
-    slope_ref, hidden_ref, logit_ref, turned_ref = refs[chunks + 3 :]
+    slope_ref, hidden_ref, logit_ref, turned_ref, rows_ref = refs[chunks + 3 :]
     rows = ins[0].shape[0]
     width = w_ref.shape[1]
     for k in range(chunks):
+        rows_ref[rows * k : rows * (k + 1), :] = ins[k][...]
         turned_ref[:, rows * k : rows * (k + 1)] = ins[k][...].T
 
     def columns(n, carry):
         cols = pl.ds(pl.multiple_of(n * 256, 256), 256)
-        w = w_ref[:, cols]
-        out_w = out_w_ref[:, cols].astype(F32)
-        for k in range(chunks):
-            act = dot_f32(ins[k][...], w) + bias_ref[:, cols]
-            sigma = sigmoid(act)
-            hidden_ref[rows * k : rows * (k + 1), cols] = (act * sigma).astype(BF16)
-            slope_ref[rows * k : rows * (k + 1), cols] = out_w * sigma * (1.0 + act * (1.0 - sigma))
+        act = dot_f32(rows_ref[...], w_ref[:, cols]) + bias_ref[:, cols]
+        sigma = sigmoid(act)
+        hidden_ref[:, cols] = (act * sigma).astype(BF16)
+        slope_ref[:, cols] = out_w_ref[:, cols].astype(F32) * sigma * (1.0 + act * (1.0 - sigma))
         return carry
 
     lax.fori_loop(0, width // 256, columns, 0)
     out_w = jnp.broadcast_to(out_w_ref[...], (16, width))
-    for k in range(chunks):
-        part = dot_f32(out_w, hidden_ref[rows * k : rows * (k + 1), :], (((1,), (1,)), ((), ())))
-        at = rows * k
-        logit_ref[at // 256 : at // 256 + 1, at % 256 : at % 256 + rows] = part[0:1, :]
+    for k in range(logit_ref.shape[0]):
+        part = dot_f32(out_w, hidden_ref[256 * k : 256 * (k + 1), :], (((1,), (1,)), ((), ())))
+        logit_ref[k : k + 1, :] = part[0:1, :]
 
 
 def forward(chunks, w, bias, out_w):
@@ -244,7 +247,13 @@
     n = len(chunks)
     total = n * rows
     outs = [((total, width), F32), ((total, width), BF16), ((total // 256, 256), F32), ((depth, total), BF16)]
-    return call(functools.partial(forward_kernel, n), outs, total * 10**7, (*chunks, w, bias, out_w))
+    return call(
+        functools.partial(forward_kernel, n),
+        outs,
+        total * 10**7,
+        (*chunks, w, bias, out_w),
+        [pltpu.VMEM((total, depth), BF16)],
+    )
 
 
 ORDER = (0, 3, 1, 2)
@@ -265,8 +274,9 @@
         logit = (own_ref[k : k + 1, :] + far_ref[PARTNERS[3][k] : PARTNERS[3][k] + 1, :]) + (
             prev_ref[PARTNERS[1][k] : PARTNERS[1][k] + 1, :] + next_ref[PARTNERS[2][k] : PARTNERS[2][k] + 1, :]
         )
-        label = labels_ref[pl.ds(at, 1), :].astype(F32)
-        dlogits.append(weight_ref[pl.ds(at, 1), :] * (sigmoid(logit) - label))
+        here = pl.ds(pl.multiple_of(at * rows, rows), rows)
+        label = labels_ref[:, here].astype(F32)
+        dlogits.append(weight_ref[:, here] * (sigmoid(logit) - label))
     rows_form = jnp.concatenate(dlogits + [jnp.zeros((4, rows), F32)], axis=0)
     cols_form = rows_form.T
     for k in range(4):
@@ -344,12 +354,10 @@
         target[...] = acc_ref[pl.ds(at, size), :].astype(target.dtype)
 
 
-def last_kernel(own_ref, a_ref, b_ref, c_ref, sums_ref, narrow_ref, mine_ref, other_ref, square_ref, full_ref):
+def last_kernel(own_ref, a_ref, b_ref, c_ref, narrow_ref, mine_ref, other_ref, square_ref, full_ref):
     core = lax.axis_index("dp_2")
     total = own_ref[...] + a_ref[...].astype(F32) + b_ref[...].astype(F32) + c_ref[...].astype(F32)
-    extra = jnp.sum(sums_ref[...], axis=0, keepdims=True)
     square = jnp.sum(jnp.sum(total * total, axis=1, keepdims=True), axis=0, keepdims=True)
-    square = square + jnp.sum(extra * extra, axis=1, keepdims=True)
     square_ref[...] = jnp.broadcast_to(square, square_ref.shape)
     full_ref[...] = total
     narrow_ref[...] = total.astype(BF16)
@@ -364,12 +372,24 @@
         refs[4][rows * k : rows * (k + 1), :] = refs[k][...]
 
 
-def weight_kernel(scale_ref, w_ref, near_ref, far_ref, rows_ref, mine_ref, theirs_ref, *refs):
+def merge_kernel(*refs):
+    stacks, out_ref = refs[:8], refs[8]
+    core = lax.axis_index("dp_2")
+    per = stacks[0].shape[0] // 4
+    for side, c in ((0, core), (1, 1 - core)):
+        for i in range(4):
+            for j in range(4):
+                at = chip_rows(c, spot_on(True, c, (4 - i) % 4), spot_on(False, c, (4 - j) % 4), 1)
+                rows = pl.ds(pl.multiple_of((at * 2 + c) * per, per), per)
+                out_ref[rows, :] = stacks[4 * side + i][per * j : per * (j + 1), :]
+
+
+def weight_kernel(scale_ref, w_ref, held_ref, rows_ref, mine_ref, theirs_ref, *refs):
     stacks, (w_out_ref, accum_ref) = refs[:8], refs[8:]
     core = lax.axis_index("dp_2")
     scale = scale_ref[0:1, 0:1]
-    _, per, _ = near_ref.shape
     half = stacks[0].shape[1]
+    size = stacks[0].shape[0] // 4
     for side, c in ((0, core), (1, 1 - core)):
         cols = pl.ds(pl.multiple_of(c * half, half), half)
         for i in range(4):
@@ -377,13 +397,11 @@
 
             def chip(j, carry, stack=stacks[4 * side + i], outer=outer, c=c, cols=cols):
                 inner = spot_on(False, c, lax.rem(4 - j, 4))
-                at = chip_rows(c, outer, inner, 1)
-                for held_ref, r in ((near_ref, core), (far_ref, 1 - core)):
-                    rows = pl.ds(pl.multiple_of((at * 2 + r) * per, per), per)
-                    grad = scale * stack[pl.ds(pl.multiple_of((j * 2 + r) * per, per), per), :].astype(F32)
-                    accum = held_ref[at, :, cols].astype(F32) + grad * grad
-                    w = w_ref[rows, cols].astype(F32)
-                    w_out_ref[rows, cols] = (w - dense_rate * grad / (jnp.sqrt(accum) + adagrad_eps)).astype(BF16)
+                rows = pl.ds(chip_rows(c, outer, inner, size), size)
+                grad = scale * stack[pl.ds(pl.multiple_of(j * size, size), size), :].astype(F32)
+                accum = held_ref[rows, cols].astype(F32) + grad * grad
+                w = w_ref[rows, cols].astype(F32)
+                w_out_ref[rows, cols] = (w - dense_rate * grad / (jnp.sqrt(accum) + adagrad_eps)).astype(BF16)
                 return carry
 
             lax.fori_loop(0, 4, chip, 0)
@@ -429,10 +447,14 @@
     lookups_t = lookup_slots.T
     pooled = gather_rows(peer_counts, lookups_t, slab_values[0])
     before, after = send(pooled, "mp", 1), send(pooled, "mp", 3)
-    chips = ("dp_0", "dp_1")
     narrow = dense_accum.astype(BF16)
-    near = lax.all_to_all(jnp.broadcast_to(narrow[None], (16, *narrow.shape)), chips, 0, 0, tiled=True)
-    distant = send(near, "dp_2", 1)
+    parts = {s: cross(narrow, False, s) for s in SHIFTS}
+    block = (depth // 8, width)
+    near = call(pack_kernel, [(block, BF16)], 10**8, (narrow, parts[1], parts[2], parts[3]))[0]
+    stacks = {s: cross(near, True, s) for s in SHIFTS}
+    stacks = [near, stacks[1], stacks[2], stacks[3]]
+    stacks = stacks + [send(g, "dp_2", 1) for g in stacks]
+    accum_full = call(merge_kernel, [((depth, width), BF16)], 10**8, stacks)[0]
     bias = bias_in.reshape(1, width)
     out_w = weight_out.reshape(1, width)
     far_low, far_high = send(before[: batch // 2], "mp", 1), send(after[batch // 2 :], "mp", 3)
@@ -458,8 +480,8 @@
             logit_before,
             logit_after,
             logit_far,
-            labels.reshape(4, batch),
-            sample_weight.reshape(4, batch),
+            labels.reshape(1, -1),
+            sample_weight.reshape(1, -1),
         ),
     )
     far_dact = send(other, "dp_2", 1)
@@ -478,7 +500,7 @@
         last_kernel,
         [((depth // 16, half), BF16)] + [((depth // 32, half), F32)] * 2 + [((8, 128), F32)],
         10**8,
-        (keep, *got, sums),
+        (keep, *got),
         [pltpu.VMEM((depth // 16, half), F32)],
     )
     theirs = send(others, "dp_2", 1)
@@ -488,13 +510,19 @@
     stacks = [pack, stacks[1], stacks[2], stacks[3]]
     stacks = stacks + [send(g, "dp_2", 1) for g in stacks]
     peers, capacity = row_ids.shape[1:]
-    outgoing = call(
-        slot_kernel,
-        [((peers, capacity // 2 + 8, 128), BF16)],
+    slot_sums, slot_square = call(
+        functools.partial(slot_kernel, capacity),
+        [((peers, capacity // 2, 128), BF16), ((8, 128), F32)],
         8 * 10**9,
-        (peer_counts, lookups_t, row_ids[0], own, from_before, from_after, from_far, square),
+        (peer_counts, lookups_t, own, from_before, from_after, from_far),
         [pltpu.VMEM((features * batch, 256), BF16), pltpu.VMEM((1, features * batch), F32)],
         24,
+    )
+    outgoing = call(
+        stamp_kernel,
+        [((peers, capacity // 2 + 8, 128), BF16)],
+        10**8,
+        (slot_sums, row_ids[0], slot_square, square, sums),
     )[0]
     arrived = lax.all_to_all(outgoing, DP_MP, 0, 0, tiled=True)
     table_t, accum_t, scale = call(
@@ -509,7 +537,9 @@
         weight_kernel,
         [((depth, width), BF16), (dense_accum.shape, F32)],
         10**9,
-        (scale, weight_in, near, distant, dense_accum, mine, theirs, *stacks),
+        (scale, weight_in, accum_full, dense_accum, mine, theirs, *stacks),
+        (),
+        16,
     )
     return (weight_new, accum_new, table_t.T, accum_t.reshape(-1))
 

time: 199 us -> 180 us (0.905)
  local copies, waits for them, and re-layouts: 26.9 us -> 12.6 us
  starting transfers between devices: 59.7 us -> 68.9 us
  waiting for transfers between devices: 51.9 us -> 42.8 us
  Pallas kernels: 59.2 us -> 53.7 us
    unnamed x69 -> x41, local copies, waits for them, and re-layouts: 24.7 us -> 11.9 us
    ppermute x12 -> x18, waiting for transfers between devices: 33.6 us -> 23.9 us  [cross(): return lax.ppermute(x, DP, moves)]
    ppermute x12 -> x18, starting transfers between devices: 18.1 us -> 27.5 us  [cross(): return lax.ppermute(x, DP, moves)]
    ppermute x20 -> x23, waiting for transfers between devices: 12.1 us -> 18.9 us  [send(): return lax.ppermute(x, axis, [(i, (i + shift) % n) for i in range(n)])]
    all_to_all x1 -> x0, starting transfers between devices: 6.75 us -> none  [inner(): lax.all_to_all(jnp.broadcast_to(narrow[None], (16, *narrow.shape)), chips...]
    all_to_all x1, waiting for transfers between devices: 6.24 us -> 0.01 us  [inner(): lax.all_to_all(sums.reshape(32, 1, 2 * width // 32), DP, 0, 0, tiled=True)]
    ppermute x20 -> x23, starting transfers between devices: 21.5 us -> 27.1 us  [send(): return lax.ppermute(x, axis, [(i, (i + shift) % n) for i in range(n)])]
    pallas_call x12 -> x15, Pallas kernels: 55.9 us -> 50.4 us  [call(): pl.pallas_call(kernel, out_shape=shapes, in_specs=[VM] * len(args), out_s...]
  transfers between devices with their start and end apart: 35 -> 43, of which waited for: 13 -> 13; matrix products, arithmetic and copies ran while one was open for 1% -> 1% of each run, Pallas kernels for 19% -> 17%
where the time goes in v1:
time: 180 us; the launch traced here: 179 us
  starting transfers between devices  68.9 us (38%)
  Pallas kernels  53.7 us (30%)
  waiting for transfers between devices  42.8 us (24%)
  local copies, waits for them, and re-layouts  12.6 us (7%)
    pallas_call x15, Pallas kernels, call(): pl.pallas_call(kernel, out_shape=shapes, in_specs=[VM] * len(args), out_s...  50.4 us
    ppermute x18, starting transfers between devices, cross(): return lax.ppermute(x, DP, moves)  27.5 us
    ppermute x23, starting transfers between devices, send(): return lax.ppermute(x, axis, [(i, (i + shift) % n) for i in range(n)])  27.1 us
    ppermute x18, waiting for transfers between devices, cross(): return lax.ppermute(x, DP, moves)  23.9 us
    ppermute x23, waiting for transfers between devices, send(): return lax.ppermute(x, axis, [(i, (i + shift) % n) for i in range(n)])  18.9 us
    unnamed x41, local copies, waits for them, and re-layouts  11.9 us
    all_to_all x1, starting transfers between devices, inner(): arrived = lax.all_to_all(outgoing, DP_MP, 0, 0, tiled=True)  7.33 us
    all_to_all x1, starting transfers between devices, inner(): lax.all_to_all(sums.reshape(32, 1, 2 * width // 32), DP, 0, 0, tiled=True)  7.02 us
  transfers between devices with their start and end apart: 43, of which 13 were waited for; matrix products, arithmetic and copies ran while one was open for 1% of the time, Pallas kernels for 17%

profile of v1, /device:TPU:1, one launch (start us, length us, event | category | flops | bytes accessed | tf_op | source)
XLA Modules:
  0.0 179.0 jit_solution(4233782966348523938)
XLA Ops:
  0.6 1.0 copy-done.8
  1.7 0.7 copy-done.11
  2.4 0.7 copy-done.15
  3.1 3.3 %gather_rows.1.refs_0_ = bf16[256,1024]{1,0:T(8,128)(2,1)S(1)} custom-call(s32[1,128]{1,0:T(1,128)S(1)} %copy-done.15, s32[16,256]{1,0:T(8,128)S(1)} %bitcast.18, bf16[128,2048]{1,0:T(8,128)(2,1)S(1)} %bitcast.17), custom_call_target="tpu_custom_call" | custom-call | flops 6000000000 | bytes 2000000 | tf_op jit(solution)/shard_map/gather_rows/pallas_call | solution.py:78
  6.3 2.5 %collective-permute-start = (bf16[256,1024]{1,0:T(8,128)(2,1)S(1)}, bf16[256,1024]{1,0:T(8,128)(2,1)S(1)}, u32[]{:S(2)}, u32[]{:S(2)}) collective-permute-start(bf16[256,1024]{1,0:T(8,128)(2,1)S(1)} %gather_rows.1.refs_0_), channel_id=1, source_target_pairs={{0,1},{1,2},{2,3},{3,0},{4,5},{5,6},{6,7},{7,4},{8,9},{9,10},{10,1... | collective-permute-start | bytes 1572872 | tf_op jit(solution)/shard_map/ppermute | solution.py:423
  8.9 2.2 %collective-permute-start.1 = (bf16[256,1024]{1,0:T(8,128)(2,1)S(1)}, bf16[256,1024]{1,0:T(8,128)(2,1)S(1)}, u32[]{:S(2)}, u32[]{:S(2)}) collective-permute-start(bf16[256,1024]{1,0:T(8,128)(2,1)S(1)} %gather_rows.1.refs_0_), channel_id=1, source_target_pairs={{0,3},{1,0},{2,1},{3,2},{4,7},{5,4},{6,5},{7,6},{8,11},{9,8},{10,9... | collective-permute-start | bytes 1572872 | tf_op jit(solution)/shard_map/ppermute | solution.py:423
  11.1 3.5 %shard_map.147 = (f32[256,2048]{1,0:T(8,128)S(1)}, bf16[256,2048]{1,0:T(8,128)(2,1)S(1)}, f32[1,256]{1,0:T(1,128)S(1)}, bf16[1024,256]{1,0:T(8,128)(2,1)S(1)}) custom-call(bf16[256,1024]{1,0:T(8,128)(2,1)S(1)} %gather_rows.1.refs_0_, bf16[1024,2048]{1,0:T(8,128)(2,1)S(1)} %copy-done.2, f32[1,2048]{1,0:T(1,128)S(1)} %bitcast.21, ...), custom_call_target="tpu_custom_call" | custom-call | flops 2560000000 | bytes 2000000 | tf_op jit(solution)/shard_map/pallas_call | solution.py:198
  14.6 8.0 %collective-permute-done.refs_0_ = bf16[256,1024]{1,0:T(8,128)(2,1)S(1)} collective-permute-done((bf16[256,1024]{1,0:T(8,128)(2,1)S(1)}, bf16[256,1024]{1,0:T(8,128)(2,1)S(1)}, u32[]{:S(2)}, u32[]{:S(2)}) %collective-permute-start) | collective-permute-done | bytes 524320 | tf_op jit(solution)/shard_map/ppermute | solution.py:423
  22.7 2.7 %collective-permute-start.3 = (bf16[128,1024]{1,0:T(8,128)(2,1)S(1)}, bf16[128,1024]{1,0:T(8,128)(2,1)S(1)}, u32[]{:S(2)}, u32[]{:S(2)}) collective-permute-start(bf16[128,1024]{1,0:T(8,128)(2,1)S(1)} %slice.9), channel_id=1, source_target_pairs={{0,3},{1,0},{2,1},{3,2},{4,7},{5,4},{6,5},{7,6},{8,11},{9,8},{10,9... | collective-permute-start | bytes 786440 | tf_op jit(solution)/shard_map/ppermute | solution.py:423
  25.5 5.3 %shard_map.148 = (f32[512,2048]{1,0:T(8,128)S(1)}, bf16[512,2048]{1,0:T(8,128)(2,1)S(1)}, f32[2,256]{1,0:T(2,128)S(1)}, bf16[1024,512]{1,0:T(8,128)(2,1)S(1)}) custom-call(bf16[256,1024]{1,0:T(8,128)(2,1)S(1)} %collective-permute-done.refs_0_, bf16[256,1024]{1,0:T(8,128)(2,1)S(1)} %collective-permute-done.1.refs_1_, bf16[1024,2048]{1,0:T(8,128)(2,1)S(1)} %copy-done.2, ...), custom_call_target="tpu_custom_call" | custom-call | flops 5120000000 | bytes 2000000 | tf_op jit(solution)/shard_map/pallas_call | solution.py:198
  30.8 3.5 %shard_map.149 = (f32[256,2048]{1,0:T(8,128)S(1)}, bf16[256,2048]{1,0:T(8,128)(2,1)S(1)}, f32[1,256]{1,0:T(1,128)S(1)}, bf16[1024,256]{1,0:T(8,128)(2,1)S(1)}) custom-call(bf16[128,1024]{1,0:T(8,128)(2,1)S(1)} %collective-permute-done.2.refs_0_, bf16[128,1024]{1,0:T(8,128)(2,1)S(1)} %collective-permute-done.3.refs_1_, bf16[1024,2048]{1,0:T(8,128)(2,1)S(1)} %copy-done.2, ...), custom_call_target="tpu_custom_call" | custom-call | flops 2560000000 | bytes 2000000 | tf_op jit(solution)/shard_map/pallas_call | solution.py:198
  34.5 2.7 %collective-permute-start.5 = (f32[4,256]{1,0:T(4,128)S(1)}, f32[4,256]{1,0:T(4,128)S(1)}, u32[]{:S(2)}, u32[]{:S(2)}) collective-permute-start(f32[4,256]{1,0:T(4,128)S(1)} %pad_maximum_fusion.refs_6_), channel_id=1, source_target_pairs={{0,3},{1,0},{2,1},{3,2},{4,7},{5,4},{6,5},{7,6},{8,11},{9,8},{10,9... | collective-permute-start | bytes 12296 | tf_op jit(solution)/shard_map/ppermute | solution.py:423
  37.1 0.7 collective-permute-start.6
  38.1 3.0 %collective-permute-done.6.refs_9_ = f32[4,256]{1,0:T(4,128)S(1)} collective-permute-done((f32[4,256]{1,0:T(4,128)S(1)}, f32[4,256]{1,0:T(4,128)S(1)}, u32[]{:S(2)}, u32[]{:S(2)}) %collective-permute-start.6) | collective-permute-done | bytes 4128 | tf_op jit(solution)/shard_map/ppermute | solution.py:423
  41.1 2.5 %shard_map.150 = (bf16[1024,2048]{1,0:T(8,128)(2,1)S(1)}, bf16[1024,1024]{1,0:T(8,128)(2,1)S(1)}, f32[2,2048]{1,0:T(2,128)S(1)}) custom-call(f32[256,2048]{1,0:T(8,128)S(1)} %get-tuple-element.42.refs_0_, f32[512,2048]{1,0:T(8,128)S(1)} %get-tuple-element.43.refs_1_, f32[256,2048]{1,0:T(8,128)S(1)} %get-tuple-element.44.refs_2_, ...), custom_call_target="tpu_custom_call" | custom-call | flops 2000000000 | bytes 2000000 | tf_op jit(solution)/shard_map/pallas_call | solution.py:198
  43.6 3.6 %collective-permute-start.13 = (bf16[1024,1024]{1,0:T(8,128)(2,1)S(1)}, bf16[1024,1024]{1,0:T(8,128)(2,1)S(1)}, u32[]{:S(2)}, u32[]{:S(2)}) collective-permute-start(bf16[1024,1024]{1,0:T(8,128)(2,1)S(1)} %get-tuple-element.61), channel_id=1, source_target_pairs={{0,4},{4,0},{1,5},{5,1},{2,6},{6,2},{3,7},{7,3},{8,12},{12,8},{9,1... | collective-permute-start | bytes 6291464 | tf_op jit(solution)/shard_map/ppermute | solution.py:423
  47.8 5.4 %collective-permute-done.10.refs_3_ = bf16[1024,256]{1,0:T(8,128)(2,1)S(1)} collective-permute-done((bf16[1024,256]{1,0:T(8,128)(2,1)S(1)}, bf16[1024,256]{1,0:T(8,128)(2,1)S(1)}, u32[]{:S(2)}, u32[]{:S(2)}) %collective-permute-start.10) | collective-permute-done | bytes 524320 | tf_op jit(solution)/shard_map/ppermute | solution.py:423
  53.2 0.7 collective-permute-done.12.refs_5_
  54.0 5.3 %shard_map.153 = (f32[256,1024]{1,0:T(8,128)S(1)}, bf16[256,1024]{1,0:T(8,128)(2,1)S(1)}, bf16[256,1024]{1,0:T(8,128)(2,1)S(1)}, bf16[256,1024]{1,0:T(8,128)(2,1)S(1)}) custom-call(bf16[1024,256]{1,0:T(8,128)(2,1)S(1)} %get-tuple-element.58.refs_0_, bf16[1024,512]{1,0:T(8,128)(2,1)S(1)} %get-tuple-element.59.refs_1_, ...), custom_call_target="tpu_custom_call" | custom-call | flops 8000000000 | bytes 2000000 | tf_op jit(solution)/shard_map/pallas_call | solution.py:198
  59.2 1.4 collective-permute-start.14
  60.6 1.5 collective-permute-start.15
  62.1 1.3 collective-permute-start.20
  63.4 2.5 %collective-permute-start.21 = (bf16[32,2048]{1,0:T(8,128)(2,1)S(1)}, bf16[32,2048]{1,0:T(8,128)(2,1)S(1)}, u32[]{:S(2)}, u32[]{:S(2)}) collective-permute-start(bf16[32,2048]{1,0:T(8,128)(2,1)S(1)} %convert_element_type.3.refs_0_), channel_id=1, source_target_pairs={{0,16},{4,68},{8,24},{12,76},{16,0},{20,84},{24,8},{28,92},{32,48}... | collective-permute-start | bytes 393224 | tf_op jit(solution)/shard_map/ppermute | solution.py:418
  65.9 1.1 collective-permute-start.22
  67.0 1.9 %collective-permute-done.20.refs_1_ = bf16[32,2048]{1,0:T(8,128)(2,1)S(1)} collective-permute-done((bf16[32,2048]{1,0:T(8,128)(2,1)S(1)}, bf16[32,2048]{1,0:T(8,128)(2,1)S(1)}, u32[]{:S(2)}, u32[]{:S(2)}) %collective-permute-start.20) | collective-permute-done | bytes 131104 | tf_op jit(solution)/shard_map/ppermute | solution.py:418
  68.9 3.8 %collective-permute-done.21.refs_2_ = bf16[32,2048]{1,0:T(8,128)(2,1)S(1)} collective-permute-done((bf16[32,2048]{1,0:T(8,128)(2,1)S(1)}, bf16[32,2048]{1,0:T(8,128)(2,1)S(1)}, u32[]{:S(2)}, u32[]{:S(2)}) %collective-permute-start.21) | collective-permute-done | bytes 131104 | tf_op jit(solution)/shard_map/ppermute | solution.py:418
  72.8 2.3 %collective-permute-start.16 = (bf16[256,1024]{1,0:T(8,128)(2,1)S(1)}, bf16[256,1024]{1,0:T(8,128)(2,1)S(1)}, u32[]{:S(2)}, u32[]{:S(2)}) collective-permute-start(bf16[256,1024]{1,0:T(8,128)(2,1)S(1)} %get-tuple-element.65), channel_id=1, source_target_pairs={{0,64},{4,20},{8,72},{12,28},{16,80},{20,4},{24,88},{28,12},{32,96... | collective-permute-start | bytes 1572872 | tf_op jit(solution)/shard_map/ppermute | solution.py:418
  75.1 5.4 %shard_map.151 = (f32[256,1024]{1,0:T(8,128)S(1)}, bf16[256,1024]{1,0:T(8,128)(2,1)}, bf16[256,1024]{1,0:T(8,128)(2,1)}, bf16[256,1024]{1,0:T(8,128)(2,1)}) custom-call(bf16[1024,2048]{1,0:T(8,128)(2,1)S(1)} %get-tuple-element.51.dact_ref.refs_6_, bf16[1024,2048]{1,0:T(8,128)(2,1)S(1)} %copy-done.2), custom_call_target="tpu_custom_call" | custom-call | flops 4000000000 | bytes 2000000 | tf_op jit(solution)/shard_map/pallas_call | solution.py:198
  80.5 1.0 copy-done.17
  81.4 2.7 %collective-permute-start.8 = (bf16[256,1024]{1,0:T(8,128)(2,1)}, bf16[256,1024]{1,0:T(8,128)(2,1)}, u32[]{:S(2)}, u32[]{:S(2)}) collective-permute-start(bf16[256,1024]{1,0:T(8,128)(2,1)} %get-tuple-element.54), channel_id=1, source_target_pairs={{0,3},{1,0},{2,1},{3,2},{4,7},{5,4},{6,5},{7,6},{8,11},{9,8},{10,9... | collective-permute-start | bytes 1572872 | tf_op jit(solution)/shard_map/ppermute | solution.py:423
  84.3 3.4 %collective-permute-done.16.c_ref = bf16[256,1024]{1,0:T(8,128)(2,1)S(1)} collective-permute-done((bf16[256,1024]{1,0:T(8,128)(2,1)S(1)}, bf16[256,1024]{1,0:T(8,128)(2,1)S(1)}, u32[]{:S(2)}, u32[]{:S(2)}) %collective-permute-start.16) | collective-permute-done | bytes 524320 | tf_op jit(solution)/shard_map/ppermute | solution.py:418
  88.1 2.7 %collective-permute-start.18 = (bf16[64,1024]{1,0:T(8,128)(2,1)S(1)}, bf16[64,1024]{1,0:T(8,128)(2,1)S(1)}, u32[]{:S(2)}, u32[]{:S(2)}) collective-permute-start(bf16[64,1024]{1,0:T(8,128)(2,1)S(1)} %get-tuple-element.68), channel_id=1, source_target_pairs={{0,24},{4,100},{8,0},{12,108},{16,8},{20,116},{24,16},{28,124},{32... | collective-permute-start | bytes 393224 | tf_op jit(solution)/shard_map/ppermute | solution.py:418
  90.8 0.8 copy.17
  92.2 7.0 %all-to-all-start = ((f32[32,1,128]{2,1,0:T(1,128)}), f32[32,1,128]{2,1,0:T(1,128)S(1)}, u32[]{:S(2)}, u32[]{:S(2)}) async-start(f32[32,1,128]{2,1,0:T(1,128)} %bitcast.6), calls=%async_computation | async-start | bytes 32768 | tf_op jit(solution)/shard_map/all_to_all | solution.py:498
  99.3 0.8 copy-done.9
  100.1 2.9 %collective-permute-start.24 = (bf16[128,2048]{1,0:T(8,128)(2,1)S(1)}, bf16[128,2048]{1,0:T(8,128)(2,1)S(1)}, u32[]{:S(2)}, u32[]{:S(2)}) collective-permute-start(bf16[128,2048]{1,0:T(8,128)(2,1)S(1)} %shard_map.158.refs_0_), channel_id=1, source_target_pairs={{0,64},{4,20},{8,72},{12,28},{16,80},{20,4},{24,88},{28,12},{32,96... | collective-permute-start | bytes 1572872 | tf_op jit(solution)/shard_map/ppermute | solution.py:418
  102.9 0.9 collective-permute-start.25
  103.8 1.4 collective-permute-done.9.c_ref
  105.2 4.6 %collective-permute-start.26 = (bf16[128,2048]{1,0:T(8,128)(2,1)S(1)}, bf16[128,2048]{1,0:T(8,128)(2,1)}, u32[]{:S(2)}, u32[]{:S(2)}) collective-permute-start(bf16[128,2048]{1,0:T(8,128)(2,1)S(1)} %shard_map.158.refs_0_), channel_id=1, source_target_pairs={{0,4},{4,0},{1,5},{5,1},{2,6},{6,2},{3,7},{7,3},{8,12},{12,8},{9,1... | collective-permute-start | bytes 1572872 | tf_op jit(solution)/shard_map/ppermute | solution.py:423
  110.0 1.6 collective-permute-start.19
  111.5 1.0 copy-done.10
  112.6 0.7 copy-done.12
  113.3 0.7 copy-done.16
  113.9 1.2 copy-done.18
  115.2 8.1 %shard_map.152 = (bf16[128,16,128]{2,1,0:T(8,128)(2,1)S(1)}, f32[8,128]{1,0:T(8,128)S(1)}) custom-call(s32[1,128]{1,0:T(1,128)S(1)} %copy-done.16, s32[16,256]{1,0:T(8,128)S(1)} %bitcast.19, f32[256,1024]{1,0:T(8,128)S(1)} %copy-done.18, bf16[256,1024]{1,0:T(8,128)(2,1)S(1)} %copy-done.10, bf16[256,1024]{1,0:T(8,128)(2,1)} %collective-permute-done.8.b_ref, ...), custom_call_target="tpu_custom_call" | custom-call | flops 8000000000 | bytes 2000000 | tf_op jit(solution)/shard_map/pallas_call | solution.py:198
  123.5 1.2 shard_map.156
  124.6 7.3 %all-to-all-start.1 = ((bf16[128,24,128]{2,1,0:T(8,128)(2,1)}), bf16[128,24,128]{2,1,0:T(8,128)(2,1)S(1)}, u32[]{:S(2)}, u32[]{:S(2)}) async-start(bf16[128,24,128]{2,1,0:T(8,128)(2,1)} %shard_map.156), calls=%async_computation.1 | async-start | bytes 1572864 | tf_op jit(solution)/shard_map/all_to_all | solution.py:527
  132.0 1.4 collective-permute-start.31
  133.4 2.4 %collective-permute-start.32 = (bf16[64,1024]{1,0:T(8,128)(2,1)S(1)}, bf16[64,1024]{1,0:T(8,128)(2,1)S(1)}, u32[]{:S(2)}, u32[]{:S(2)}) collective-permute-start(bf16[64,1024]{1,0:T(8,128)(2,1)S(1)} %get-tuple-element.75.refs_0_), channel_id=1, source_target_pairs={{0,16},{4,68},{8,24},{12,76},{16,0},{20,84},{24,8},{28,92},{32,48}... | collective-permute-start | bytes 393224 | tf_op jit(solution)/shard_map/ppermute | solution.py:418
  135.8 1.2 collective-permute-start.33
  137.0 8.0 %collective-permute-done.31.refs_1_ = bf16[64,1024]{1,0:T(8,128)(2,1)S(1)} collective-permute-done((bf16[64,1024]{1,0:T(8,128)(2,1)S(1)}, bf16[64,1024]{1,0:T(8,128)(2,1)S(1)}, u32[]{:S(2)}, u32[]{:S(2)}) %collective-permute-start.31) | collective-permute-done | bytes 131104 | tf_op jit(solution)/shard_map/ppermute | solution.py:418
  145.4 1.2 collective-permute-done.32.refs_2_
  147.2 0.8 collective-permute-start.34
  148.0 2.5 %collective-permute-start.35 = (bf16[256,1024]{1,0:T(8,128)(2,1)S(1)}, bf16[256,1024]{1,0:T(8,128)(2,1)}, u32[]{:S(2)}, u32[]{:S(2)}) collective-permute-start(bf16[256,1024]{1,0:T(8,128)(2,1)S(1)} %shard_map.160.refs_0_), channel_id=1, source_target_pairs={{0,64},{4,20},{8,72},{12,28},{16,80},{20,4},{24,88},{28,12},{32,96... | collective-permute-start | bytes 1572872 | tf_op jit(solution)/shard_map/ppermute | solution.py:418
  150.4 1.1 collective-permute-start.36
  151.6 1.6 shard_map.159.held_ref
  153.2 2.0 %copy-done = bf16[1024,2048]{1,0:T(8,128)(2,1)} copy-done((bf16[1024,2048]{1,0:T(8,128)(2,1)}, bf16[1024,2048]{1,0:T(8,128)(2,1)S(1)}, u32[]{:S(2)}) %copy-start) | copy-done | bytes 4194328
  155.2 1.2 collective-permute-start.30
  156.9 0.9 collective-permute-start.38
  157.8 5.2 %collective-permute-done.35.refs_2_ = bf16[256,1024]{1,0:T(8,128)(2,1)} collective-permute-done((bf16[256,1024]{1,0:T(8,128)(2,1)S(1)}, bf16[256,1024]{1,0:T(8,128)(2,1)}, u32[]{:S(2)}, u32[]{:S(2)}) %collective-permute-start.35) | collective-permute-done | bytes 524320 | tf_op jit(solution)/shard_map/ppermute | solution.py:418
  163.0 1.2 collective-permute-start.39
  164.3 1.2 copy-done.7
  165.5 4.2 %shard_map.157 = (f32[64,4096]{1,0:T(8,128)}, f32[1,4096]{1,0:T(1,128)}, f32[8,128]{1,0:T(8,128)S(1)}) custom-call(bf16[128,24,128]{2,1,0:T(8,128)(2,1)S(1)} %all-to-all-done.1.arrived_ref, f32[64,4096]{1,0:T(8,128)S(1)} %bitcast.16, f32[1,4096]{1,0:T(1,128)S(1)} %bitcast.20), custom_call_target="tpu_custom_call" | custom-call | flops 6000000000 | bytes 2000000 | tf_op jit(solution)/shard_map/pallas_call | solution.py:198
  169.8 9.2 %shard_map.161 = (bf16[1024,2048]{1,0:T(8,128)(2,1)}, f32[32,2048]{1,0:T(8,128)}) custom-call(f32[8,128]{1,0:T(8,128)S(1)} %get-tuple-element.72.scale_ref, bf16[1024,2048]{1,0:T(8,128)(2,1)S(1)} %copy-done.3, bf16[1024,2048]{1,0:T(8,128)(2,1)S(1)} %copy-done.1, f32[32,2048]{1,0:T(8,128)S(1)} %copy-done.4, f32[32,1024]{1,0:T(8,128)S(1)} %get-tuple-element.73.mine_ref, ...), custom_call_target="tpu_custom_call" | custom-call | flops 1000000000 | bytes 2000000 | tf_op jit(solution)/shard_map/pallas_call | solution.py:198
  (85 shorter events, 4.3 us)
Async XLA Ops:
  0.6 1.0 copy-start.8
  1.7 0.7 copy-start.11
  2.4 0.7 copy-start.15
  3.0 8.0 %copy-start.19 = (bf16[2048]{0:T(1024)(128)(2,1)S(1)}, bf16[2048]{0:T(1024)(128)(2,1)}, u32[]{:S(2)}) copy-start(bf16[2048]{0:T(1024)(128)(2,1)} %param.20) | copy-start | bytes 12292
  3.0 8.0 %copy-start.2 = (bf16[1024,2048]{1,0:T(8,128)(2,1)S(1)}, bf16[1024,2048]{1,0:T(8,128)(2,1)}, u32[]{:S(2)}) copy-start(bf16[1024,2048]{1,0:T(8,128)(2,1)} %w_ref.3) | copy-start | bytes 12582916
  3.1 8.0 %copy-start.14 = (f32[2048]{0:T(1024)S(1)}, f32[2048]{0:T(1024)}, u32[]{:S(2)}) copy-start(f32[2048]{0:T(1024)} %param.19) | copy-start | bytes 24580
  6.3 16.3 %collective-permute-start = (bf16[256,1024]{1,0:T(8,128)(2,1)S(1)}, bf16[256,1024]{1,0:T(8,128)(2,1)S(1)}, u32[]{:S(2)}, u32[]{:S(2)}) collective-permute-start(bf16[256,1024]{1,0:T(8,128)(2,1)S(1)} %gather_rows.1.refs_0_), channel_id=1, source_target_pairs={{0,1},{1,2},{2,3},{3,0},{4,5},{5,6},{6,7},{7,4},{8,9},{9,10},{10,1... | collective-permute-start | bytes 1572872 | tf_op jit(solution)/shard_map/ppermute | solution.py:423
  8.9 13.9 %collective-permute-start.1 = (bf16[256,1024]{1,0:T(8,128)(2,1)S(1)}, bf16[256,1024]{1,0:T(8,128)(2,1)S(1)}, u32[]{:S(2)}, u32[]{:S(2)}) collective-permute-start(bf16[256,1024]{1,0:T(8,128)(2,1)S(1)} %gather_rows.1.refs_0_), channel_id=1, source_target_pairs={{0,3},{1,0},{2,1},{3,2},{4,7},{5,4},{6,5},{7,6},{8,11},{9,8},{10,9... | collective-permute-start | bytes 1572872 | tf_op jit(solution)/shard_map/ppermute | solution.py:423
  22.6 8.2 %collective-permute-start.2 = (bf16[128,1024]{1,0:T(8,128)(2,1)S(1)}, bf16[128,1024]{1,0:T(8,128)(2,1)S(1)}, u32[]{:S(2)}, u32[]{:S(2)}) collective-permute-start(bf16[128,1024]{1,0:T(8,128)(2,1)S(1)} %slice.8), channel_id=1, source_target_pairs={{0,1},{1,2},{2,3},{3,0},{4,5},{5,6},{6,7},{7,4},{8,9},{9,10},{10,1... | collective-permute-start | bytes 786440 | tf_op jit(solution)/shard_map/ppermute | solution.py:423
  22.7 8.1 %collective-permute-start.3 = (bf16[128,1024]{1,0:T(8,128)(2,1)S(1)}, bf16[128,1024]{1,0:T(8,128)(2,1)S(1)}, u32[]{:S(2)}, u32[]{:S(2)}) collective-permute-start(bf16[128,1024]{1,0:T(8,128)(2,1)S(1)} %slice.9), channel_id=1, source_target_pairs={{0,3},{1,0},{2,1},{3,2},{4,7},{5,4},{6,5},{7,6},{8,11},{9,8},{10,9... | collective-permute-start | bytes 786440 | tf_op jit(solution)/shard_map/ppermute | solution.py:423
  30.8 10.3 %copy-start.5 = (s32[1024]{0:T(1024)S(1)}, s32[1024]{0:T(1024)}, u32[]{:S(2)}) copy-start(s32[1024]{0:T(1024)} %param.16) | copy-start | bytes 12292
  30.8 10.3 %copy-start.6 = (f32[1024]{0:T(1024)S(1)}, f32[1024]{0:T(1024)}, u32[]{:S(2)}) copy-start(f32[1024]{0:T(1024)} %param.17) | copy-start | bytes 12292
  34.4 3.7 %collective-permute-start.4 = (f32[4,256]{1,0:T(4,128)S(1)}, f32[4,256]{1,0:T(4,128)S(1)}, u32[]{:S(2)}, u32[]{:S(2)}) collective-permute-start(f32[4,256]{1,0:T(4,128)S(1)} %pad_maximum_fusion.refs_6_), channel_id=1, source_target_pairs={{0,1},{1,2},{2,3},{3,0},{4,5},{5,6},{6,7},{7,4},{8,9},{9,10},{10,1... | collective-permute-start | bytes 12296 | tf_op jit(solution)/shard_map/ppermute | solution.py:423
  34.5 3.7 %collective-permute-start.5 = (f32[4,256]{1,0:T(4,128)S(1)}, f32[4,256]{1,0:T(4,128)S(1)}, u32[]{:S(2)}, u32[]{:S(2)}) collective-permute-start(f32[4,256]{1,0:T(4,128)S(1)} %pad_maximum_fusion.refs_6_), channel_id=1, source_target_pairs={{0,3},{1,0},{2,1},{3,2},{4,7},{5,4},{6,5},{7,6},{8,11},{9,8},{10,9... | collective-permute-start | bytes 12296 | tf_op jit(solution)/shard_map/ppermute | solution.py:423
  37.1 4.0 %collective-permute-start.6 = (f32[4,256]{1,0:T(4,128)S(1)}, f32[4,256]{1,0:T(4,128)S(1)}, u32[]{:S(2)}, u32[]{:S(2)}) collective-permute-start(f32[4,256]{1,0:T(4,128)S(1)} %pad_maximum_fusion.refs_6_), channel_id=1, source_target_pairs={{0,2},{1,3},{2,0},{3,1},{4,6},{5,7},{6,4},{7,5},{8,10},{9,11},{10,... | collective-permute-start | bytes 12296 | tf_op jit(solution)/shard_map/ppermute | solution.py:423
  43.6 10.4 %collective-permute-start.13 = (bf16[1024,1024]{1,0:T(8,128)(2,1)S(1)}, bf16[1024,1024]{1,0:T(8,128)(2,1)S(1)}, u32[]{:S(2)}, u32[]{:S(2)}) collective-permute-start(bf16[1024,1024]{1,0:T(8,128)(2,1)S(1)} %get-tuple-element.61), channel_id=1, source_target_pairs={{0,4},{4,0},{1,5},{5,1},{2,6},{6,2},{3,7},{7,3},{8,12},{12,8},{9,1... | collective-permute-start | bytes 6291464 | tf_op jit(solution)/shard_map/ppermute | solution.py:423
  47.2 6.8 %collective-permute-start.11 = (bf16[1024,512]{1,0:T(8,128)(2,1)S(1)}, bf16[1024,512]{1,0:T(8,128)(2,1)S(1)}, u32[]{:S(2)}, u32[]{:S(2)}) collective-permute-start(bf16[1024,512]{1,0:T(8,128)(2,1)S(1)} %get-tuple-element.59.refs_1_), channel_id=1, source_target_pairs={{0,4},{4,0},{1,5},{5,1},{2,6},{6,2},{3,7},{7,3},{8,12},{12,8},{9,1... | collective-permute-start | bytes 3145736 | tf_op jit(solution)/shard_map/ppermute | solution.py:423
  47.2 5.9 %collective-permute-start.10 = (bf16[1024,256]{1,0:T(8,128)(2,1)S(1)}, bf16[1024,256]{1,0:T(8,128)(2,1)S(1)}, u32[]{:S(2)}, u32[]{:S(2)}) collective-permute-start(bf16[1024,256]{1,0:T(8,128)(2,1)S(1)} %get-tuple-element.58.refs_0_), channel_id=1, source_target_pairs={{0,4},{4,0},{1,5},{5,1},{2,6},{6,2},{3,7},{7,3},{8,12},{12,8},{9,1... | collective-permute-start | bytes 1572872 | tf_op jit(solution)/shard_map/ppermute | solution.py:423
  47.7 6.3 %collective-permute-start.12 = (bf16[1024,256]{1,0:T(8,128)(2,1)S(1)}, bf16[1024,256]{1,0:T(8,128)(2,1)S(1)}, u32[]{:S(2)}, u32[]{:S(2)}) collective-permute-start(bf16[1024,256]{1,0:T(8,128)(2,1)S(1)} %get-tuple-element.60.refs_2_), channel_id=1, source_target_pairs={{0,4},{4,0},{1,5},{5,1},{2,6},{6,2},{3,7},{7,3},{8,12},{12,8},{9,1... | collective-permute-start | bytes 1572872 | tf_op jit(solution)/shard_map/ppermute | solution.py:423
  53.9 8.1 %copy-start.4 = (f32[32,2048]{1,0:T(8,128)S(1)}, f32[32,2048]{1,0:T(8,128)}, u32[]{:S(2)}) copy-start(f32[32,2048]{1,0:T(8,128)} %rows_ref.1) | copy-start | bytes 786436
  59.2 22.2 %collective-permute-start.14 = (bf16[256,1024]{1,0:T(8,128)(2,1)S(1)}, bf16[256,1024]{1,0:T(8,128)(2,1)S(1)}, u32[]{:S(2)}, u32[]{:S(2)}) collective-permute-start(bf16[256,1024]{1,0:T(8,128)(2,1)S(1)} %get-tuple-element.63), channel_id=1, source_target_pairs={{0,32},{4,12},{8,40},{12,20},{16,48},{20,28},{24,56},{28,4},{32,64... | collective-permute-start | bytes 1572872 | tf_op jit(solution)/shard_map/ppermute | solution.py:418
  60.6 23.5 %collective-permute-start.15 = (bf16[256,1024]{1,0:T(8,128)(2,1)S(1)}, bf16[256,1024]{1,0:T(8,128)(2,1)S(1)}, u32[]{:S(2)}, u32[]{:S(2)}) collective-permute-start(bf16[256,1024]{1,0:T(8,128)(2,1)S(1)} %get-tuple-element.64), channel_id=1, source_target_pairs={{0,96},{4,28},{8,104},{12,4},{16,112},{20,12},{24,120},{28,20},{32... | collective-permute-start | bytes 1572872 | tf_op jit(solution)/shard_map/ppermute | solution.py:418
  62.1 6.8 %collective-permute-start.20 = (bf16[32,2048]{1,0:T(8,128)(2,1)S(1)}, bf16[32,2048]{1,0:T(8,128)(2,1)S(1)}, u32[]{:S(2)}, u32[]{:S(2)}) collective-permute-start(bf16[32,2048]{1,0:T(8,128)(2,1)S(1)} %convert_element_type.3.refs_0_), channel_id=1, source_target_pairs={{0,8},{4,36},{8,16},{12,44},{16,24},{20,52},{24,0},{28,60},{32,40}... | collective-permute-start | bytes 393224 | tf_op jit(solution)/shard_map/ppermute | solution.py:418
  63.4 9.3 %collective-permute-start.21 = (bf16[32,2048]{1,0:T(8,128)(2,1)S(1)}, bf16[32,2048]{1,0:T(8,128)(2,1)S(1)}, u32[]{:S(2)}, u32[]{:S(2)}) collective-permute-start(bf16[32,2048]{1,0:T(8,128)(2,1)S(1)} %convert_element_type.3.refs_0_), channel_id=1, source_target_pairs={{0,16},{4,68},{8,24},{12,76},{16,0},{20,84},{24,8},{28,92},{32,48}... | collective-permute-start | bytes 393224 | tf_op jit(solution)/shard_map/ppermute | solution.py:418
  65.9 6.9 %collective-permute-start.22 = (bf16[32,2048]{1,0:T(8,128)(2,1)S(1)}, bf16[32,2048]{1,0:T(8,128)(2,1)S(1)}, u32[]{:S(2)}, u32[]{:S(2)}) collective-permute-start(bf16[32,2048]{1,0:T(8,128)(2,1)S(1)} %convert_element_type.3.refs_0_), channel_id=1, source_target_pairs={{0,24},{4,100},{8,0},{12,108},{16,8},{20,116},{24,16},{28,124},{32... | collective-permute-start | bytes 393224 | tf_op jit(solution)/shard_map/ppermute | solution.py:418
  72.8 15.4 %collective-permute-start.23 = (bf16[128,2048]{1,0:T(8,128)(2,1)S(1)}, bf16[128,2048]{1,0:T(8,128)(2,1)S(1)}, u32[]{:S(2)}, u32[]{:S(2)}) collective-permute-start(bf16[128,2048]{1,0:T(8,128)(2,1)S(1)} %shard_map.158.refs_0_), channel_id=1, source_target_pairs={{0,32},{4,12},{8,40},{12,20},{16,48},{20,28},{24,56},{28,4},{32,64... | collective-permute-start | bytes 1572872 | tf_op jit(solution)/shard_map/ppermute | solution.py:418
  72.8 14.8 %collective-permute-start.16 = (bf16[256,1024]{1,0:T(8,128)(2,1)S(1)}, bf16[256,1024]{1,0:T(8,128)(2,1)S(1)}, u32[]{:S(2)}, u32[]{:S(2)}) collective-permute-start(bf16[256,1024]{1,0:T(8,128)(2,1)S(1)} %get-tuple-element.65), channel_id=1, source_target_pairs={{0,64},{4,20},{8,72},{12,28},{16,80},{20,4},{24,88},{28,12},{32,96... | collective-permute-start | bytes 1572872 | tf_op jit(solution)/shard_map/ppermute | solution.py:418
  80.5 1.0 copy-start.17
  81.4 17.8 %collective-permute-start.7 = (bf16[256,1024]{1,0:T(8,128)(2,1)}, bf16[256,1024]{1,0:T(8,128)(2,1)S(1)}, u32[]{:S(2)}, u32[]{:S(2)}) collective-permute-start(bf16[256,1024]{1,0:T(8,128)(2,1)} %get-tuple-element.53), channel_id=1, source_target_pairs={{0,1},{1,2},{2,3},{3,0},{4,5},{5,6},{6,7},{7,4},{8,9},{9,10},{10,1... | collective-permute-start | bytes 1572872 | tf_op jit(solution)/shard_map/ppermute | solution.py:423
  81.4 21.5 %collective-permute-start.8 = (bf16[256,1024]{1,0:T(8,128)(2,1)}, bf16[256,1024]{1,0:T(8,128)(2,1)}, u32[]{:S(2)}, u32[]{:S(2)}) collective-permute-start(bf16[256,1024]{1,0:T(8,128)(2,1)} %get-tuple-element.54), channel_id=1, source_target_pairs={{0,3},{1,0},{2,1},{3,2},{4,7},{5,4},{6,5},{7,6},{8,11},{9,8},{10,9... | collective-permute-start | bytes 1572872 | tf_op jit(solution)/shard_map/ppermute | solution.py:423
  84.1 21.1 %collective-permute-start.9 = (bf16[256,1024]{1,0:T(8,128)(2,1)}, bf16[256,1024]{1,0:T(8,128)(2,1)}, u32[]{:S(2)}, u32[]{:S(2)}) collective-permute-start(bf16[256,1024]{1,0:T(8,128)(2,1)} %get-tuple-element.55), channel_id=1, source_target_pairs={{0,2},{1,3},{2,0},{3,1},{4,6},{5,7},{6,4},{7,5},{8,10},{9,11},{10,... | collective-permute-start | bytes 1572872 | tf_op jit(solution)/shard_map/ppermute | solution.py:423
  88.0 21.8 %collective-permute-start.17 = (bf16[64,1024]{1,0:T(8,128)(2,1)S(1)}, bf16[64,1024]{1,0:T(8,128)(2,1)S(1)}, u32[]{:S(2)}, u32[]{:S(2)}) collective-permute-start(bf16[64,1024]{1,0:T(8,128)(2,1)S(1)} %get-tuple-element.67), channel_id=1, source_target_pairs={{0,8},{4,36},{8,16},{12,44},{16,24},{20,52},{24,0},{28,60},{32,40}... | collective-permute-start | bytes 393224 | tf_op jit(solution)/shard_map/ppermute | solution.py:418
  88.1 21.8 %collective-permute-start.18 = (bf16[64,1024]{1,0:T(8,128)(2,1)S(1)}, bf16[64,1024]{1,0:T(8,128)(2,1)S(1)}, u32[]{:S(2)}, u32[]{:S(2)}) collective-permute-start(bf16[64,1024]{1,0:T(8,128)(2,1)S(1)} %get-tuple-element.68), channel_id=1, source_target_pairs={{0,24},{4,100},{8,0},{12,108},{16,8},{20,116},{24,16},{28,124},{32... | collective-permute-start | bytes 393224 | tf_op jit(solution)/shard_map/ppermute | solution.py:418
  92.2 31.2 %all-to-all-start = ((f32[32,1,128]{2,1,0:T(1,128)}), f32[32,1,128]{2,1,0:T(1,128)S(1)}, u32[]{:S(2)}, u32[]{:S(2)}) async-start(f32[32,1,128]{2,1,0:T(1,128)} %bitcast.6), calls=%async_computation | async-start | bytes 32768 | tf_op jit(solution)/shard_map/all_to_all | solution.py:498
  99.3 0.8 copy-start.9
  100.1 33.3 %collective-permute-start.24 = (bf16[128,2048]{1,0:T(8,128)(2,1)S(1)}, bf16[128,2048]{1,0:T(8,128)(2,1)S(1)}, u32[]{:S(2)}, u32[]{:S(2)}) collective-permute-start(bf16[128,2048]{1,0:T(8,128)(2,1)S(1)} %shard_map.158.refs_0_), channel_id=1, source_target_pairs={{0,64},{4,20},{8,72},{12,28},{16,80},{20,4},{24,88},{28,12},{32,96... | collective-permute-start | bytes 1572872 | tf_op jit(solution)/shard_map/ppermute | solution.py:418
  102.9 32.9 %collective-permute-start.25 = (bf16[128,2048]{1,0:T(8,128)(2,1)S(1)}, bf16[128,2048]{1,0:T(8,128)(2,1)}, u32[]{:S(2)}, u32[]{:S(2)}) collective-permute-start(bf16[128,2048]{1,0:T(8,128)(2,1)S(1)} %shard_map.158.refs_0_), channel_id=1, source_target_pairs={{0,96},{4,28},{8,104},{12,4},{16,112},{20,12},{24,120},{28,20},{32... | collective-permute-start | bytes 1572872 | tf_op jit(solution)/shard_map/ppermute | solution.py:418
  105.2 42.7 %collective-permute-start.26 = (bf16[128,2048]{1,0:T(8,128)(2,1)S(1)}, bf16[128,2048]{1,0:T(8,128)(2,1)}, u32[]{:S(2)}, u32[]{:S(2)}) collective-permute-start(bf16[128,2048]{1,0:T(8,128)(2,1)S(1)} %shard_map.158.refs_0_), channel_id=1, source_target_pairs={{0,4},{4,0},{1,5},{5,1},{2,6},{6,2},{3,7},{7,3},{8,12},{12,8},{9,1... | collective-permute-start | bytes 1572872 | tf_op jit(solution)/shard_map/ppermute | solution.py:423
  109.9 40.6 %collective-permute-start.27 = (bf16[128,2048]{1,0:T(8,128)(2,1)S(1)}, bf16[128,2048]{1,0:T(8,128)(2,1)}, u32[]{:S(2)}, u32[]{:S(2)}) collective-permute-start(bf16[128,2048]{1,0:T(8,128)(2,1)S(1)} %collective-permute-done.23.refs_1_), channel_id=1, source_target_pairs={{0,4},{4,0},{1,5},{5,1},{2,6},{6,2},{3,7},{7,3},{8,12},{12,8},{9,1... | collective-permute-start | bytes 1572872 | tf_op jit(solution)/shard_map/ppermute | solution.py:423
  110.0 13.3 %collective-permute-start.19 = (bf16[64,1024]{1,0:T(8,128)(2,1)S(1)}, bf16[64,1024]{1,0:T(8,128)(2,1)S(1)}, u32[]{:S(2)}, u32[]{:S(2)}) collective-permute-start(bf16[64,1024]{1,0:T(8,128)(2,1)S(1)} %get-tuple-element.69), channel_id=1, source_target_pairs={{0,16},{4,68},{8,24},{12,76},{16,0},{20,84},{24,8},{28,92},{32,48}... | collective-permute-start | bytes 393224 | tf_op jit(solution)/shard_map/ppermute | solution.py:418
  111.5 1.0 copy-start.10
  112.6 0.7 copy-start.12
  113.3 0.7 copy-start.16
  113.9 1.2 copy-start.18
  124.6 39.7 %all-to-all-start.1 = ((bf16[128,24,128]{2,1,0:T(8,128)(2,1)}), bf16[128,24,128]{2,1,0:T(8,128)(2,1)S(1)}, u32[]{:S(2)}, u32[]{:S(2)}) async-start(bf16[128,24,128]{2,1,0:T(8,128)(2,1)} %shard_map.156), calls=%async_computation.1 | async-start | bytes 1572864 | tf_op jit(solution)/shard_map/all_to_all | solution.py:527
  132.0 13.0 %collective-permute-start.31 = (bf16[64,1024]{1,0:T(8,128)(2,1)S(1)}, bf16[64,1024]{1,0:T(8,128)(2,1)S(1)}, u32[]{:S(2)}, u32[]{:S(2)}) collective-permute-start(bf16[64,1024]{1,0:T(8,128)(2,1)S(1)} %get-tuple-element.75.refs_0_), channel_id=1, source_target_pairs={{0,8},{4,36},{8,16},{12,44},{16,24},{20,52},{24,0},{28,60},{32,40}... | collective-permute-start | bytes 393224 | tf_op jit(solution)/shard_map/ppermute | solution.py:418
  133.4 13.2 %collective-permute-start.32 = (bf16[64,1024]{1,0:T(8,128)(2,1)S(1)}, bf16[64,1024]{1,0:T(8,128)(2,1)S(1)}, u32[]{:S(2)}, u32[]{:S(2)}) collective-permute-start(bf16[64,1024]{1,0:T(8,128)(2,1)S(1)} %get-tuple-element.75.refs_0_), channel_id=1, source_target_pairs={{0,16},{4,68},{8,24},{12,76},{16,0},{20,84},{24,8},{28,92},{32,48}... | collective-permute-start | bytes 393224 | tf_op jit(solution)/shard_map/ppermute | solution.py:418
  135.8 11.3 %collective-permute-start.33 = (bf16[64,1024]{1,0:T(8,128)(2,1)S(1)}, bf16[64,1024]{1,0:T(8,128)(2,1)S(1)}, u32[]{:S(2)}, u32[]{:S(2)}) collective-permute-start(bf16[64,1024]{1,0:T(8,128)(2,1)S(1)} %get-tuple-element.75.refs_0_), channel_id=1, source_target_pairs={{0,24},{4,100},{8,0},{12,108},{16,8},{20,116},{24,16},{28,124},{32... | collective-permute-start | bytes 393224 | tf_op jit(solution)/shard_map/ppermute | solution.py:418
  144.9 6.6 %collective-permute-start.28 = (bf16[128,2048]{1,0:T(8,128)(2,1)S(1)}, bf16[128,2048]{1,0:T(8,128)(2,1)S(1)}, u32[]{:S(2)}, u32[]{:S(2)}) collective-permute-start(bf16[128,2048]{1,0:T(8,128)(2,1)S(1)} %collective-permute-done.24.refs_2_), channel_id=1, source_target_pairs={{0,4},{4,0},{1,5},{5,1},{2,6},{6,2},{3,7},{7,3},{8,12},{12,8},{9,1... | collective-permute-start | bytes 1572872 | tf_op jit(solution)/shard_map/ppermute | solution.py:423
  146.6 4.9 %collective-permute-start.29 = (bf16[128,2048]{1,0:T(8,128)(2,1)}, bf16[128,2048]{1,0:T(8,128)(2,1)S(1)}, u32[]{:S(2)}, u32[]{:S(2)}) collective-permute-start(bf16[128,2048]{1,0:T(8,128)(2,1)} %collective-permute-done.25.refs_3_), channel_id=1, source_target_pairs={{0,4},{4,0},{1,5},{5,1},{2,6},{6,2},{3,7},{7,3},{8,12},{12,8},{9,1... | collective-permute-start | bytes 1572872 | tf_op jit(solution)/shard_map/ppermute | solution.py:423
  147.2 17.1 %copy-start.13 = (f32[4096]{0:T(1024)S(1)}, f32[4096]{0:T(1024)}, u32[]{:S(2)}) copy-start(f32[4096]{0:T(1024)} %param.23) | copy-start | bytes 49156
  147.2 9.7 %collective-permute-start.34 = (bf16[256,1024]{1,0:T(8,128)(2,1)S(1)}, bf16[256,1024]{1,0:T(8,128)(2,1)}, u32[]{:S(2)}, u32[]{:S(2)}) collective-permute-start(bf16[256,1024]{1,0:T(8,128)(2,1)S(1)} %shard_map.160.refs_0_), channel_id=1, source_target_pairs={{0,32},{4,12},{8,40},{12,20},{16,48},{20,28},{24,56},{28,4},{32,64... | collective-permute-start | bytes 1572872 | tf_op jit(solution)/shard_map/ppermute | solution.py:418
  148.0 15.1 %collective-permute-start.35 = (bf16[256,1024]{1,0:T(8,128)(2,1)S(1)}, bf16[256,1024]{1,0:T(8,128)(2,1)}, u32[]{:S(2)}, u32[]{:S(2)}) collective-permute-start(bf16[256,1024]{1,0:T(8,128)(2,1)S(1)} %shard_map.160.refs_0_), channel_id=1, source_target_pairs={{0,64},{4,20},{8,72},{12,28},{16,80},{20,4},{24,88},{28,12},{32,96... | collective-permute-start | bytes 1572872 | tf_op jit(solution)/shard_map/ppermute | solution.py:418
  150.4 13.8 %collective-permute-start.36 = (bf16[256,1024]{1,0:T(8,128)(2,1)S(1)}, bf16[256,1024]{1,0:T(8,128)(2,1)}, u32[]{:S(2)}, u32[]{:S(2)}) collective-permute-start(bf16[256,1024]{1,0:T(8,128)(2,1)S(1)} %shard_map.160.refs_0_), channel_id=1, source_target_pairs={{0,96},{4,28},{8,104},{12,4},{16,112},{20,12},{24,120},{28,20},{32... | collective-permute-start | bytes 1572872 | tf_op jit(solution)/shard_map/ppermute | solution.py:418
  153.2 2.0 %copy-start = (bf16[1024,2048]{1,0:T(8,128)(2,1)}, bf16[1024,2048]{1,0:T(8,128)(2,1)S(1)}, u32[]{:S(2)}) copy-start(bf16[1024,2048]{1,0:T(8,128)(2,1)S(1)} %shard_map.159.held_ref) | copy-start | bytes 12582916
  155.2 14.5 %collective-permute-start.30 = (f32[32,1024]{1,0:T(8,128)S(1)}, f32[32,1024]{1,0:T(8,128)S(1)}, u32[]{:S(2)}, u32[]{:S(2)}) collective-permute-start(f32[32,1024]{1,0:T(8,128)S(1)} %get-tuple-element.74), channel_id=1, source_target_pairs={{0,4},{4,0},{1,5},{5,1},{2,6},{6,2},{3,7},{7,3},{8,12},{12,8},{9,1... | collective-permute-start | bytes 393224 | tf_op jit(solution)/shard_map/ppermute | solution.py:423
  156.5 13.2 %collective-permute-start.37 = (bf16[256,1024]{1,0:T(8,128)(2,1)S(1)}, bf16[256,1024]{1,0:T(8,128)(2,1)S(1)}, u32[]{:S(2)}, u32[]{:S(2)}) collective-permute-start(bf16[256,1024]{1,0:T(8,128)(2,1)S(1)} %shard_map.160.refs_0_), channel_id=1, source_target_pairs={{0,4},{4,0},{1,5},{5,1},{2,6},{6,2},{3,7},{7,3},{8,12},{12,8},{9,1... | collective-permute-start | bytes 1572872 | tf_op jit(solution)/shard_map/ppermute | solution.py:423
  156.9 12.8 %collective-permute-start.38 = (bf16[256,1024]{1,0:T(8,128)(2,1)}, bf16[256,1024]{1,0:T(8,128)(2,1)S(1)}, u32[]{:S(2)}, u32[]{:S(2)}) collective-permute-start(bf16[256,1024]{1,0:T(8,128)(2,1)} %collective-permute-done.34.refs_1_), channel_id=1, source_target_pairs={{0,4},{4,0},{1,5},{5,1},{2,6},{6,2},{3,7},{7,3},{8,12},{12,8},{9,1... | collective-permute-start | bytes 1572872 | tf_op jit(solution)/shard_map/ppermute | solution.py:423
  163.0 6.7 %collective-permute-start.39 = (bf16[256,1024]{1,0:T(8,128)(2,1)}, bf16[256,1024]{1,0:T(8,128)(2,1)S(1)}, u32[]{:S(2)}, u32[]{:S(2)}) collective-permute-start(bf16[256,1024]{1,0:T(8,128)(2,1)} %collective-permute-done.35.refs_2_), channel_id=1, source_target_pairs={{0,4},{4,0},{1,5},{5,1},{2,6},{6,2},{3,7},{7,3},{8,12},{12,8},{9,1... | collective-permute-start | bytes 1572872 | tf_op jit(solution)/shard_map/ppermute | solution.py:423
  164.2 5.5 %collective-permute-start.40 = (bf16[256,1024]{1,0:T(8,128)(2,1)}, bf16[256,1024]{1,0:T(8,128)(2,1)}, u32[]{:S(2)}, u32[]{:S(2)}) collective-permute-start(bf16[256,1024]{1,0:T(8,128)(2,1)} %collective-permute-done.36.refs_3_), channel_id=1, source_target_pairs={{0,4},{4,0},{1,5},{5,1},{2,6},{6,2},{3,7},{7,3},{8,12},{12,8},{9,1... | collective-permute-start | bytes 1572872 | tf_op jit(solution)/shard_map/ppermute | solution.py:423
  164.3 1.2 copy-start.7
  165.5 4.2 %copy-start.1 = (bf16[1024,2048]{1,0:T(8,128)(2,1)S(1)}, bf16[1024,2048]{1,0:T(8,128)(2,1)}, u32[]{:S(2)}) copy-start(bf16[1024,2048]{1,0:T(8,128)(2,1)} %copy-done) | copy-start | bytes 12582916
  165.5 4.2 %copy-start.3 = (bf16[1024,2048]{1,0:T(8,128)(2,1)S(1)}, bf16[1024,2048]{1,0:T(8,128)(2,1)}, u32[]{:S(2)}) copy-start(bf16[1024,2048]{1,0:T(8,128)(2,1)} %w_ref.3) | copy-start | bytes 12582916

commit v2 on v1

v2 whole, which is shorter than its diff:
```python
import functools
import math

import jax
import jax.numpy as jnp
from jax import lax
from jax.experimental import pallas as pl
from jax.experimental.pallas import tpu as pltpu
from jax.sharding import Mesh
from jax.sharding import PartitionSpec as P


DP = ("dp_0", "dp_1", "dp_2")
DP_MP = ("dp_0", "dp_1", "dp_2", "mp")

clip_norm = 1.0
dense_rate = 0.02
table_rate = 0.5
adagrad_eps = 1e-10

F32 = jnp.float32
BF16 = jnp.bfloat16
VM = pl.BlockSpec(memory_space=pltpu.VMEM)
HBM = pl.BlockSpec(memory_space=pltpu.MemorySpace.HBM)


def iota(shape, dim):
    return lax.broadcasted_iota(jnp.int32, shape, dim)


def dot_f32(a, b, dims=(((1,), (0,)), ((), ()))):
    return lax.dot_general(a, b, dims, preferred_element_type=F32)


def spans_of(counts_ref):
    owners = counts_ref.shape[1]
    spread = jnp.broadcast_to(counts_ref[...].astype(F32), (owners, owners))
    at, of = iota((owners, owners), 0), iota((owners, owners), 1)
    ends = jnp.sum(jnp.where(of <= at, spread, 0.0), axis=1, keepdims=True)
    return ends - jnp.sum(jnp.where(of == at, spread, 0.0), axis=1, keepdims=True), ends


def gather_kernel(counts_hbm, lookups_hbm, slab_hbm, out_ref, counts_ref, lookups_ref, slab_ref, sems):
    copies = [
        pltpu.make_async_copy(a, b, sems.at[k])
        for k, (a, b) in enumerate(
            ((counts_hbm, counts_ref), (lookups_hbm, lookups_ref), (slab_hbm, slab_ref))
        )
    ]
    for copy in copies:
        copy.start()
    features, batch = lookups_ref.shape
    copies[0].wait()
    copies[1].wait()
    halfway = slab_ref.shape[1] // 2
    starts, ends = spans_of(counts_ref)
    copies[2].wait()
    halves = jnp.concatenate([slab_ref[:, :halfway], slab_ref[:, halfway:]], axis=0)
    low_lane = iota((batch, 128), 1) < 64

    def pair(p, carry):
        hots, inners = [], []
        for parity in range(2):
            q = lookups_ref[pl.ds(2 * p + parity, 1), :].astype(F32)
            match = (q >= starts) & (q < ends)
            slot = q - jnp.sum(jnp.where(match, starts, 0.0), axis=0, keepdims=True)
            upper = slot >= 16.0
            hot = jnp.where(match, 1.0, 0.0)
            hots.append(
                jnp.concatenate([jnp.where(upper, 0.0, hot), jnp.where(upper, hot, 0.0)], axis=0).astype(BF16)
            )
            inners.append(jnp.where(upper, slot - 16.0, slot))
        inner = jnp.concatenate([*inners, jnp.zeros((6, batch), F32)], axis=0).T
        both = []
        for parity in range(2):
            rows = dot_f32(hots[parity], halves, (((0,), (0,)), ((), ())))
            place = jnp.broadcast_to(inner[:, parity : parity + 1], (batch, 128))
            block = jnp.floor(place * 0.5)
            found = rows[:, :128]
            for k in range(1, 8):
                found = jnp.where(block == float(k), rows[:, 128 * k : 128 * (k + 1)], found)
            swap = place - 2.0 * block != float(parity)
            both.append(jnp.where(swap, pltpu.roll(found, 64, 1), found))
        out_ref[:, pl.ds(pl.multiple_of(p * 128, 128), 128)] = jnp.where(low_lane, both[0], both[1]).astype(BF16)
        return carry

    lax.fori_loop(0, features // 2, pair, 0, unroll=4)


def gather_rows(counts, lookups_t, slab):
    features, batch = lookups_t.shape
    return pl.pallas_call(
        gather_kernel,
        out_shape=jax.ShapeDtypeStruct((batch, features * 64), BF16),
        in_specs=[HBM, HBM, HBM],
        out_specs=VM,
        scratch_shapes=[
            pltpu.VMEM(counts.shape, counts.dtype),
            pltpu.VMEM(lookups_t.shape, lookups_t.dtype),
            pltpu.VMEM(slab.shape, slab.dtype),
            pltpu.SemaphoreType.DMA((3,)),
        ],
        name="gather_rows",
        compiler_params=pltpu.CompilerParams(vmem_limit_bytes=16 * 2**20),
        cost_estimate=pl.CostEstimate(flops=6 * 10**9, transcendentals=0, bytes_accessed=2 * 10**6),
    )(counts, lookups_t, slab)


def slot_kernel(
    capacity, counts_ref, lookups_ref, own_ref, a_ref, b_ref, c_ref, out_ref, square_ref, value_ref, at_ref
):
    owners = counts_ref.shape[1]
    features, batch = lookups_ref.shape
    spread = jnp.broadcast_to(counts_ref[...].astype(F32), (owners, owners))
    at, of = iota((owners, owners), 0), iota((owners, owners), 1)
    ends = jnp.sum(jnp.where(of <= at, spread, 0.0), axis=1, keepdims=True)
    starts = ends - jnp.sum(jnp.where(of == at, spread, 0.0), axis=1, keepdims=True)
    moves = iota((owners, 1), 0).astype(F32) * float(capacity) - starts
    indices = []
    for f in range(features):
        q = lookups_ref[f : f + 1, :].astype(F32)
        match = (q >= starts) & (q < ends)
        indices.append(q + jnp.sum(jnp.where(match, moves, 0.0), axis=0, keepdims=True))
        at_ref[0:1, batch * f : batch * (f + 1)] = jnp.floor(indices[f] * 0.5)
    index = jnp.concatenate(indices, axis=0)
    odd = (index - 2.0 * jnp.floor(index * 0.5)).T
    low_lane = iota((batch, 128), 1) < 64
    lane_odd = jnp.where(low_lane, 0.0, 1.0)
    for pair in range(features // 2):
        cols = slice(128 * pair, 128 * (pair + 1))
        total = own_ref[:, cols]
        for piece_ref in (a_ref, b_ref, c_ref):
            total = total + piece_ref[:, cols].astype(F32)
        turned = pltpu.roll(total, 64, 1)
        for parity in range(2):
            f = 2 * pair + parity
            rows = jnp.where(low_lane, total, turned) if parity == 0 else jnp.where(low_lane, turned, total)
            rows = jnp.where(jnp.broadcast_to(odd[:, f : f + 1], (batch, 128)) == lane_odd, rows, 0.0)
            high = rows.astype(BF16)
            value_ref[batch * f : batch * (f + 1), 0:128] = high
            value_ref[batch * f : batch * (f + 1), 128:256] = (rows - high.astype(F32)).astype(BF16)
    block = 512
    each = block * 2 // capacity
    where = jnp.broadcast_to(at_ref[...], (block, features * batch))
    lines = iota((block, features * batch), 0).astype(F32)

    def part(m, square):
        hot = jnp.where(lines == where - (m * block).astype(F32), 1.0, 0.0).astype(BF16)
        both = dot_f32(hot, value_ref[...])
        sums = both[:, 0:128] + both[:, 128:256]
        first = pl.multiple_of(m * each, each)
        out_ref[pl.ds(first, each), :, :] = sums.astype(BF16).reshape(each, capacity // 2, 128)
        return square + jnp.sum(jnp.sum(sums * sums, axis=1, keepdims=True), axis=0, keepdims=True)

    square = lax.fori_loop(0, owners // each, part, jnp.zeros((1, 1), F32))
    square_ref[...] = jnp.broadcast_to(square, square_ref.shape)


def final_kernel(
    rates,
    arrived_ref,
    rows_ref,
    mine_ref,
    theirs_ref,
    table_hbm,
    accum_hbm,
    w_hbm,
    held_hbm,
    grad_hbm,
    table_out,
    accum_out,
    w_out_hbm,
    dense_out,
    acc_ref,
    table_ref,
    accum_ref,
    w_ref,
    held_ref,
    grad_ref,
    sems,
    in_sems,
    out_sems,
):
    rate, dense, eps, clip = rates
    size = 64
    count = w_ref.shape[0] // size
    copies = [
        pltpu.make_async_copy(a, b, sems.at[k])
        for k, (a, b) in enumerate(((table_hbm, table_ref), (accum_hbm, accum_ref)))
    ]
    for copy in copies:
        copy.start()
    sides = ((w_hbm, w_ref), (held_hbm, held_ref), (grad_hbm, grad_ref))

    def fetch(k):
        at = pl.ds(pl.multiple_of(k * size, size), size)
        return [pltpu.make_async_copy(a.at[at, :], b.at[at, :], in_sems.at[m, k]) for m, (a, b) in enumerate(sides)]

    def begin(k, carry):
        for copy in fetch(k):
            copy.start()
        return carry

    lax.fori_loop(0, count, begin, 0)
    sources, lines, _ = arrived_ref.shape
    half = lines - 8
    capacity = 2 * half
    rows = table_ref.shape[1]
    blocks = rows // 256
    every = sources * half
    info = arrived_ref[:, half:, :].reshape(sources * 8, 128)
    squares = jnp.sum(info.astype(F32)[:, 2 * capacity : 2 * capacity + 3], axis=0, keepdims=True)
    total = jnp.sum(squares, axis=1, keepdims=True) * 0.125
    scale = clip / jnp.maximum(jnp.sqrt(total), clip)
    share = jnp.where(iota((sources * 8, every), 0) >> 3 == iota((sources * 8, every), 1) // half, 0.125, 0.0)
    spread_info = dot_f32(info, share.astype(BF16), (((0,), (0,)), ((), ())))
    slot = iota((capacity, every), 0)
    line = iota((capacity, every), 1) & (half - 1)
    inside_at = iota((256, every), 0).astype(F32)
    turned = arrived_ref[:, :half, :].reshape(every, 128).astype(F32).T
    acc = None
    for parity in range(2):
        mine = slot == 2 * line + parity
        block = jnp.sum(jnp.where(mine, spread_info[0:capacity], 0.0), axis=0, keepdims=True)
        inside = jnp.sum(jnp.where(mine, spread_info[capacity : 2 * capacity], 0.0), axis=0, keepdims=True)
        piece = turned[64 * parity : 64 * (parity + 1), :]
        hot = jnp.where(inside_at == inside, 1.0, 0.0).astype(BF16)
        spread = jnp.concatenate([jnp.where(block == float(k), piece, 0.0).astype(BF16) for k in range(blocks)], axis=0)
        part = dot_f32(spread, hot, (((1,), (1,)), ((), ())))
        acc = part if acc is None else acc + part
    acc_ref[...] = acc
    for copy in copies:
        copy.wait()

    def finish(k, carry):
        received = scale * acc_ref[pl.ds(pl.multiple_of(64 * k, 64), 64), :]
        cols = pl.ds(pl.multiple_of(256 * k, 256), 256)
        accum = accum_ref[:, cols] + jnp.sum(received * received, axis=0, keepdims=True) * (1.0 / 64.0)
        accum_out[:, cols] = accum
        table_out[:, cols] = table_ref[:, cols] - rate * received / (accum * lax.rsqrt(accum) + eps)
        return carry

    lax.fori_loop(0, blocks, finish, 0, unroll=2)

    def update(k, carry):
        for copy in fetch(k):
            copy.wait()
        at = pl.ds(pl.multiple_of(k * size, size), size)
        grad = scale * grad_ref[at, :].astype(F32)
        accum = held_ref[at, :].astype(F32) + grad * grad
        step = dense * grad / (accum * lax.rsqrt(accum) + eps)
        w_ref[at, :] = (w_ref[at, :].astype(F32) - step).astype(BF16)
        pltpu.make_async_copy(w_ref.at[at, :], w_out_hbm.at[at, :], out_sems.at[k]).start()
        return carry

    lax.fori_loop(0, count, update, 0)
    core = lax.axis_index("dp_2")
    half = mine_ref.shape[1]
    for grad, c in ((mine_ref[...], core), (theirs_ref[...], 1 - core)):
        cols = pl.ds(pl.multiple_of(c * half, half), half)
        grad = scale * grad
        dense_out[:, cols] = rows_ref[:, cols] + grad * grad

    def drain(k, carry):
        at = pl.ds(pl.multiple_of(k * size, size), size)
        pltpu.make_async_copy(w_ref.at[at, :], w_out_hbm.at[at, :], out_sems.at[k]).wait()
        return carry

    lax.fori_loop(0, count, drain, 0)


def footprint(shapes):
    return sum(math.prod(s.shape) * 4 for s in shapes)


def call(kernel, outs, flops, args, scratch=(), spare=8, far=(), far_out=(), aliases=None):
    shapes = tuple(jax.ShapeDtypeStruct(s, t) for s, t in outs)
    return pl.pallas_call(
        kernel,
        out_shape=shapes,
        in_specs=[HBM if k in far else VM for k in range(len(args))],
        out_specs=tuple(HBM if k in far_out else VM for k in range(len(shapes))),
        scratch_shapes=list(scratch),
        input_output_aliases=aliases or {},
        compiler_params=pltpu.CompilerParams(vmem_limit_bytes=footprint(scratch) + spare * 2**20),
        cost_estimate=pl.CostEstimate(flops=flops, transcendentals=0, bytes_accessed=2 * 10**6),
    )(*args)


SHIFTS = (1, 3, 2)


def spot(axis, shift):
    return lax.rem(lax.axis_index(axis) + shift, 4)


def sigmoid(x):
    return 0.5 * jnp.tanh(0.5 * x) + 0.5


def forward_kernel(chunks, *refs):
    ins, (w_ref, bias_ref, out_w_ref) = refs[:chunks], refs[chunks : chunks + 3]
    slope_ref, hidden_ref, logit_ref, turned_ref, rows_ref = refs[chunks + 3 :]
    rows = ins[0].shape[0]
    width = w_ref.shape[1]
    for k in range(chunks):
        rows_ref[rows * k : rows * (k + 1), :] = ins[k][...]
        turned_ref[:, rows * k : rows * (k + 1)] = ins[k][...].T

    def columns(n, carry):
        cols = pl.ds(pl.multiple_of(n * 256, 256), 256)
        act = dot_f32(rows_ref[...], w_ref[:, cols]) + bias_ref[:, cols]
        sigma = sigmoid(act)
        hidden_ref[:, cols] = (act * sigma).astype(BF16)
        slope_ref[:, cols] = out_w_ref[:, cols].astype(F32) * sigma * (1.0 + act * (1.0 - sigma))
        return carry

    lax.fori_loop(0, width // 256, columns, 0, unroll=8)
    out_w = jnp.broadcast_to(out_w_ref[...], (16, width))
    for k in range(logit_ref.shape[0]):
        part = dot_f32(out_w, hidden_ref[256 * k : 256 * (k + 1), :], (((1,), (1,)), ((), ())))
        logit_ref[k : k + 1, :] = part[0:1, :]


def forward(chunks, w, bias, out_w):
    rows, depth = chunks[0].shape
    width = w.shape[1]
    n = len(chunks)
    total = n * rows
    outs = [((total, width), F32), ((total, width), BF16), ((total // 256, 256), F32), ((depth, total), BF16)]
    return call(
        functools.partial(forward_kernel, n),
        outs,
        total * 10**7,
        (*chunks, w, bias, out_w),
        [pltpu.VMEM((total, depth), BF16)],
    )


ORDER = (0, 3, 1, 2)
PARTNERS = ((0, 1, 2, 3), (2, 0, 3, 1), (1, 3, 0, 2), (3, 2, 1, 0))


def slope_kernel(*refs):
    slopes, hiddens = refs[0:3], refs[3:6]
    own_ref, prev_ref, next_ref, far_ref, labels_ref, weight_ref = refs[6:12]
    dact_ref, other_ref, sums_mine_ref, sums_other_ref, sums_ref = refs[12:]
    rows, width = slopes[0].shape
    spans = ((0, 0), (1, 0), (1, rows), (2, 0))
    half = width // 2
    core = lax.axis_index("dp_2")
    dlogits = []
    for k in range(4):
        at = spot("mp", ORDER[k])
        logit = (own_ref[k : k + 1, :] + far_ref[PARTNERS[3][k] : PARTNERS[3][k] + 1, :]) + (
            prev_ref[PARTNERS[1][k] : PARTNERS[1][k] + 1, :] + next_ref[PARTNERS[2][k] : PARTNERS[2][k] + 1, :]
        )
        here = pl.ds(pl.multiple_of(at * rows, rows), rows)
        label = labels_ref[:, here].astype(F32)
        dlogits.append(weight_ref[:, here] * (sigmoid(logit) - label))
    rows_form = jnp.concatenate(dlogits + [jnp.zeros((4, rows), F32)], axis=0)
    cols_form = rows_form.T
    pick = iota((16, rows), 0)
    ones = jnp.ones((16, rows), BF16)
    cols, lefts = [], []
    for k in range(4):
        cols.append(cols_form[:, k : k + 1])
        top = dlogits[k].astype(BF16).astype(F32)
        rest = dlogits[k] - top
        lefts.append(jnp.where(pick == 0, top, jnp.where(pick == 1, rest, 0.0)).astype(BF16))
    block = 256
    line = iota((16, block), 0)

    def columns(n, carry):
        span = pl.ds(pl.multiple_of(n * block, block), block)
        bias_sum = out_sum = jnp.zeros((16, block), F32)
        for k in range(4):
            which, start = spans[k]
            part = (slopes[which][start : start + rows, span] * cols[k]).astype(BF16)
            dact_ref[rows * k : rows * (k + 1), span] = part
            bias_sum = bias_sum + dot_f32(ones, part)
            out_sum = out_sum + dot_f32(lefts[k], hiddens[which][start : start + rows, span])
        total = jnp.sum(out_sum, axis=0, keepdims=True)
        sums_ref[:, span] = jnp.where(line == 0, bias_sum, jnp.where(line == 1, total, 0.0))
        return carry

    lax.fori_loop(0, width // block, columns, 0)
    other_ref[...] = dact_ref[:, pl.ds(pl.multiple_of((1 - core) * half, half), half)]
    sums_mine_ref[...] = sums_ref[:, pl.ds(pl.multiple_of(core * half, half), half)]
    sums_other_ref[...] = sums_ref[:, pl.ds(pl.multiple_of((1 - core) * half, half), half)]


def back_kernel(dact_ref, w_ref, own_ref, *outs):
    rows, depth = own_ref.shape
    block = 512

    def columns(n, carry):
        span = pl.ds(pl.multiple_of(n * block, block), block)
        part = dot_f32(dact_ref[...], w_ref[span, :], (((1,), (1,)), ((), ())))
        for k, target in enumerate((own_ref, *outs)):
            target[:, span] = part[rows * k : rows * (k + 1), :].astype(target.dtype)
        return carry

    lax.fori_loop(0, depth // block, columns, 0)


def spot_on(first, core, shift):
    x, y = lax.axis_index("dp_0"), lax.axis_index("dp_1")
    along = x * (1 - core) + y * core if first else y * (1 - core) + x * core
    return lax.rem(along + shift, 4)


def chip_rows(core, outer, inner, size):
    return pl.multiple_of((outer * (4 - 3 * core) + inner * (1 + 3 * core)) * size, size)


def grad_kernel(shifts, *refs):
    turned, (dact_ref, far_dact_ref, sums_ref, far_sums_ref), outs = refs[0:6], refs[6:10], refs[10:]
    size = turned[0].shape[0] // 16
    half = far_dact_ref.shape[1]
    spans = ((0, 256), (256, 512), (768, 256))
    core = lax.axis_index("dp_2")
    local = pl.ds(pl.multiple_of(core * half, half), half)
    for target, shift in zip(outs, shifts):
        at = [pl.ds(chip_rows(core, spot_on(True, core, shift), t, size), size) for t in range(4)]
        part = None
        for i, (s, n) in enumerate(spans):
            near = jnp.concatenate([turned[i][a, :] for a in at], axis=0)
            away = jnp.concatenate([turned[i + 3][a, :] for a in at], axis=0)
            p = dot_f32(near, dact_ref[s : s + n, local]) + dot_f32(away, far_dact_ref[s : s + n, :])
            part = p if part is None else part + p
        target[0:256, :] = part.astype(target.dtype)
        target[256:272, :] = split_rows(sums_ref[...] + far_sums_ref[...]).astype(target.dtype)


def split_rows(sums):
    top = sums.astype(BF16).astype(F32)
    return jnp.concatenate([top[0:8], (sums - top)[0:8]], axis=0)


def joined_rows(rows):
    return jnp.concatenate([rows[0:8] + rows[8:16], jnp.zeros_like(rows[0:8])], axis=0)


def middle_kernel(own_ref, a_ref, b_ref, c_ref, out_ref):
    total = own_ref[...] + a_ref[...].astype(F32) + b_ref[...].astype(F32) + c_ref[...].astype(F32)
    out_ref[0:256, :] = total[0:256].astype(BF16)
    out_ref[256:272, :] = split_rows(joined_rows(total[256:272])).astype(BF16)


def last_kernel(
    own_ref,
    before_ref,
    after_ref,
    far_ref,
    sums_ref,
    ids_ref,
    slot_square_ref,
    narrow_ref,
    mine_ref,
    other_ref,
    out_ref,
    full_ref,
):
    core = lax.axis_index("dp_2")
    at = spot_on(False, core, 0)
    even = lax.rem(at, 2) == 0
    before, after = before_ref[...].astype(F32), after_ref[...].astype(F32)
    partner, other = jnp.where(even, after, before), jnp.where(even, before, after)
    total = (own_ref[...].astype(F32) + partner) + (other + far_ref[...].astype(F32))
    count = narrow_ref.shape[0]
    extra = joined_rows(total[count:])
    full_ref[...] = total[:count]
    narrow_ref[...] = total[:count].astype(BF16)
    size = count // 4
    per = size // 2
    chunk = full_ref[pl.ds(pl.multiple_of(at * size, size), size), :]
    mine_ref[...] = full_ref[pl.ds(pl.multiple_of(at * size + core * per, per), per), :]
    other_ref[...] = full_ref[pl.ds(pl.multiple_of(at * size + (1 - core) * per, per), per), :]
    lead = jnp.where((lax.axis_index("dp_0") == 0) & (lax.axis_index("dp_1") == 0), 1.0, 0.0)
    square = slot_square_ref[0:1, 0:1] + jnp.sum(jnp.sum(chunk * chunk, axis=1, keepdims=True), axis=0, keepdims=True)
    square = square + lead * jnp.sum(jnp.sum(extra * extra, axis=1, keepdims=True), axis=0, keepdims=True)
    owners, capacity = ids_ref.shape
    lines = capacity // 2
    top = square.astype(BF16).astype(F32)
    mid = (square - top).astype(BF16).astype(F32)
    end = square - top - mid
    ids = ids_ref[...]
    lane = iota((owners, 128 - 2 * capacity), 1)
    tail = jnp.where(lane == 0, top, jnp.where(lane == 1, mid, jnp.where(lane == 2, end, 0.0)))
    info = jnp.concatenate([(ids >> 8).astype(F32), (ids & 255).astype(F32), tail], axis=1)
    out_ref[:, :lines, :] = sums_ref[...]
    out_ref[:, lines:, :] = jnp.broadcast_to(info[:, None, :], (owners, 8, 128)).astype(BF16)


def pack_kernel(*refs):
    rows = refs[0].shape[0]
    for k in range(4):
        refs[4][rows * k : rows * (k + 1), :] = refs[k][...]


def merge_kernel(*refs):
    stacks, out_ref = refs[:8], refs[8]
    core = lax.axis_index("dp_2")
    per = stacks[0].shape[0] // 4
    for side, c in ((0, core), (1, 1 - core)):
        for i in range(4):
            for j in range(4):
                at = chip_rows(c, spot_on(True, c, (4 - i) % 4), spot_on(False, c, (4 - j) % 4), 1)
                rows = pl.ds(pl.multiple_of((at * 2 + c) * per, per), per)
                out_ref[rows, :] = stacks[4 * side + i][per * j : per * (j + 1), :]


def grad_merge_kernel(*refs):
    stacks, out_ref = refs[:8], refs[8]
    core = lax.axis_index("dp_2")
    size = stacks[0].shape[0] // 4
    half = stacks[0].shape[1]
    for side, c in ((0, core), (1, 1 - core)):
        cols = pl.ds(pl.multiple_of(c * half, half), half)
        for i in range(4):
            outer = spot_on(True, c, (4 - i) % 4)
            for j in range(4):
                out_ref[pl.ds(chip_rows(c, outer, j, size), size), cols] = stacks[4 * side + i][size * j : size * (j + 1), :]


def cross(x, first, shift):
    moves = []
    for i in range(32):
        a, b, c = i // 8, i // 2 % 4, i % 2
        a, b = ((a + shift) % 4, b) if (c == 0) == first else (a, (b + shift) % 4)
        moves.append((i, a * 8 + b * 2 + c))
    return lax.ppermute(x, DP, moves)


def send(x, axis, shift):
    n = lax.axis_size(axis)
    return lax.ppermute(x, axis, [(i, (i + shift) % n) for i in range(n)])


def around(x, axis):
    return [send(x, axis, s) for s in SHIFTS]


def inner(
    slab_values,
    row_ids,
    peer_counts,
    lookup_slots,
    labels,
    sample_weight,
    weight_in,
    bias_in,
    weight_out,
    dense_accum,
    table_rows,
    table_accum,
):
    batch, features = lookup_slots.shape
    depth, width = weight_in.shape
    half = width // 2
    lookups_t = lookup_slots.T
    pooled = gather_rows(peer_counts, lookups_t, slab_values[0])
    before, after = send(pooled, "mp", 1), send(pooled, "mp", 3)
    narrow = dense_accum.astype(BF16)
    parts = {s: cross(narrow, False, s) for s in SHIFTS}
    block = (depth // 8, width)
    near = call(pack_kernel, [(block, BF16)], 10**8, (narrow, parts[1], parts[2], parts[3]))[0]
    stacks = {s: cross(near, True, s) for s in SHIFTS}
    stacks = [near, stacks[1], stacks[2], stacks[3]]
    stacks = stacks + [send(g, "dp_2", 1) for g in stacks]
    accum_full = call(merge_kernel, [((depth, width), BF16)], 10**8, stacks)[0]
    bias = bias_in.reshape(1, width)
    out_w = weight_out.reshape(1, width)
    far_low, far_high = send(before[: batch // 2], "mp", 1), send(after[batch // 2 :], "mp", 3)
    slope_0, hidden_0, logit_0, turned_0 = forward([pooled], weight_in, bias, out_w)
    slope_1, hidden_1, logit_1, turned_1 = forward([before, after], weight_in, bias, out_w)
    slope_2, hidden_2, logit_2, turned_2 = forward([far_low, far_high], weight_in, bias, out_w)
    turned = [turned_0, turned_1, turned_2]
    turned = turned + [send(t, "dp_2", 1) for t in turned]
    logits = jnp.concatenate([logit_0, logit_1, logit_2], axis=0)
    logit_before, logit_after, logit_far = around(logits, "mp")
    dact, other, sums_mine, sums_other = call(
        slope_kernel,
        [((4 * batch, width), BF16), ((4 * batch, half), BF16), ((16, half), F32), ((16, half), F32)],
        2 * 10**9,
        (
            slope_0,
            slope_1,
            slope_2,
            hidden_0,
            hidden_1,
            hidden_2,
            logits,
            logit_before,
            logit_after,
            logit_far,
            labels.reshape(1, -1),
            sample_weight.reshape(1, -1),
        ),
        [pltpu.VMEM((16, width), F32)],
    )
    far_dact = send(other, "dp_2", 1)
    far_sums = send(sums_other, "dp_2", 1)
    own, to_before, to_after, to_far = call(
        back_kernel, [((batch, depth), F32)] + [((batch, depth), BF16)] * 3, 4 * 10**9, (dact, weight_in)
    )
    from_after, from_before, from_far = send(to_before, "mp", 3), send(to_after, "mp", 1), send(to_far, "mp", 2)
    held = (*turned, dact, far_dact, sums_mine, far_sums)
    block = (depth // 4 + 16, half)
    to_next, to_prev = call(functools.partial(grad_kernel, SHIFTS[:2]), [(block, BF16)] * 2, 4 * 10**9, held)
    from_prev, from_next = cross(to_next, True, 1), cross(to_prev, True, 3)
    to_far, keep = call(functools.partial(grad_kernel, (2, 0)), [(block, BF16), (block, F32)], 4 * 10**9, held)
    distant = cross(to_far, True, 2)
    keep = call(middle_kernel, [(block, BF16)], 10**8, (keep, from_prev, from_next, distant))[0]
    got = [cross(keep, False, s) for s in SHIFTS]
    peers, capacity = row_ids.shape[1:]
    slot_sums, slot_square = call(
        functools.partial(slot_kernel, capacity),
        [((peers, capacity // 2, 128), BF16), ((8, 128), F32)],
        8 * 10**9,
        (peer_counts, lookups_t, own, from_before, from_after, from_far),
        [pltpu.VMEM((features * batch, 256), BF16), pltpu.VMEM((1, features * batch), F32)],
        24,
    )
    narrow, mine, others, outgoing = call(
        last_kernel,
        [((depth // 4, half), BF16)] + [((depth // 32, half), F32)] * 2 + [((peers, capacity // 2 + 8, 128), BF16)],
        10**8,
        (keep, *got, slot_sums, row_ids[0], slot_square),
        [pltpu.VMEM((depth // 4, half), F32)],
    )
    theirs = send(others, "dp_2", 1)
    stacks = {s: cross(narrow, True, s) for s in SHIFTS}
    stacks = [narrow, stacks[1], stacks[2], stacks[3]]
    stacks = stacks + [send(g, "dp_2", 1) for g in stacks]
    arrived = lax.all_to_all(outgoing, DP_MP, 0, 0, tiled=True)
    grad_full = call(grad_merge_kernel, [((depth, width), BF16)], 10**8, stacks)[0]
    size = depth // 64
    table_t, accum_t, weight_new, accum_new = call(
        functools.partial(final_kernel, (table_rate, dense_rate, adagrad_eps, clip_norm)),
        [
            (table_rows.shape[::-1], F32),
            ((1, table_rows.shape[0]), F32),
            ((depth, width), BF16),
            (dense_accum.shape, F32),
        ],
        8 * 10**9,
        (
            arrived,
            dense_accum,
            mine,
            theirs,
            table_rows.T,
            table_accum.reshape(1, -1),
            weight_in,
            accum_full,
            grad_full,
        ),
        [
            pltpu.VMEM((table_rows.shape[0] // 4, 256), F32),
            pltpu.VMEM(table_rows.shape[::-1], F32),
            pltpu.VMEM((1, table_rows.shape[0]), F32),
            pltpu.VMEM((depth, width), BF16),
            pltpu.VMEM((depth, width), BF16),
            pltpu.VMEM((depth, width), BF16),
            pltpu.SemaphoreType.DMA((2,)),
            pltpu.SemaphoreType.DMA((3, size)),
            pltpu.SemaphoreType.DMA((size,)),
        ],
        33,
        (4, 5, 6, 7, 8),
        (2,),
    )
    return (weight_new, accum_new, table_t.T, accum_t.reshape(-1))


def solution(mesh):
    torus = Mesh(mesh.devices.reshape(4, 4, 2, mesh.shape["mp"]), ("dp_0", "dp_1", "dp_2", "mp"))
    placed = (
        P(DP_MP, None, None),
        P(DP_MP, None, None),
        P(DP_MP, None),
        P(DP_MP, None),
        P(DP),
        P(DP),
        P(None, "mp"),
        P("mp"),
        P("mp"),
        P(DP, "mp"),
        P(DP_MP, None),
        P(DP_MP),
    )
    return jax.shard_map(
        inner,
        mesh=torus,
        in_specs=placed,
        out_specs=(P(None, "mp"), P(DP, "mp"), P(DP_MP, None), P(DP_MP)),
        check_vma=False,
    )
```

time: 180 us -> 175 us (0.972)
  waiting for transfers between devices: 42.8 us -> 38 us
  starting transfers between devices: 68.9 us -> 73.3 us
  Pallas kernels: 53.7 us -> 49.7 us
    ppermute x23 -> x24, starting transfers between devices: 27.1 us -> 40.3 us  [send(): return lax.ppermute(x, axis, [(i, (i + shift) % n) for i in range(n)])]
    ppermute x18 -> x15, waiting for transfers between devices: 23.9 us -> 14.2 us  [cross(): return lax.ppermute(x, DP, moves)]
    all_to_all x1 -> x0, starting transfers between devices: 7.02 us -> none  [inner(): lax.all_to_all(sums.reshape(32, 1, 2 * width // 32), DP, 0, 0, tiled=True)]
    ppermute x18 -> x15, starting transfers between devices: 27.5 us -> 22.2 us  [cross(): return lax.ppermute(x, DP, moves)]
    pallas_call x15 -> x14, Pallas kernels: 50.4 us -> 45.5 us  [call(): pl.pallas_call(kernel, out_shape=shapes, in_specs=[HBM if k in far else V...]
    all_to_all x1, starting transfers between devices: 7.33 us -> 10.8 us  [inner(): arrived = lax.all_to_all(outgoing, DP_MP, 0, 0, tiled=True)]
    all_to_all x1, waiting for transfers between devices: 0.01 us -> 3.37 us  [inner(): arrived = lax.all_to_all(outgoing, DP_MP, 0, 0, tiled=True)]
    ppermute x23 -> x24, waiting for transfers between devices: 18.9 us -> 20.5 us  [send(): return lax.ppermute(x, axis, [(i, (i + shift) % n) for i in range(n)])]
  transfers between devices with their start and end apart: 43 -> 40, of which waited for: 13 -> 12; matrix products, arithmetic and copies ran while one was open for 1% -> 0% of each run, Pallas kernels for 17% -> 16%
where the time goes in v2:
time: 175 us; the launch traced here: 173 us
  starting transfers between devices  73.3 us (42%)
  Pallas kernels  49.7 us (28%)
  waiting for transfers between devices  38 us (22%)
  local copies, waits for them, and re-layouts  11.3 us (6%)
    pallas_call x14, Pallas kernels, call(): pl.pallas_call(kernel, out_shape=shapes, in_specs=[HBM if k in far else V...  45.5 us
    ppermute x24, starting transfers between devices, send(): return lax.ppermute(x, axis, [(i, (i + shift) % n) for i in range(n)])  40.3 us
    ppermute x15, starting transfers between devices, cross(): return lax.ppermute(x, DP, moves)  22.2 us
    ppermute x24, waiting for transfers between devices, send(): return lax.ppermute(x, axis, [(i, (i + shift) % n) for i in range(n)])  20.5 us
    ppermute x15, waiting for transfers between devices, cross(): return lax.ppermute(x, DP, moves)  14.2 us
    unnamed x41, local copies, waits for them, and re-layouts  11.2 us
    all_to_all x1, starting transfers between devices, inner(): arrived = lax.all_to_all(outgoing, DP_MP, 0, 0, tiled=True)  10.8 us
    pallas_call x1, Pallas kernels, gather_rows(): pl.pallas_call(gather_kernel, out_shape=jax.ShapeDtypeStruct((batch, feat...  4.14 us
  transfers between devices with their start and end apart: 40, of which 12 were waited for; matrix products, arithmetic and copies ran while one was open for 0% of the time, Pallas kernels for 16%

profile of v2, /device:TPU:1, one launch (start us, length us, event | category | flops | bytes accessed | tf_op | source)
XLA Modules:
  0.0 173.4 jit_solution(10396097947400934193)
XLA Ops:
  0.6 1.0 copy-done.7
  1.7 0.7 copy-done.9
  2.4 0.7 copy-done.12
  3.1 4.1 %gather_rows.1.refs_0_ = bf16[256,1024]{1,0:T(8,128)(2,1)S(1)} custom-call(s32[1,128]{1,0:T(1,128)S(1)} %copy-done.12, s32[16,256]{1,0:T(8,128)S(1)} %bitcast.14, bf16[128,2048]{1,0:T(8,128)(2,1)S(1)} %bitcast.13), custom_call_target="tpu_custom_call" | custom-call | flops 6000000000 | bytes 2000000 | tf_op jit(solution)/shard_map/gather_rows/pallas_call | solution.py:92
  7.2 2.5 %collective-permute-start = (bf16[256,1024]{1,0:T(8,128)(2,1)S(1)}, bf16[256,1024]{1,0:T(8,128)(2,1)S(1)}, u32[]{:S(2)}, u32[]{:S(2)}) collective-permute-start(bf16[256,1024]{1,0:T(8,128)(2,1)S(1)} %gather_rows.1.refs_0_), channel_id=1, source_target_pairs={{0,1},{1,2},{2,3},{3,0},{4,5},{5,6},{6,7},{7,4},{8,9},{9,10},{10,1... | collective-permute-start | bytes 1572872 | tf_op jit(solution)/shard_map/ppermute | solution.py:538
  9.7 2.2 %collective-permute-start.1 = (bf16[256,1024]{1,0:T(8,128)(2,1)S(1)}, bf16[256,1024]{1,0:T(8,128)(2,1)S(1)}, u32[]{:S(2)}, u32[]{:S(2)}) collective-permute-start(bf16[256,1024]{1,0:T(8,128)(2,1)S(1)} %gather_rows.1.refs_0_), channel_id=1, source_target_pairs={{0,3},{1,0},{2,1},{3,2},{4,7},{5,4},{6,5},{7,6},{8,11},{9,8},{10,9... | collective-permute-start | bytes 1572872 | tf_op jit(solution)/shard_map/ppermute | solution.py:538
  12.0 1.8 %shard_map.147 = (f32[256,2048]{1,0:T(8,128)S(1)}, bf16[256,2048]{1,0:T(8,128)(2,1)S(1)}, f32[1,256]{1,0:T(1,128)S(1)}, bf16[1024,256]{1,0:T(8,128)(2,1)S(1)}) custom-call(bf16[256,1024]{1,0:T(8,128)(2,1)S(1)} %gather_rows.1.refs_0_, bf16[1024,2048]{1,0:T(8,128)(2,1)S(1)} %copy-done.6, f32[1,2048]{1,0:T(1,128)S(1)} %bitcast.16, ...), custom_call_target="tpu_custom_call" | custom-call | flops 2560000000 | bytes 2000000 | tf_op jit(solution)/shard_map/pallas_call | solution.py:278
  13.8 9.7 %collective-permute-done.refs_0_ = bf16[256,1024]{1,0:T(8,128)(2,1)S(1)} collective-permute-done((bf16[256,1024]{1,0:T(8,128)(2,1)S(1)}, bf16[256,1024]{1,0:T(8,128)(2,1)S(1)}, u32[]{:S(2)}, u32[]{:S(2)}) %collective-permute-start) | collective-permute-done | bytes 524320 | tf_op jit(solution)/shard_map/ppermute | solution.py:538
  23.6 2.7 %collective-permute-start.3 = (bf16[128,1024]{1,0:T(8,128)(2,1)S(1)}, bf16[128,1024]{1,0:T(8,128)(2,1)S(1)}, u32[]{:S(2)}, u32[]{:S(2)}) collective-permute-start(bf16[128,1024]{1,0:T(8,128)(2,1)S(1)} %slice.9), channel_id=1, source_target_pairs={{0,3},{1,0},{2,1},{3,2},{4,7},{5,4},{6,5},{7,6},{8,11},{9,8},{10,9... | collective-permute-start | bytes 786440 | tf_op jit(solution)/shard_map/ppermute | solution.py:538
  26.3 3.9 %shard_map.148 = (f32[512,2048]{1,0:T(8,128)S(1)}, bf16[512,2048]{1,0:T(8,128)(2,1)S(1)}, f32[2,256]{1,0:T(2,128)S(1)}, bf16[1024,512]{1,0:T(8,128)(2,1)S(1)}) custom-call(bf16[256,1024]{1,0:T(8,128)(2,1)S(1)} %collective-permute-done.refs_0_, bf16[256,1024]{1,0:T(8,128)(2,1)S(1)} %collective-permute-done.1.refs_1_, bf16[1024,2048]{1,0:T(8,128)(2,1)S(1)} %copy-done.6, ...), custom_call_target="tpu_custom_call" | custom-call | flops 5120000000 | bytes 2000000 | tf_op jit(solution)/shard_map/pallas_call | solution.py:278
  30.3 1.1 collective-permute-done.2.refs_0_
  31.4 1.9 %shard_map.149 = (f32[256,2048]{1,0:T(8,128)S(1)}, bf16[256,2048]{1,0:T(8,128)(2,1)S(1)}, f32[1,256]{1,0:T(1,128)S(1)}, bf16[1024,256]{1,0:T(8,128)(2,1)S(1)}) custom-call(bf16[128,1024]{1,0:T(8,128)(2,1)S(1)} %collective-permute-done.2.refs_0_, bf16[128,1024]{1,0:T(8,128)(2,1)S(1)} %collective-permute-done.3.refs_1_, bf16[1024,2048]{1,0:T(8,128)(2,1)S(1)} %copy-done.6, ...), custom_call_target="tpu_custom_call" | custom-call | flops 2560000000 | bytes 2000000 | tf_op jit(solution)/shard_map/pallas_call | solution.py:278
  33.3 2.7 %collective-permute-start.8 = (f32[4,256]{1,0:T(4,128)S(1)}, f32[4,256]{1,0:T(4,128)S(1)}, u32[]{:S(2)}, u32[]{:S(2)}) collective-permute-start(f32[4,256]{1,0:T(4,128)S(1)} %pad_maximum_fusion.refs_6_), channel_id=1, source_target_pairs={{0,3},{1,0},{2,1},{3,2},{4,7},{5,4},{6,5},{7,6},{8,11},{9,8},{10,9... | collective-permute-start | bytes 12296 | tf_op jit(solution)/shard_map/ppermute | solution.py:538
  36.0 1.0 collective-permute-start.9
  37.0 3.0 %collective-permute-done.9.refs_9_ = f32[4,256]{1,0:T(4,128)S(1)} collective-permute-done((f32[4,256]{1,0:T(4,128)S(1)}, f32[4,256]{1,0:T(4,128)S(1)}, u32[]{:S(2)}, u32[]{:S(2)}) %collective-permute-start.9) | collective-permute-done | bytes 4128 | tf_op jit(solution)/shard_map/ppermute | solution.py:538
  40.0 2.8 %shard_map.150 = (bf16[1024,2048]{1,0:T(8,128)(2,1)S(1)}, bf16[1024,1024]{1,0:T(8,128)(2,1)S(1)}, f32[16,1024]{1,0:T(8,128)S(1)}, f32[16,1024]{1,0:T(8,128)S(1)}) custom-call(f32[256,2048]{1,0:T(8,128)S(1)} %get-tuple-element.41.refs_0_, f32[512,2048]{1,0:T(8,128)S(1)} %get-tuple-element.42.refs_1_, f32[256,2048]{1,0:T(8,128)S(1)} %get-tuple-element.43.refs_2_, ...), custom_call_target="tpu_custom_call" | custom-call | flops 2000000000 | bytes 2000000 | tf_op jit(solution)/shard_map/pallas_call | solution.py:278
  42.8 3.9 %collective-permute-start.10 = (bf16[1024,1024]{1,0:T(8,128)(2,1)S(1)}, bf16[1024,1024]{1,0:T(8,128)(2,1)S(1)}, u32[]{:S(2)}, u32[]{:S(2)}) collective-permute-start(bf16[1024,1024]{1,0:T(8,128)(2,1)S(1)} %get-tuple-element.51), channel_id=1, source_target_pairs={{0,4},{4,0},{1,5},{5,1},{2,6},{6,2},{3,7},{7,3},{8,12},{12,8},{9,1... | collective-permute-start | bytes 6291464 | tf_op jit(solution)/shard_map/ppermute | solution.py:538
  46.7 0.3 collective-permute-start.5
  47.2 0.3 collective-permute-start.6
  47.7 5.0 %collective-permute-done.4.refs_3_ = bf16[1024,256]{1,0:T(8,128)(2,1)S(1)} collective-permute-done((bf16[1024,256]{1,0:T(8,128)(2,1)S(1)}, bf16[1024,256]{1,0:T(8,128)(2,1)S(1)}, u32[]{:S(2)}, u32[]{:S(2)}) %collective-permute-start.4) | collective-permute-done | bytes 524320 | tf_op jit(solution)/shard_map/ppermute | solution.py:538
  52.7 0.8 collective-permute-done.11.refs_9_
  53.6 2.4 %shard_map.152 = (bf16[272,1024]{1,0:T(8,128)(2,1)S(1)}, bf16[272,1024]{1,0:T(8,128)(2,1)S(1)}) custom-call(bf16[1024,256]{1,0:T(8,128)(2,1)S(1)} %get-tuple-element.38.refs_0_, bf16[1024,512]{1,0:T(8,128)(2,1)S(1)} %get-tuple-element.39.refs_1_, bf16[1024,256]{1,0:T(8,128)(2,1)S(1)} %get-tuple-element.40.refs_2_, ...), custom_call_target="tpu_custom_call" | custom-call | flops 4000000000 | bytes 2000000 | tf_op jit(solution)/shard_map/pallas_call | solution.py:278
  55.9 1.4 collective-permute-start.12
  57.3 1.5 collective-permute-start.13
  58.9 2.4 %shard_map.151 = (bf16[272,1024]{1,0:T(8,128)(2,1)S(1)}, f32[272,1024]{1,0:T(8,128)S(1)}) custom-call(bf16[1024,256]{1,0:T(8,128)(2,1)S(1)} %get-tuple-element.38.refs_0_, bf16[1024,512]{1,0:T(8,128)(2,1)S(1)} %get-tuple-element.39.refs_1_, bf16[1024,256]{1,0:T(8,128)(2,1)S(1)} %get-tuple-element.40.refs_2_, ...), custom_call_target="tpu_custom_call" | custom-call | flops 4000000000 | bytes 2000000 | tf_op jit(solution)/shard_map/pallas_call | solution.py:278
  61.2 1.6 collective-permute-start.14
  62.9 1.3 collective-permute-start.22
  64.1 2.5 %collective-permute-start.23 = (bf16[32,2048]{1,0:T(8,128)(2,1)S(1)}, bf16[32,2048]{1,0:T(8,128)(2,1)S(1)}, u32[]{:S(2)}, u32[]{:S(2)}) collective-permute-start(bf16[32,2048]{1,0:T(8,128)(2,1)S(1)} %convert_element_type.3.refs_0_), channel_id=1, source_target_pairs={{0,16},{4,68},{8,24},{12,76},{16,0},{20,84},{24,8},{28,92},{32,48}... | collective-permute-start | bytes 393224 | tf_op jit(solution)/shard_map/ppermute | solution.py:533
  66.6 2.3 %collective-permute-done.22.refs_1_ = bf16[32,2048]{1,0:T(8,128)(2,1)S(1)} collective-permute-done((bf16[32,2048]{1,0:T(8,128)(2,1)S(1)}, bf16[32,2048]{1,0:T(8,128)(2,1)S(1)}, u32[]{:S(2)}, u32[]{:S(2)}) %collective-permute-start.22) | collective-permute-done | bytes 131104 | tf_op jit(solution)/shard_map/ppermute | solution.py:533
  68.9 2.0 %collective-permute-start.24 = (bf16[32,2048]{1,0:T(8,128)(2,1)S(1)}, bf16[32,2048]{1,0:T(8,128)(2,1)S(1)}, u32[]{:S(2)}, u32[]{:S(2)}) collective-permute-start(bf16[32,2048]{1,0:T(8,128)(2,1)S(1)} %convert_element_type.3.refs_0_), channel_id=1, source_target_pairs={{0,24},{4,100},{8,0},{12,108},{16,8},{20,116},{24,16},{28,124},{32... | collective-permute-start | bytes 393224 | tf_op jit(solution)/shard_map/ppermute | solution.py:533
  70.9 2.5 %collective-permute-done.23.refs_2_ = bf16[32,2048]{1,0:T(8,128)(2,1)S(1)} collective-permute-done((bf16[32,2048]{1,0:T(8,128)(2,1)S(1)}, bf16[32,2048]{1,0:T(8,128)(2,1)S(1)}, u32[]{:S(2)}, u32[]{:S(2)}) %collective-permute-start.23) | collective-permute-done | bytes 131104 | tf_op jit(solution)/shard_map/ppermute | solution.py:533
  73.5 1.8 %collective-permute-done.24.refs_3_ = bf16[32,2048]{1,0:T(8,128)(2,1)S(1)} collective-permute-done((bf16[32,2048]{1,0:T(8,128)(2,1)S(1)}, bf16[32,2048]{1,0:T(8,128)(2,1)S(1)}, u32[]{:S(2)}, u32[]{:S(2)}) %collective-permute-start.24) | collective-permute-done | bytes 131104 | tf_op jit(solution)/shard_map/ppermute | solution.py:533
  75.3 1.4 collective-permute-start.25
  76.7 2.4 %collective-permute-start.26 = (bf16[128,2048]{1,0:T(8,128)(2,1)S(1)}, bf16[128,2048]{1,0:T(8,128)(2,1)S(1)}, u32[]{:S(2)}, u32[]{:S(2)}) collective-permute-start(bf16[128,2048]{1,0:T(8,128)(2,1)S(1)} %shard_map.157.refs_0_), channel_id=1, source_target_pairs={{0,64},{4,20},{8,72},{12,28},{16,80},{20,4},{24,88},{28,12},{32,96... | collective-permute-start | bytes 1572872 | tf_op jit(solution)/shard_map/ppermute | solution.py:533
  79.5 5.7 %shard_map.154 = (f32[256,1024]{1,0:T(8,128)S(1)}, bf16[256,1024]{1,0:T(8,128)(2,1)}, bf16[256,1024]{1,0:T(8,128)(2,1)}, bf16[256,1024]{1,0:T(8,128)(2,1)}) custom-call(bf16[1024,2048]{1,0:T(8,128)(2,1)S(1)} %get-tuple-element.50.refs_6_.dact_ref, bf16[1024,2048]{1,0:T(8,128)(2,1)S(1)} %copy-done.6), custom_call_target="tpu_custom_call" | custom-call | flops 4000000000 | bytes 2000000 | tf_op jit(solution)/shard_map/pallas_call | solution.py:278
  85.2 1.0 copy-done.14
  86.2 2.7 %collective-permute-start.19 = (bf16[256,1024]{1,0:T(8,128)(2,1)}, bf16[256,1024]{1,0:T(8,128)(2,1)}, u32[]{:S(2)}, u32[]{:S(2)}) collective-permute-start(bf16[256,1024]{1,0:T(8,128)(2,1)} %get-tuple-element.60), channel_id=1, source_target_pairs={{0,3},{1,0},{2,1},{3,2},{4,7},{5,4},{6,5},{7,6},{8,11},{9,8},{10,9... | collective-permute-start | bytes 1572872 | tf_op jit(solution)/shard_map/ppermute | solution.py:538
  89.0 6.0 %collective-permute-done.26.refs_2_ = bf16[128,2048]{1,0:T(8,128)(2,1)S(1)} collective-permute-done((bf16[128,2048]{1,0:T(8,128)(2,1)S(1)}, bf16[128,2048]{1,0:T(8,128)(2,1)S(1)}, u32[]{:S(2)}, u32[]{:S(2)}) %collective-permute-start.26) | collective-permute-done | bytes 524320 | tf_op jit(solution)/shard_map/ppermute | solution.py:533
  95.1 0.9 collective-permute-done.18.a_ref
  95.9 11.8 %collective-permute-start.28 = (bf16[128,2048]{1,0:T(8,128)(2,1)S(1)}, bf16[128,2048]{1,0:T(8,128)(2,1)S(1)}, u32[]{:S(2)}, u32[]{:S(2)}) collective-permute-start(bf16[128,2048]{1,0:T(8,128)(2,1)S(1)} %shard_map.157.refs_0_), channel_id=1, source_target_pairs={{0,4},{4,0},{1,5},{5,1},{2,6},{6,2},{3,7},{7,3},{8,12},{12,8},{9,1... | collective-permute-start | bytes 1572872 | tf_op jit(solution)/shard_map/ppermute | solution.py:538
  107.7 4.9 %collective-permute-start.29 = (bf16[128,2048]{1,0:T(8,128)(2,1)S(1)}, bf16[128,2048]{1,0:T(8,128)(2,1)}, u32[]{:S(2)}, u32[]{:S(2)}) collective-permute-start(bf16[128,2048]{1,0:T(8,128)(2,1)S(1)} %collective-permute-done.25.refs_1_), channel_id=1, source_target_pairs={{0,4},{4,0},{1,5},{5,1},{2,6},{6,2},{3,7},{7,3},{8,12},{12,8},{9,1... | collective-permute-start | bytes 1572872 | tf_op jit(solution)/shard_map/ppermute | solution.py:538
  112.6 3.2 %collective-permute-start.16 = (bf16[272,1024]{1,0:T(8,128)(2,1)S(1)}, bf16[272,1024]{1,0:T(8,128)(2,1)S(1)}, u32[]{:S(2)}, u32[]{:S(2)}) collective-permute-start(bf16[272,1024]{1,0:T(8,128)(2,1)S(1)} %shard_map.153.own_ref), channel_id=1, source_target_pairs={{0,24},{4,100},{8,0},{12,108},{16,8},{20,116},{24,16},{28,124},{32... | collective-permute-start | bytes 1671176 | tf_op jit(solution)/shard_map/ppermute | solution.py:533
  115.7 1.5 collective-permute-start.17
  117.2 1.2 copy-done.15
  118.4 8.3 %shard_map.155 = (bf16[128,16,128]{2,1,0:T(8,128)(2,1)S(1)}, f32[8,128]{1,0:T(8,128)S(1)}) custom-call(s32[1,128]{1,0:T(1,128)S(1)} %copy-done.13, s32[16,256]{1,0:T(8,128)S(1)} %bitcast.15, f32[256,1024]{1,0:T(8,128)S(1)} %copy-done.15, bf16[256,1024]{1,0:T(8,128)(2,1)} %collective-permute-done.18.a_ref, bf16[256,1024]{1,0:T(8,128)(2,1)} %collective-permute-done.19.b_ref, ...), custom_call_target="tpu_custom_call" | custom-call | flops 8000000000 | bytes 2000000 | tf_op jit(solution)/shard_map/pallas_call | solution.py:278
  126.7 1.5 collective-permute-done.16.after_ref
  128.2 1.7 shard_map.156
  129.9 0.7 copy-done.8
  130.5 1.0 collective-permute-start.32
  131.6 1.2 collective-permute-start.33
  132.8 0.8 copy-done.2
  133.6 1.2 collective-permute-start.34
  134.8 10.8 %all-to-all-start = ((bf16[128,24,128]{2,1,0:T(8,128)(2,1)}), bf16[128,24,128]{2,1,0:T(8,128)(2,1)}, u32[]{:S(2)}, u32[]{:S(2)}) async-start(bf16[128,24,128]{2,1,0:T(8,128)(2,1)} %get-tuple-element.64), calls=%async_computation | async-start | bytes 1572864 | tf_op jit(solution)/shard_map/all_to_all | solution.py:637
  145.6 1.2 collective-permute-start.31
  146.9 0.4 collective-permute-start.36
  147.3 1.7 collective-permute-start.37
  149.0 1.4 collective-permute-start.38
  150.4 1.0 copy-done.3
  151.4 1.5 shard_map.158.held_hbm
  152.9 2.0 %copy-done = bf16[1024,2048]{1,0:T(8,128)(2,1)} copy-done((bf16[1024,2048]{1,0:T(8,128)(2,1)}, bf16[1024,2048]{1,0:T(8,128)(2,1)S(1)}, u32[]{:S(2)}) %copy-start) | copy-done | bytes 4194328
  154.9 1.7 shard_map.159.grad_hbm
  156.6 2.0 %copy-done.1 = bf16[1024,2048]{1,0:T(8,128)(2,1)} copy-done((bf16[1024,2048]{1,0:T(8,128)(2,1)}, bf16[1024,2048]{1,0:T(8,128)(2,1)S(1)}, u32[]{:S(2)}) %copy-start.1) | copy-done | bytes 4194328
  158.6 3.4 %all-to-all-done.arrived_ref = bf16[128,24,128]{2,1,0:T(8,128)(2,1)} async-done(((bf16[128,24,128]{2,1,0:T(8,128)(2,1)}), bf16[128,24,128]{2,1,0:T(8,128)(2,1)}, u32[]{:S(2)}, u32[]{:S(2)}) %all-to-all-start) | async-done | bytes 786464 | tf_op jit(solution)/shard_map/all_to_all | solution.py:637
  162.0 11.2 %shard_map.160 = (f32[64,4096]{1,0:T(8,128)}, f32[1,4096]{1,0:T(1,128)}, bf16[1024,2048]{1,0:T(8,128)(2,1)}, f32[32,2048]{1,0:T(8,128)}) custom-call(bf16[128,24,128]{2,1,0:T(8,128)(2,1)} %all-to-all-done.arrived_ref, f32[32,2048]{1,0:T(8,128)} %rows_ref.1, f32[32,1024]{1,0:T(8,128)} %copy-done.8, f32[32,1024]{1,0:T(8,128)} %copy-done.19, ...), custom_call_target="tpu_custom_call" | custom-call | flops 8000000000 | bytes 2000000 | tf_op jit(solution)/shard_map/pallas_call | solution.py:278
  (77 shorter events, 1.5 us)
Async XLA Ops:
  0.6 1.0 copy-start.7
  1.7 0.7 copy-start.9
  2.4 0.7 copy-start.12
  3.0 8.9 %copy-start.18 = (bf16[2048]{0:T(1024)(128)(2,1)S(1)}, bf16[2048]{0:T(1024)(128)(2,1)}, u32[]{:S(2)}) copy-start(bf16[2048]{0:T(1024)(128)(2,1)} %param.20) | copy-start | bytes 12292
  3.0 8.9 %copy-start.6 = (bf16[1024,2048]{1,0:T(8,128)(2,1)S(1)}, bf16[1024,2048]{1,0:T(8,128)(2,1)}, u32[]{:S(2)}) copy-start(bf16[1024,2048]{1,0:T(8,128)(2,1)} %w_hbm.1) | copy-start | bytes 12582916
  3.1 8.9 %copy-start.11 = (f32[2048]{0:T(1024)S(1)}, f32[2048]{0:T(1024)}, u32[]{:S(2)}) copy-start(f32[2048]{0:T(1024)} %param.19) | copy-start | bytes 24580
  7.2 16.3 %collective-permute-start = (bf16[256,1024]{1,0:T(8,128)(2,1)S(1)}, bf16[256,1024]{1,0:T(8,128)(2,1)S(1)}, u32[]{:S(2)}, u32[]{:S(2)}) collective-permute-start(bf16[256,1024]{1,0:T(8,128)(2,1)S(1)} %gather_rows.1.refs_0_), channel_id=1, source_target_pairs={{0,1},{1,2},{2,3},{3,0},{4,5},{5,6},{6,7},{7,4},{8,9},{9,10},{10,1... | collective-permute-start | bytes 1572872 | tf_op jit(solution)/shard_map/ppermute | solution.py:538
  9.7 13.8 %collective-permute-start.1 = (bf16[256,1024]{1,0:T(8,128)(2,1)S(1)}, bf16[256,1024]{1,0:T(8,128)(2,1)S(1)}, u32[]{:S(2)}, u32[]{:S(2)}) collective-permute-start(bf16[256,1024]{1,0:T(8,128)(2,1)S(1)} %gather_rows.1.refs_0_), channel_id=1, source_target_pairs={{0,3},{1,0},{2,1},{3,2},{4,7},{5,4},{6,5},{7,6},{8,11},{9,8},{10,9... | collective-permute-start | bytes 1572872 | tf_op jit(solution)/shard_map/ppermute | solution.py:538
  23.5 7.9 %collective-permute-start.2 = (bf16[128,1024]{1,0:T(8,128)(2,1)S(1)}, bf16[128,1024]{1,0:T(8,128)(2,1)S(1)}, u32[]{:S(2)}, u32[]{:S(2)}) collective-permute-start(bf16[128,1024]{1,0:T(8,128)(2,1)S(1)} %slice.8), channel_id=1, source_target_pairs={{0,1},{1,2},{2,3},{3,0},{4,5},{5,6},{6,7},{7,4},{8,9},{9,10},{10,1... | collective-permute-start | bytes 786440 | tf_op jit(solution)/shard_map/ppermute | solution.py:538
  23.6 7.8 %collective-permute-start.3 = (bf16[128,1024]{1,0:T(8,128)(2,1)S(1)}, bf16[128,1024]{1,0:T(8,128)(2,1)S(1)}, u32[]{:S(2)}, u32[]{:S(2)}) collective-permute-start(bf16[128,1024]{1,0:T(8,128)(2,1)S(1)} %slice.9), channel_id=1, source_target_pairs={{0,3},{1,0},{2,1},{3,2},{4,7},{5,4},{6,5},{7,6},{8,11},{9,8},{10,9... | collective-permute-start | bytes 786440 | tf_op jit(solution)/shard_map/ppermute | solution.py:538
  30.3 9.7 %copy-start.4 = (s32[1024]{0:T(1024)S(1)}, s32[1024]{0:T(1024)}, u32[]{:S(2)}) copy-start(s32[1024]{0:T(1024)} %param.16) | copy-start | bytes 12292
  30.3 9.7 %copy-start.5 = (f32[1024]{0:T(1024)S(1)}, f32[1024]{0:T(1024)}, u32[]{:S(2)}) copy-start(f32[1024]{0:T(1024)} %param.17) | copy-start | bytes 12292
  33.3 3.7 %collective-permute-start.7 = (f32[4,256]{1,0:T(4,128)S(1)}, f32[4,256]{1,0:T(4,128)S(1)}, u32[]{:S(2)}, u32[]{:S(2)}) collective-permute-start(f32[4,256]{1,0:T(4,128)S(1)} %pad_maximum_fusion.refs_6_), channel_id=1, source_target_pairs={{0,1},{1,2},{2,3},{3,0},{4,5},{5,6},{6,7},{7,4},{8,9},{9,10},{10,1... | collective-permute-start | bytes 12296 | tf_op jit(solution)/shard_map/ppermute | solution.py:538
  33.3 3.7 %collective-permute-start.8 = (f32[4,256]{1,0:T(4,128)S(1)}, f32[4,256]{1,0:T(4,128)S(1)}, u32[]{:S(2)}, u32[]{:S(2)}) collective-permute-start(f32[4,256]{1,0:T(4,128)S(1)} %pad_maximum_fusion.refs_6_), channel_id=1, source_target_pairs={{0,3},{1,0},{2,1},{3,2},{4,7},{5,4},{6,5},{7,6},{8,11},{9,8},{10,9... | collective-permute-start | bytes 12296 | tf_op jit(solution)/shard_map/ppermute | solution.py:538
  36.0 4.0 %collective-permute-start.9 = (f32[4,256]{1,0:T(4,128)S(1)}, f32[4,256]{1,0:T(4,128)S(1)}, u32[]{:S(2)}, u32[]{:S(2)}) collective-permute-start(f32[4,256]{1,0:T(4,128)S(1)} %pad_maximum_fusion.refs_6_), channel_id=1, source_target_pairs={{0,2},{1,3},{2,0},{3,1},{4,6},{5,7},{6,4},{7,5},{8,10},{9,11},{10,... | collective-permute-start | bytes 12296 | tf_op jit(solution)/shard_map/ppermute | solution.py:538
  42.8 10.8 %collective-permute-start.10 = (bf16[1024,1024]{1,0:T(8,128)(2,1)S(1)}, bf16[1024,1024]{1,0:T(8,128)(2,1)S(1)}, u32[]{:S(2)}, u32[]{:S(2)}) collective-permute-start(bf16[1024,1024]{1,0:T(8,128)(2,1)S(1)} %get-tuple-element.51), channel_id=1, source_target_pairs={{0,4},{4,0},{1,5},{5,1},{2,6},{6,2},{3,7},{7,3},{8,12},{12,8},{9,1... | collective-permute-start | bytes 6291464 | tf_op jit(solution)/shard_map/ppermute | solution.py:538
  46.7 6.9 %collective-permute-start.5 = (bf16[1024,512]{1,0:T(8,128)(2,1)S(1)}, bf16[1024,512]{1,0:T(8,128)(2,1)S(1)}, u32[]{:S(2)}, u32[]{:S(2)}) collective-permute-start(bf16[1024,512]{1,0:T(8,128)(2,1)S(1)} %get-tuple-element.39.refs_1_), channel_id=1, source_target_pairs={{0,4},{4,0},{1,5},{5,1},{2,6},{6,2},{3,7},{7,3},{8,12},{12,8},{9,1... | collective-permute-start | bytes 3145736 | tf_op jit(solution)/shard_map/ppermute | solution.py:538
  47.0 5.8 %collective-permute-start.4 = (bf16[1024,256]{1,0:T(8,128)(2,1)S(1)}, bf16[1024,256]{1,0:T(8,128)(2,1)S(1)}, u32[]{:S(2)}, u32[]{:S(2)}) collective-permute-start(bf16[1024,256]{1,0:T(8,128)(2,1)S(1)} %get-tuple-element.38.refs_0_), channel_id=1, source_target_pairs={{0,4},{4,0},{1,5},{5,1},{2,6},{6,2},{3,7},{7,3},{8,12},{12,8},{9,1... | collective-permute-start | bytes 1572872 | tf_op jit(solution)/shard_map/ppermute | solution.py:538
  47.2 6.4 %collective-permute-start.6 = (bf16[1024,256]{1,0:T(8,128)(2,1)S(1)}, bf16[1024,256]{1,0:T(8,128)(2,1)S(1)}, u32[]{:S(2)}, u32[]{:S(2)}) collective-permute-start(bf16[1024,256]{1,0:T(8,128)(2,1)S(1)} %get-tuple-element.40.refs_2_), channel_id=1, source_target_pairs={{0,4},{4,0},{1,5},{5,1},{2,6},{6,2},{3,7},{7,3},{8,12},{12,8},{9,1... | collective-permute-start | bytes 1572872 | tf_op jit(solution)/shard_map/ppermute | solution.py:538
  47.5 6.1 %collective-permute-start.11 = (f32[16,1024]{1,0:T(8,128)S(1)}, f32[16,1024]{1,0:T(8,128)S(1)}, u32[]{:S(2)}, u32[]{:S(2)}) collective-permute-start(f32[16,1024]{1,0:T(8,128)S(1)} %get-tuple-element.53), channel_id=1, source_target_pairs={{0,4},{4,0},{1,5},{5,1},{2,6},{6,2},{3,7},{7,3},{8,12},{12,8},{9,1... | collective-permute-start | bytes 196616 | tf_op jit(solution)/shard_map/ppermute | solution.py:538
  55.9 23.1 %collective-permute-start.12 = (bf16[272,1024]{1,0:T(8,128)(2,1)S(1)}, bf16[272,1024]{1,0:T(8,128)(2,1)S(1)}, u32[]{:S(2)}, u32[]{:S(2)}) collective-permute-start(bf16[272,1024]{1,0:T(8,128)(2,1)S(1)} %get-tuple-element.55), channel_id=1, source_target_pairs={{0,32},{4,12},{8,40},{12,20},{16,48},{20,28},{24,56},{28,4},{32,64... | collective-permute-start | bytes 1671176 | tf_op jit(solution)/shard_map/ppermute | solution.py:533
  57.3 5.5 %copy-start.16 = (f32[32,2048]{1,0:T(8,128)S(1)}, f32[32,2048]{1,0:T(8,128)}, u32[]{:S(2)}) copy-start(f32[32,2048]{1,0:T(8,128)} %rows_ref.1) | copy-start | bytes 786436
  57.3 21.8 %collective-permute-start.13 = (bf16[272,1024]{1,0:T(8,128)(2,1)S(1)}, bf16[272,1024]{1,0:T(8,128)(2,1)S(1)}, u32[]{:S(2)}, u32[]{:S(2)}) collective-permute-start(bf16[272,1024]{1,0:T(8,128)(2,1)S(1)} %get-tuple-element.56), channel_id=1, source_target_pairs={{0,96},{4,28},{8,104},{12,4},{16,112},{20,12},{24,120},{28,20},{32... | collective-permute-start | bytes 1671176 | tf_op jit(solution)/shard_map/ppermute | solution.py:533
  61.2 17.9 %collective-permute-start.14 = (bf16[272,1024]{1,0:T(8,128)(2,1)S(1)}, bf16[272,1024]{1,0:T(8,128)(2,1)S(1)}, u32[]{:S(2)}, u32[]{:S(2)}) collective-permute-start(bf16[272,1024]{1,0:T(8,128)(2,1)S(1)} %get-tuple-element.57), channel_id=1, source_target_pairs={{0,64},{4,20},{8,72},{12,28},{16,80},{20,4},{24,88},{28,12},{32,96... | collective-permute-start | bytes 1671176 | tf_op jit(solution)/shard_map/ppermute | solution.py:533
  62.9 6.0 %collective-permute-start.22 = (bf16[32,2048]{1,0:T(8,128)(2,1)S(1)}, bf16[32,2048]{1,0:T(8,128)(2,1)S(1)}, u32[]{:S(2)}, u32[]{:S(2)}) collective-permute-start(bf16[32,2048]{1,0:T(8,128)(2,1)S(1)} %convert_element_type.3.refs_0_), channel_id=1, source_target_pairs={{0,8},{4,36},{8,16},{12,44},{16,24},{20,52},{24,0},{28,60},{32,40}... | collective-permute-start | bytes 393224 | tf_op jit(solution)/shard_map/ppermute | solution.py:533
  64.1 9.3 %collective-permute-start.23 = (bf16[32,2048]{1,0:T(8,128)(2,1)S(1)}, bf16[32,2048]{1,0:T(8,128)(2,1)S(1)}, u32[]{:S(2)}, u32[]{:S(2)}) collective-permute-start(bf16[32,2048]{1,0:T(8,128)(2,1)S(1)} %convert_element_type.3.refs_0_), channel_id=1, source_target_pairs={{0,16},{4,68},{8,24},{12,76},{16,0},{20,84},{24,8},{28,92},{32,48}... | collective-permute-start | bytes 393224 | tf_op jit(solution)/shard_map/ppermute | solution.py:533
  68.9 6.4 %collective-permute-start.24 = (bf16[32,2048]{1,0:T(8,128)(2,1)S(1)}, bf16[32,2048]{1,0:T(8,128)(2,1)S(1)}, u32[]{:S(2)}, u32[]{:S(2)}) collective-permute-start(bf16[32,2048]{1,0:T(8,128)(2,1)S(1)} %convert_element_type.3.refs_0_), channel_id=1, source_target_pairs={{0,24},{4,100},{8,0},{12,108},{16,8},{20,116},{24,16},{28,124},{32... | collective-permute-start | bytes 393224 | tf_op jit(solution)/shard_map/ppermute | solution.py:533
  75.3 13.6 %collective-permute-start.25 = (bf16[128,2048]{1,0:T(8,128)(2,1)S(1)}, bf16[128,2048]{1,0:T(8,128)(2,1)S(1)}, u32[]{:S(2)}, u32[]{:S(2)}) collective-permute-start(bf16[128,2048]{1,0:T(8,128)(2,1)S(1)} %shard_map.157.refs_0_), channel_id=1, source_target_pairs={{0,32},{4,12},{8,40},{12,20},{16,48},{20,28},{24,56},{28,4},{32,64... | collective-permute-start | bytes 1572872 | tf_op jit(solution)/shard_map/ppermute | solution.py:533
  76.7 18.3 %collective-permute-start.26 = (bf16[128,2048]{1,0:T(8,128)(2,1)S(1)}, bf16[128,2048]{1,0:T(8,128)(2,1)S(1)}, u32[]{:S(2)}, u32[]{:S(2)}) collective-permute-start(bf16[128,2048]{1,0:T(8,128)(2,1)S(1)} %shard_map.157.refs_0_), channel_id=1, source_target_pairs={{0,64},{4,20},{8,72},{12,28},{16,80},{20,4},{24,88},{28,12},{32,96... | collective-permute-start | bytes 1572872 | tf_op jit(solution)/shard_map/ppermute | solution.py:533
  79.4 9.6 %copy-start.17 = (s32[1,128,32]{1,2,0:T(8,128)S(1)}, s32[1,128,32]{1,2,0:T(8,128)}, u32[]{:S(2)}) copy-start(s32[1,128,32]{1,2,0:T(8,128)} %param.13) | copy-start | bytes 49156
  79.4 37.8 %copy-start.10 = (s32[256,16]{0,1:T(8,128)S(1)}, s32[256,16]{0,1:T(8,128)}, u32[]{:S(2)}) copy-start(s32[256,16]{0,1:T(8,128)} %param.15) | copy-start | bytes 49156
  79.4 37.8 %copy-start.13 = (s32[1,128]{1,0:T(1,128)S(1)}, s32[1,128]{1,0:T(1,128)}, u32[]{:S(2)}) copy-start(s32[1,128]{1,0:T(1,128)} %counts_ref.1) | copy-start | bytes 1540
  79.4 36.3 %collective-permute-start.15 = (bf16[272,1024]{1,0:T(8,128)(2,1)S(1)}, bf16[272,1024]{1,0:T(8,128)(2,1)S(1)}, u32[]{:S(2)}, u32[]{:S(2)}) collective-permute-start(bf16[272,1024]{1,0:T(8,128)(2,1)S(1)} %shard_map.153.own_ref), channel_id=1, source_target_pairs={{0,8},{4,36},{8,16},{12,44},{16,24},{20,52},{24,0},{28,60},{32,40}... | collective-permute-start | bytes 1671176 | tf_op jit(solution)/shard_map/ppermute | solution.py:533
  85.2 1.0 copy-start.14
  86.2 9.7 %collective-permute-start.18 = (bf16[256,1024]{1,0:T(8,128)(2,1)}, bf16[256,1024]{1,0:T(8,128)(2,1)}, u32[]{:S(2)}, u32[]{:S(2)}) collective-permute-start(bf16[256,1024]{1,0:T(8,128)(2,1)} %get-tuple-element.59), channel_id=1, source_target_pairs={{0,1},{1,2},{2,3},{3,0},{4,5},{5,6},{6,7},{7,4},{8,9},{9,10},{10,1... | collective-permute-start | bytes 1572872 | tf_op jit(solution)/shard_map/ppermute | solution.py:538
  86.2 21.5 %collective-permute-start.19 = (bf16[256,1024]{1,0:T(8,128)(2,1)}, bf16[256,1024]{1,0:T(8,128)(2,1)}, u32[]{:S(2)}, u32[]{:S(2)}) collective-permute-start(bf16[256,1024]{1,0:T(8,128)(2,1)} %get-tuple-element.60), channel_id=1, source_target_pairs={{0,3},{1,0},{2,1},{3,2},{4,7},{5,4},{6,5},{7,6},{8,11},{9,8},{10,9... | collective-permute-start | bytes 1572872 | tf_op jit(solution)/shard_map/ppermute | solution.py:538
  88.9 23.7 %collective-permute-start.20 = (bf16[256,1024]{1,0:T(8,128)(2,1)}, bf16[256,1024]{1,0:T(8,128)(2,1)}, u32[]{:S(2)}, u32[]{:S(2)}) collective-permute-start(bf16[256,1024]{1,0:T(8,128)(2,1)} %get-tuple-element.61), channel_id=1, source_target_pairs={{0,2},{1,3},{2,0},{3,1},{4,6},{5,7},{6,4},{7,5},{8,10},{9,11},{10,... | collective-permute-start | bytes 1572872 | tf_op jit(solution)/shard_map/ppermute | solution.py:538
  95.1 36.5 %collective-permute-start.27 = (bf16[128,2048]{1,0:T(8,128)(2,1)S(1)}, bf16[128,2048]{1,0:T(8,128)(2,1)S(1)}, u32[]{:S(2)}, u32[]{:S(2)}) collective-permute-start(bf16[128,2048]{1,0:T(8,128)(2,1)S(1)} %shard_map.157.refs_0_), channel_id=1, source_target_pairs={{0,96},{4,28},{8,104},{12,4},{16,112},{20,12},{24,120},{28,20},{32... | collective-permute-start | bytes 1572872 | tf_op jit(solution)/shard_map/ppermute | solution.py:533
  95.9 36.9 %collective-permute-start.28 = (bf16[128,2048]{1,0:T(8,128)(2,1)S(1)}, bf16[128,2048]{1,0:T(8,128)(2,1)S(1)}, u32[]{:S(2)}, u32[]{:S(2)}) collective-permute-start(bf16[128,2048]{1,0:T(8,128)(2,1)S(1)} %shard_map.157.refs_0_), channel_id=1, source_target_pairs={{0,4},{4,0},{1,5},{5,1},{2,6},{6,2},{3,7},{7,3},{8,12},{12,8},{9,1... | collective-permute-start | bytes 1572872 | tf_op jit(solution)/shard_map/ppermute | solution.py:538
  107.7 37.9 %collective-permute-start.29 = (bf16[128,2048]{1,0:T(8,128)(2,1)S(1)}, bf16[128,2048]{1,0:T(8,128)(2,1)}, u32[]{:S(2)}, u32[]{:S(2)}) collective-permute-start(bf16[128,2048]{1,0:T(8,128)(2,1)S(1)} %collective-permute-done.25.refs_1_), channel_id=1, source_target_pairs={{0,4},{4,0},{1,5},{5,1},{2,6},{6,2},{3,7},{7,3},{8,12},{12,8},{9,1... | collective-permute-start | bytes 1572872 | tf_op jit(solution)/shard_map/ppermute | solution.py:538
  112.6 15.6 %collective-permute-start.16 = (bf16[272,1024]{1,0:T(8,128)(2,1)S(1)}, bf16[272,1024]{1,0:T(8,128)(2,1)S(1)}, u32[]{:S(2)}, u32[]{:S(2)}) collective-permute-start(bf16[272,1024]{1,0:T(8,128)(2,1)S(1)} %shard_map.153.own_ref), channel_id=1, source_target_pairs={{0,24},{4,100},{8,0},{12,108},{16,8},{20,116},{24,16},{28,124},{32... | collective-permute-start | bytes 1671176 | tf_op jit(solution)/shard_map/ppermute | solution.py:533
  115.7 12.4 %collective-permute-start.17 = (bf16[272,1024]{1,0:T(8,128)(2,1)S(1)}, bf16[272,1024]{1,0:T(8,128)(2,1)S(1)}, u32[]{:S(2)}, u32[]{:S(2)}) collective-permute-start(bf16[272,1024]{1,0:T(8,128)(2,1)S(1)} %shard_map.153.own_ref), channel_id=1, source_target_pairs={{0,16},{4,68},{8,24},{12,76},{16,0},{20,84},{24,8},{28,92},{32,48}... | collective-permute-start | bytes 1671176 | tf_op jit(solution)/shard_map/ppermute | solution.py:533
  117.2 1.2 copy-start.15
  128.2 18.6 %collective-permute-start.30 = (bf16[128,2048]{1,0:T(8,128)(2,1)S(1)}, bf16[128,2048]{1,0:T(8,128)(2,1)}, u32[]{:S(2)}, u32[]{:S(2)}) collective-permute-start(bf16[128,2048]{1,0:T(8,128)(2,1)S(1)} %collective-permute-done.26.refs_2_), channel_id=1, source_target_pairs={{0,4},{4,0},{1,5},{5,1},{2,6},{6,2},{3,7},{7,3},{8,12},{12,8},{9,1... | collective-permute-start | bytes 1572872 | tf_op jit(solution)/shard_map/ppermute | solution.py:538
  129.9 0.7 copy-start.8
  130.5 16.4 %collective-permute-start.32 = (bf16[256,1024]{1,0:T(8,128)(2,1)}, bf16[256,1024]{1,0:T(8,128)(2,1)S(1)}, u32[]{:S(2)}, u32[]{:S(2)}) collective-permute-start(bf16[256,1024]{1,0:T(8,128)(2,1)} %get-tuple-element.67.refs_0_), channel_id=1, source_target_pairs={{0,32},{4,12},{8,40},{12,20},{16,48},{20,28},{24,56},{28,4},{32,64... | collective-permute-start | bytes 1572872 | tf_op jit(solution)/shard_map/ppermute | solution.py:533
  131.6 15.7 %collective-permute-start.33 = (bf16[256,1024]{1,0:T(8,128)(2,1)}, bf16[256,1024]{1,0:T(8,128)(2,1)}, u32[]{:S(2)}, u32[]{:S(2)}) collective-permute-start(bf16[256,1024]{1,0:T(8,128)(2,1)} %get-tuple-element.67.refs_0_), channel_id=1, source_target_pairs={{0,64},{4,20},{8,72},{12,28},{16,80},{20,4},{24,88},{28,12},{32,96... | collective-permute-start | bytes 1572872 | tf_op jit(solution)/shard_map/ppermute | solution.py:533
  132.8 0.8 copy-start.2
  133.6 15.4 %collective-permute-start.34 = (bf16[256,1024]{1,0:T(8,128)(2,1)}, bf16[256,1024]{1,0:T(8,128)(2,1)}, u32[]{:S(2)}, u32[]{:S(2)}) collective-permute-start(bf16[256,1024]{1,0:T(8,128)(2,1)} %get-tuple-element.67.refs_0_), channel_id=1, source_target_pairs={{0,96},{4,28},{8,104},{12,4},{16,112},{20,12},{24,120},{28,20},{32... | collective-permute-start | bytes 1572872 | tf_op jit(solution)/shard_map/ppermute | solution.py:533
  134.8 27.2 %all-to-all-start = ((bf16[128,24,128]{2,1,0:T(8,128)(2,1)}), bf16[128,24,128]{2,1,0:T(8,128)(2,1)}, u32[]{:S(2)}, u32[]{:S(2)}) async-start(bf16[128,24,128]{2,1,0:T(8,128)(2,1)} %get-tuple-element.64), calls=%async_computation | async-start | bytes 1572864 | tf_op jit(solution)/shard_map/all_to_all | solution.py:637
  145.6 4.8 %collective-permute-start.31 = (bf16[128,2048]{1,0:T(8,128)(2,1)S(1)}, bf16[128,2048]{1,0:T(8,128)(2,1)S(1)}, u32[]{:S(2)}, u32[]{:S(2)}) collective-permute-start(bf16[128,2048]{1,0:T(8,128)(2,1)S(1)} %collective-permute-done.27.refs_3_), channel_id=1, source_target_pairs={{0,4},{4,0},{1,5},{5,1},{2,6},{6,2},{3,7},{7,3},{8,12},{12,8},{9,1... | collective-permute-start | bytes 1572872 | tf_op jit(solution)/shard_map/ppermute | solution.py:538
  146.8 8.1 %collective-permute-start.35 = (bf16[256,1024]{1,0:T(8,128)(2,1)}, bf16[256,1024]{1,0:T(8,128)(2,1)S(1)}, u32[]{:S(2)}, u32[]{:S(2)}) collective-permute-start(bf16[256,1024]{1,0:T(8,128)(2,1)} %get-tuple-element.67.refs_0_), channel_id=1, source_target_pairs={{0,4},{4,0},{1,5},{5,1},{2,6},{6,2},{3,7},{7,3},{8,12},{12,8},{9,1... | collective-permute-start | bytes 1572872 | tf_op jit(solution)/shard_map/ppermute | solution.py:538
  146.9 8.0 %collective-permute-start.36 = (bf16[256,1024]{1,0:T(8,128)(2,1)S(1)}, bf16[256,1024]{1,0:T(8,128)(2,1)S(1)}, u32[]{:S(2)}, u32[]{:S(2)}) collective-permute-start(bf16[256,1024]{1,0:T(8,128)(2,1)S(1)} %collective-permute-done.32.refs_1_), channel_id=1, source_target_pairs={{0,4},{4,0},{1,5},{5,1},{2,6},{6,2},{3,7},{7,3},{8,12},{12,8},{9,1... | collective-permute-start | bytes 1572872 | tf_op jit(solution)/shard_map/ppermute | solution.py:538
  147.3 7.6 %collective-permute-start.37 = (bf16[256,1024]{1,0:T(8,128)(2,1)}, bf16[256,1024]{1,0:T(8,128)(2,1)S(1)}, u32[]{:S(2)}, u32[]{:S(2)}) collective-permute-start(bf16[256,1024]{1,0:T(8,128)(2,1)} %collective-permute-done.33.refs_2_), channel_id=1, source_target_pairs={{0,4},{4,0},{1,5},{5,1},{2,6},{6,2},{3,7},{7,3},{8,12},{12,8},{9,1... | collective-permute-start | bytes 1572872 | tf_op jit(solution)/shard_map/ppermute | solution.py:538
  149.0 5.9 %collective-permute-start.38 = (bf16[256,1024]{1,0:T(8,128)(2,1)}, bf16[256,1024]{1,0:T(8,128)(2,1)S(1)}, u32[]{:S(2)}, u32[]{:S(2)}) collective-permute-start(bf16[256,1024]{1,0:T(8,128)(2,1)} %collective-permute-done.34.refs_3_), channel_id=1, source_target_pairs={{0,4},{4,0},{1,5},{5,1},{2,6},{6,2},{3,7},{7,3},{8,12},{12,8},{9,1... | collective-permute-start | bytes 1572872 | tf_op jit(solution)/shard_map/ppermute | solution.py:538
  150.4 8.2 %collective-permute-start.21 = (f32[32,1024]{1,0:T(8,128)S(1)}, f32[32,1024]{1,0:T(8,128)S(1)}, u32[]{:S(2)}, u32[]{:S(2)}) collective-permute-start(f32[32,1024]{1,0:T(8,128)S(1)} %get-tuple-element.66), channel_id=1, source_target_pairs={{0,4},{4,0},{1,5},{5,1},{2,6},{6,2},{3,7},{7,3},{8,12},{12,8},{9,1... | collective-permute-start | bytes 393224 | tf_op jit(solution)/shard_map/ppermute | solution.py:538
  150.4 1.0 copy-start.3
  152.9 2.0 %copy-start = (bf16[1024,2048]{1,0:T(8,128)(2,1)}, bf16[1024,2048]{1,0:T(8,128)(2,1)S(1)}, u32[]{:S(2)}) copy-start(bf16[1024,2048]{1,0:T(8,128)(2,1)S(1)} %shard_map.158.held_hbm) | copy-start | bytes 12582916
  156.6 2.0 %copy-start.1 = (bf16[1024,2048]{1,0:T(8,128)(2,1)}, bf16[1024,2048]{1,0:T(8,128)(2,1)S(1)}, u32[]{:S(2)}) copy-start(bf16[1024,2048]{1,0:T(8,128)(2,1)S(1)} %shard_map.159.grad_hbm) | copy-start | bytes 12582916
  158.6 3.4 %copy-start.19 = (f32[32,1024]{1,0:T(8,128)}, f32[32,1024]{1,0:T(8,128)S(1)}, u32[]{:S(2)}) copy-start(f32[32,1024]{1,0:T(8,128)S(1)} %collective-permute-done.21.theirs_ref) | copy-start | bytes 393220

commit v3 on v2

--- a/solution.py
+++ b/solution.py
@@ -40,7 +40,7 @@
     return ends - jnp.sum(jnp.where(of == at, spread, 0.0), axis=1, keepdims=True), ends
 
 
-def gather_kernel(counts_hbm, lookups_hbm, slab_hbm, out_ref, counts_ref, lookups_ref, slab_ref, sems):
+def gather_kernel(counts_hbm, lookups_hbm, slab_hbm, low_ref, high_ref, counts_ref, lookups_ref, slab_ref, sems):
     copies = [
         pltpu.make_async_copy(a, b, sems.at[k])
         for k, (a, b) in enumerate(
@@ -81,7 +81,10 @@
                 found = jnp.where(block == float(k), rows[:, 128 * k : 128 * (k + 1)], found)
             swap = place - 2.0 * block != float(parity)
             both.append(jnp.where(swap, pltpu.roll(found, 64, 1), found))
-        out_ref[:, pl.ds(pl.multiple_of(p * 128, 128), 128)] = jnp.where(low_lane, both[0], both[1]).astype(BF16)
+        pooled = jnp.where(low_lane, both[0], both[1]).astype(BF16)
+        cols = pl.ds(pl.multiple_of(p * 128, 128), 128)
+        low_ref[:, cols] = pooled[: batch // 2]
+        high_ref[:, cols] = pooled[batch // 2 :]
         return carry
 
     lax.fori_loop(0, features // 2, pair, 0, unroll=4)
@@ -91,9 +94,9 @@
     features, batch = lookups_t.shape
     return pl.pallas_call(
         gather_kernel,
-        out_shape=jax.ShapeDtypeStruct((batch, features * 64), BF16),
+        out_shape=(jax.ShapeDtypeStruct((batch // 2, features * 64), BF16),) * 2,
         in_specs=[HBM, HBM, HBM],
-        out_specs=VM,
+        out_specs=(VM, VM),
         scratch_shapes=[
             pltpu.VMEM(counts.shape, counts.dtype),
             pltpu.VMEM(lookups_t.shape, lookups_t.dtype),
@@ -248,8 +251,9 @@
         at = pl.ds(pl.multiple_of(k * size, size), size)
         grad = scale * grad_ref[at, :].astype(F32)
         accum = held_ref[at, :].astype(F32) + grad * grad
-        step = dense * grad / (accum * lax.rsqrt(accum) + eps)
-        w_ref[at, :] = (w_ref[at, :].astype(F32) - step).astype(BF16)
+        seed = lax.rsqrt(accum)
+        inverse = seed * (2.0 - (accum * seed + eps) * seed)
+        w_ref[at, :] = (w_ref[at, :].astype(F32) - (dense * grad) * inverse).astype(BF16)
         pltpu.make_async_copy(w_ref.at[at, :], w_out_hbm.at[at, :], out_sems.at[k]).start()
         return carry
 
@@ -560,8 +564,9 @@
     depth, width = weight_in.shape
     half = width // 2
     lookups_t = lookup_slots.T
-    pooled = gather_rows(peer_counts, lookups_t, slab_values[0])
-    before, after = send(pooled, "mp", 1), send(pooled, "mp", 3)
+    low, high = gather_rows(peer_counts, lookups_t, slab_values[0])
+    before_low, after_high = send(low, "mp", 1), send(high, "mp", 3)
+    before_high, after_low = send(high, "mp", 1), send(low, "mp", 3)
     narrow = dense_accum.astype(BF16)
     parts = {s: cross(narrow, False, s) for s in SHIFTS}
     block = (depth // 8, width)
@@ -572,9 +577,11 @@
     accum_full = call(merge_kernel, [((depth, width), BF16)], 10**8, stacks)[0]
     bias = bias_in.reshape(1, width)
     out_w = weight_out.reshape(1, width)
-    far_low, far_high = send(before[: batch // 2], "mp", 1), send(after[batch // 2 :], "mp", 3)
-    slope_0, hidden_0, logit_0, turned_0 = forward([pooled], weight_in, bias, out_w)
-    slope_1, hidden_1, logit_1, turned_1 = forward([before, after], weight_in, bias, out_w)
+    far_low, far_high = send(before_low, "mp", 1), send(after_high, "mp", 3)
+    slope_0, hidden_0, logit_0, turned_0 = forward([low, high], weight_in, bias, out_w)
+    slope_1, hidden_1, logit_1, turned_1 = forward(
+        [before_low, before_high, after_low, after_high], weight_in, bias, out_w
+    )
     slope_2, hidden_2, logit_2, turned_2 = forward([far_low, far_high], weight_in, bias, out_w)
     turned = [turned_0, turned_1, turned_2]
     turned = turned + [send(t, "dp_2", 1) for t in turned]
@@ -608,10 +615,10 @@
     from_after, from_before, from_far = send(to_before, "mp", 3), send(to_after, "mp", 1), send(to_far, "mp", 2)
     held = (*turned, dact, far_dact, sums_mine, far_sums)
     block = (depth // 4 + 16, half)
-    to_next, to_prev = call(functools.partial(grad_kernel, SHIFTS[:2]), [(block, BF16)] * 2, 4 * 10**9, held)
-    from_prev, from_next = cross(to_next, True, 1), cross(to_prev, True, 3)
-    to_far, keep = call(functools.partial(grad_kernel, (2, 0)), [(block, BF16), (block, F32)], 4 * 10**9, held)
-    distant = cross(to_far, True, 2)
+    to_far, to_next = call(functools.partial(grad_kernel, (2, 1)), [(block, BF16)] * 2, 4 * 10**9, held)
+    distant, from_prev = cross(to_far, True, 2), cross(to_next, True, 1)
+    to_prev, keep = call(functools.partial(grad_kernel, (3, 0)), [(block, BF16), (block, F32)], 4 * 10**9, held)
+    from_next = cross(to_prev, True, 3)
     keep = call(middle_kernel, [(block, BF16)], 10**8, (keep, from_prev, from_next, distant))[0]
     got = [cross(keep, False, s) for s in SHIFTS]
     peers, capacity = row_ids.shape[1:]

time: 175 us -> 174 us (level); the launches traced: 173 us -> 170 us
  waiting for transfers between devices: 38 us -> 32 us
  starting transfers between devices: 73.3 us -> 76 us
    ppermute x24 -> x26, starting transfers between devices: 40.3 us -> 46.5 us  [send(): return lax.ppermute(x, axis, [(i, (i + shift) % n) for i in range(n)])]
    ppermute x24 -> x26, waiting for transfers between devices: 20.5 us -> 16.4 us  [send(): return lax.ppermute(x, axis, [(i, (i + shift) % n) for i in range(n)])]
    all_to_all x1, starting transfers between devices: 10.8 us -> 7.3 us  [inner(): arrived = lax.all_to_all(outgoing, DP_MP, 0, 0, tiled=True)]
  transfers between devices with their start and end apart: 40 -> 42, of which waited for: 12 -> 14; matrix products, arithmetic and copies ran while one was open for 0% -> 0% of each run, Pallas kernels for 16% -> 16%
where the time goes in v3:
time: 174 us; the launch traced here: 170 us
  starting transfers between devices  76 us (44%)
  Pallas kernels  50.1 us (29%)
  waiting for transfers between devices  32 us (18%)
  local copies, waits for them, and re-layouts  11.2 us (6%)
    ppermute x26, starting transfers between devices, send(): return lax.ppermute(x, axis, [(i, (i + shift) % n) for i in range(n)])  46.5 us
    pallas_call x14, Pallas kernels, call(): pl.pallas_call(kernel, out_shape=shapes, in_specs=[HBM if k in far else V...  46 us
    ppermute x15, starting transfers between devices, cross(): return lax.ppermute(x, DP, moves)  22.2 us
    ppermute x26, waiting for transfers between devices, send(): return lax.ppermute(x, axis, [(i, (i + shift) % n) for i in range(n)])  16.4 us
    ppermute x15, waiting for transfers between devices, cross(): return lax.ppermute(x, DP, moves)  13.1 us
    unnamed x41, local copies, waits for them, and re-layouts  11.2 us
    all_to_all x1, starting transfers between devices, inner(): arrived = lax.all_to_all(outgoing, DP_MP, 0, 0, tiled=True)  7.3 us
    pallas_call x1, Pallas kernels, gather_rows(): pl.pallas_call(gather_kernel, out_shape=(jax.ShapeDtypeStruct((batch // 2...  4.15 us
  transfers between devices with their start and end apart: 42, of which 14 were waited for; matrix products, arithmetic and copies ran while one was open for 0% of the time, Pallas kernels for 16%

profile of v3, /device:TPU:1, one launch (start us, length us, event | category | flops | bytes accessed | tf_op | source)
XLA Modules:
  0.0 170.5 jit_solution(2883437796602435479)
XLA Ops:
  0.6 1.0 copy-done.7
  1.7 0.7 copy-done.9
  2.4 0.7 copy-done.12
  3.1 4.2 %gather_rows.1 = (bf16[128,1024]{1,0:T(8,128)(2,1)S(1)}, bf16[128,1024]{1,0:T(8,128)(2,1)S(1)}) custom-call(s32[1,128]{1,0:T(1,128)S(1)} %copy-done.12, s32[16,256]{1,0:T(8,128)S(1)} %bitcast.14, bf16[128,2048]{1,0:T(8,128)(2,1)S(1)} %bitcast.13), custom_call_target="tpu_custom_call" | custom-call | flops 6000000000 | bytes 2000000 | tf_op jit(solution)/shard_map/gather_rows/pallas_call | solution.py:95
  7.2 2.5 %collective-permute-start = (bf16[128,1024]{1,0:T(8,128)(2,1)S(1)}, bf16[128,1024]{1,0:T(8,128)(2,1)S(1)}, u32[]{:S(2)}, u32[]{:S(2)}) collective-permute-start(bf16[128,1024]{1,0:T(8,128)(2,1)S(1)} %get-tuple-element.40.refs_0_), channel_id=1, source_target_pairs={{0,1},{1,2},{2,3},{3,0},{4,5},{5,6},{6,7},{7,4},{8,9},{9,10},{10,1... | collective-permute-start | bytes 786440 | tf_op jit(solution)/shard_map/ppermute | solution.py:542
  9.7 2.2 %collective-permute-start.3 = (bf16[128,1024]{1,0:T(8,128)(2,1)S(1)}, bf16[128,1024]{1,0:T(8,128)(2,1)S(1)}, u32[]{:S(2)}, u32[]{:S(2)}) collective-permute-start(bf16[128,1024]{1,0:T(8,128)(2,1)S(1)} %get-tuple-element.41.refs_1_), channel_id=1, source_target_pairs={{0,3},{1,0},{2,1},{3,2},{4,7},{5,4},{6,5},{7,6},{8,11},{9,8},{10,9... | collective-permute-start | bytes 786440 | tf_op jit(solution)/shard_map/ppermute | solution.py:542
  11.9 2.7 %collective-permute-start.2 = (bf16[128,1024]{1,0:T(8,128)(2,1)S(1)}, bf16[128,1024]{1,0:T(8,128)(2,1)S(1)}, u32[]{:S(2)}, u32[]{:S(2)}) collective-permute-start(bf16[128,1024]{1,0:T(8,128)(2,1)S(1)} %get-tuple-element.40.refs_0_), channel_id=1, source_target_pairs={{0,3},{1,0},{2,1},{3,2},{4,7},{5,4},{6,5},{7,6},{8,11},{9,8},{10,9... | collective-permute-start | bytes 786440 | tf_op jit(solution)/shard_map/ppermute | solution.py:542
  14.6 1.9 %shard_map.147 = (f32[256,2048]{1,0:T(8,128)S(1)}, bf16[256,2048]{1,0:T(8,128)(2,1)S(1)}, f32[1,256]{1,0:T(1,128)S(1)}, bf16[1024,256]{1,0:T(8,128)(2,1)S(1)}) custom-call(bf16[128,1024]{1,0:T(8,128)(2,1)S(1)} %get-tuple-element.40.refs_0_, bf16[128,1024]{1,0:T(8,128)(2,1)S(1)} %get-tuple-element.41.refs_1_, bf16[1024,2048]{1,0:T(8,128)(2,1)S(1)} %copy-done.6, ...), custom_call_target="tpu_custom_call" | custom-call | flops 2560000000 | bytes 2000000 | tf_op jit(solution)/shard_map/pallas_call | solution.py:282
  16.5 1.3 collective-permute-done.refs_0_
  17.8 2.7 %collective-permute-start.5 = (bf16[128,1024]{1,0:T(8,128)(2,1)S(1)}, bf16[128,1024]{1,0:T(8,128)(2,1)S(1)}, u32[]{:S(2)}, u32[]{:S(2)}) collective-permute-start(bf16[128,1024]{1,0:T(8,128)(2,1)S(1)} %collective-permute-done.3.refs_3_), channel_id=1, source_target_pairs={{0,3},{1,0},{2,1},{3,2},{4,7},{5,4},{6,5},{7,6},{8,11},{9,8},{10,9... | collective-permute-start | bytes 786440 | tf_op jit(solution)/shard_map/ppermute | solution.py:542
  20.5 2.9 %collective-permute-done.1.refs_1_ = bf16[128,1024]{1,0:T(8,128)(2,1)S(1)} collective-permute-done((bf16[128,1024]{1,0:T(8,128)(2,1)S(1)}, bf16[128,1024]{1,0:T(8,128)(2,1)S(1)}, u32[]{:S(2)}, u32[]{:S(2)}) %collective-permute-start.1) | collective-permute-done | bytes 262176 | tf_op jit(solution)/shard_map/ppermute | solution.py:542
  23.5 3.9 %shard_map.148 = (f32[512,2048]{1,0:T(8,128)S(1)}, bf16[512,2048]{1,0:T(8,128)(2,1)S(1)}, f32[2,256]{1,0:T(2,128)S(1)}, bf16[1024,512]{1,0:T(8,128)(2,1)S(1)}) custom-call(bf16[128,1024]{1,0:T(8,128)(2,1)S(1)} %collective-permute-done.refs_0_, bf16[128,1024]{1,0:T(8,128)(2,1)S(1)} %collective-permute-done.1.refs_1_, ...), custom_call_target="tpu_custom_call" | custom-call | flops 5120000000 | bytes 2000000 | tf_op jit(solution)/shard_map/pallas_call | solution.py:282
  27.4 1.7 collective-permute-done.4.refs_0_
  29.1 1.8 %shard_map.149 = (f32[256,2048]{1,0:T(8,128)S(1)}, bf16[256,2048]{1,0:T(8,128)(2,1)S(1)}, f32[1,256]{1,0:T(1,128)S(1)}, bf16[1024,256]{1,0:T(8,128)(2,1)S(1)}) custom-call(bf16[128,1024]{1,0:T(8,128)(2,1)S(1)} %collective-permute-done.4.refs_0_, bf16[128,1024]{1,0:T(8,128)(2,1)S(1)} %collective-permute-done.5.refs_1_, bf16[1024,2048]{1,0:T(8,128)(2,1)S(1)} %copy-done.6, ...), custom_call_target="tpu_custom_call" | custom-call | flops 2560000000 | bytes 2000000 | tf_op jit(solution)/shard_map/pallas_call | solution.py:282
  30.9 2.5 %collective-permute-start.10 = (f32[4,256]{1,0:T(4,128)S(1)}, f32[4,256]{1,0:T(4,128)S(1)}, u32[]{:S(2)}, u32[]{:S(2)}) collective-permute-start(f32[4,256]{1,0:T(4,128)S(1)} %pad_maximum_fusion.refs_6_), channel_id=1, source_target_pairs={{0,3},{1,0},{2,1},{3,2},{4,7},{5,4},{6,5},{7,6},{8,11},{9,8},{10,9... | collective-permute-start | bytes 12296 | tf_op jit(solution)/shard_map/ppermute | solution.py:542
  33.5 0.7 collective-permute-start.9
  34.2 3.2 %collective-permute-done.11.refs_9_ = f32[4,256]{1,0:T(4,128)S(1)} collective-permute-done((f32[4,256]{1,0:T(4,128)S(1)}, f32[4,256]{1,0:T(4,128)S(1)}, u32[]{:S(2)}, u32[]{:S(2)}) %collective-permute-start.11) | collective-permute-done | bytes 4128 | tf_op jit(solution)/shard_map/ppermute | solution.py:542
  37.4 2.8 %shard_map.150 = (bf16[1024,2048]{1,0:T(8,128)(2,1)S(1)}, bf16[1024,1024]{1,0:T(8,128)(2,1)S(1)}, f32[16,1024]{1,0:T(8,128)S(1)}, f32[16,1024]{1,0:T(8,128)S(1)}) custom-call(f32[256,2048]{1,0:T(8,128)S(1)} %get-tuple-element.45.refs_0_, f32[512,2048]{1,0:T(8,128)S(1)} %get-tuple-element.46.refs_1_, f32[256,2048]{1,0:T(8,128)S(1)} %get-tuple-element.47.refs_2_, ...), custom_call_target="tpu_custom_call" | custom-call | flops 2000000000 | bytes 2000000 | tf_op jit(solution)/shard_map/pallas_call | solution.py:282
  40.3 3.1 %collective-permute-start.12 = (bf16[1024,1024]{1,0:T(8,128)(2,1)S(1)}, bf16[1024,1024]{1,0:T(8,128)(2,1)S(1)}, u32[]{:S(2)}, u32[]{:S(2)}) collective-permute-start(bf16[1024,1024]{1,0:T(8,128)(2,1)S(1)} %get-tuple-element.55), channel_id=1, source_target_pairs={{0,4},{4,0},{1,5},{5,1},{2,6},{6,2},{3,7},{7,3},{8,12},{12,8},{9,1... | collective-permute-start | bytes 6291464 | tf_op jit(solution)/shard_map/ppermute | solution.py:542
  44.0 0.4 collective-permute-start.13
  44.4 5.0 %collective-permute-done.6.refs_3_ = bf16[1024,256]{1,0:T(8,128)(2,1)S(1)} collective-permute-done((bf16[1024,256]{1,0:T(8,128)(2,1)S(1)}, bf16[1024,256]{1,0:T(8,128)(2,1)S(1)}, u32[]{:S(2)}, u32[]{:S(2)}) %collective-permute-start.6) | collective-permute-done | bytes 524320 | tf_op jit(solution)/shard_map/ppermute | solution.py:542
  49.4 0.8 collective-permute-done.13.refs_9_
  50.3 2.4 %shard_map.152 = (bf16[272,1024]{1,0:T(8,128)(2,1)S(1)}, bf16[272,1024]{1,0:T(8,128)(2,1)S(1)}) custom-call(bf16[1024,256]{1,0:T(8,128)(2,1)S(1)} %get-tuple-element.42.refs_0_, bf16[1024,512]{1,0:T(8,128)(2,1)S(1)} %get-tuple-element.43.refs_1_, bf16[1024,256]{1,0:T(8,128)(2,1)S(1)} %get-tuple-element.44.refs_2_, ...), custom_call_target="tpu_custom_call" | custom-call | flops 4000000000 | bytes 2000000 | tf_op jit(solution)/shard_map/pallas_call | solution.py:282
  52.6 1.4 collective-permute-start.14
  54.0 2.6 %collective-permute-start.16 = (bf16[272,1024]{1,0:T(8,128)(2,1)S(1)}, bf16[272,1024]{1,0:T(8,128)(2,1)S(1)}, u32[]{:S(2)}, u32[]{:S(2)}) collective-permute-start(bf16[272,1024]{1,0:T(8,128)(2,1)S(1)} %get-tuple-element.61), channel_id=1, source_target_pairs={{0,64},{4,20},{8,72},{12,28},{16,80},{20,4},{24,88},{28,12},{32,96... | collective-permute-start | bytes 1671176 | tf_op jit(solution)/shard_map/ppermute | solution.py:537
  56.6 2.4 %shard_map.151 = (bf16[272,1024]{1,0:T(8,128)(2,1)S(1)}, f32[272,1024]{1,0:T(8,128)S(1)}) custom-call(bf16[1024,256]{1,0:T(8,128)(2,1)S(1)} %get-tuple-element.42.refs_0_, bf16[1024,512]{1,0:T(8,128)(2,1)S(1)} %get-tuple-element.43.refs_1_, bf16[1024,256]{1,0:T(8,128)(2,1)S(1)} %get-tuple-element.44.refs_2_, ...), custom_call_target="tpu_custom_call" | custom-call | flops 4000000000 | bytes 2000000 | tf_op jit(solution)/shard_map/pallas_call | solution.py:282
  59.0 1.1 collective-permute-start.15
  60.1 1.3 collective-permute-start.24
  61.4 2.5 %collective-permute-start.25 = (bf16[32,2048]{1,0:T(8,128)(2,1)S(1)}, bf16[32,2048]{1,0:T(8,128)(2,1)S(1)}, u32[]{:S(2)}, u32[]{:S(2)}) collective-permute-start(bf16[32,2048]{1,0:T(8,128)(2,1)S(1)} %convert_element_type.3.refs_0_), channel_id=1, source_target_pairs={{0,16},{4,68},{8,24},{12,76},{16,0},{20,84},{24,8},{28,92},{32,48}... | collective-permute-start | bytes 393224 | tf_op jit(solution)/shard_map/ppermute | solution.py:537
  63.9 3.5 %collective-permute-done.24.refs_1_ = bf16[32,2048]{1,0:T(8,128)(2,1)S(1)} collective-permute-done((bf16[32,2048]{1,0:T(8,128)(2,1)S(1)}, bf16[32,2048]{1,0:T(8,128)(2,1)S(1)}, u32[]{:S(2)}, u32[]{:S(2)}) %collective-permute-start.24) | collective-permute-done | bytes 131104 | tf_op jit(solution)/shard_map/ppermute | solution.py:537
  67.4 0.8 collective-permute-start.26
  68.2 2.5 %collective-permute-done.25.refs_2_ = bf16[32,2048]{1,0:T(8,128)(2,1)S(1)} collective-permute-done((bf16[32,2048]{1,0:T(8,128)(2,1)S(1)}, bf16[32,2048]{1,0:T(8,128)(2,1)S(1)}, u32[]{:S(2)}, u32[]{:S(2)}) %collective-permute-start.25) | collective-permute-done | bytes 131104 | tf_op jit(solution)/shard_map/ppermute | solution.py:537
  70.7 2.1 %collective-permute-done.26.refs_3_ = bf16[32,2048]{1,0:T(8,128)(2,1)S(1)} collective-permute-done((bf16[32,2048]{1,0:T(8,128)(2,1)S(1)}, bf16[32,2048]{1,0:T(8,128)(2,1)S(1)}, u32[]{:S(2)}, u32[]{:S(2)}) %collective-permute-start.26) | collective-permute-done | bytes 131104 | tf_op jit(solution)/shard_map/ppermute | solution.py:537
  73.0 0.8 collective-permute-start.28
  74.1 2.3 %collective-permute-start.17 = (bf16[272,1024]{1,0:T(8,128)(2,1)S(1)}, bf16[272,1024]{1,0:T(8,128)(2,1)S(1)}, u32[]{:S(2)}, u32[]{:S(2)}) collective-permute-start(bf16[272,1024]{1,0:T(8,128)(2,1)S(1)} %shard_map.153.own_ref), channel_id=1, source_target_pairs={{0,8},{4,36},{8,16},{12,44},{16,24},{20,52},{24,0},{28,60},{32,40}... | collective-permute-start | bytes 1671176 | tf_op jit(solution)/shard_map/ppermute | solution.py:537
  76.4 5.7 %shard_map.154 = (f32[256,1024]{1,0:T(8,128)S(1)}, bf16[256,1024]{1,0:T(8,128)(2,1)}, bf16[256,1024]{1,0:T(8,128)(2,1)}, bf16[256,1024]{1,0:T(8,128)(2,1)}) custom-call(bf16[1024,2048]{1,0:T(8,128)(2,1)S(1)} %get-tuple-element.54.refs_6_.dact_ref, bf16[1024,2048]{1,0:T(8,128)(2,1)S(1)} %copy-done.6), custom_call_target="tpu_custom_call" | custom-call | flops 4000000000 | bytes 2000000 | tf_op jit(solution)/shard_map/pallas_call | solution.py:282
  82.1 1.0 copy-done.14
  83.1 2.7 %collective-permute-start.21 = (bf16[256,1024]{1,0:T(8,128)(2,1)}, bf16[256,1024]{1,0:T(8,128)(2,1)}, u32[]{:S(2)}, u32[]{:S(2)}) collective-permute-start(bf16[256,1024]{1,0:T(8,128)(2,1)} %get-tuple-element.64), channel_id=1, source_target_pairs={{0,3},{1,0},{2,1},{3,2},{4,7},{5,4},{6,5},{7,6},{8,11},{9,8},{10,9... | collective-permute-start | bytes 1572872 | tf_op jit(solution)/shard_map/ppermute | solution.py:542
  85.7 4.2 %collective-permute-done.27.refs_1_ = bf16[128,2048]{1,0:T(8,128)(2,1)S(1)} collective-permute-done((bf16[128,2048]{1,0:T(8,128)(2,1)S(1)}, bf16[128,2048]{1,0:T(8,128)(2,1)S(1)}, u32[]{:S(2)}, u32[]{:S(2)}) %collective-permute-start.27) | collective-permute-done | bytes 524320 | tf_op jit(solution)/shard_map/ppermute | solution.py:537
  89.9 1.7 %collective-permute-start.22 = (bf16[256,1024]{1,0:T(8,128)(2,1)}, bf16[256,1024]{1,0:T(8,128)(2,1)}, u32[]{:S(2)}, u32[]{:S(2)}) collective-permute-start(bf16[256,1024]{1,0:T(8,128)(2,1)} %get-tuple-element.65), channel_id=1, source_target_pairs={{0,2},{1,3},{2,0},{3,1},{4,6},{5,7},{6,4},{7,5},{8,10},{9,11},{10,... | collective-permute-start | bytes 1572872 | tf_op jit(solution)/shard_map/ppermute | solution.py:542
  91.8 1.2 collective-permute-done.20.a_ref
  93.1 17.1 %collective-permute-start.30 = (bf16[128,2048]{1,0:T(8,128)(2,1)S(1)}, bf16[128,2048]{1,0:T(8,128)(2,1)S(1)}, u32[]{:S(2)}, u32[]{:S(2)}) collective-permute-start(bf16[128,2048]{1,0:T(8,128)(2,1)S(1)} %shard_map.157.refs_0_), channel_id=1, source_target_pairs={{0,4},{4,0},{1,5},{5,1},{2,6},{6,2},{3,7},{7,3},{8,12},{12,8},{9,1... | collective-permute-start | bytes 1572872 | tf_op jit(solution)/shard_map/ppermute | solution.py:542
  110.2 1.1 collective-permute-start.18
  111.2 2.3 %collective-permute-start.19 = (bf16[272,1024]{1,0:T(8,128)(2,1)S(1)}, bf16[272,1024]{1,0:T(8,128)(2,1)S(1)}, u32[]{:S(2)}, u32[]{:S(2)}) collective-permute-start(bf16[272,1024]{1,0:T(8,128)(2,1)S(1)} %shard_map.153.own_ref), channel_id=1, source_target_pairs={{0,16},{4,68},{8,24},{12,76},{16,0},{20,84},{24,8},{28,92},{32,48}... | collective-permute-start | bytes 1671176 | tf_op jit(solution)/shard_map/ppermute | solution.py:537
  113.5 1.2 copy-done.15
  114.7 8.3 %shard_map.155 = (bf16[128,16,128]{2,1,0:T(8,128)(2,1)S(1)}, f32[8,128]{1,0:T(8,128)S(1)}) custom-call(s32[1,128]{1,0:T(1,128)S(1)} %copy-done.13, s32[16,256]{1,0:T(8,128)S(1)} %bitcast.15, f32[256,1024]{1,0:T(8,128)S(1)} %copy-done.15, bf16[256,1024]{1,0:T(8,128)(2,1)} %collective-permute-done.20.a_ref, bf16[256,1024]{1,0:T(8,128)(2,1)} %collective-permute-done.21.b_ref, ...), custom_call_target="tpu_custom_call" | custom-call | flops 8000000000 | bytes 2000000 | tf_op jit(solution)/shard_map/pallas_call | solution.py:282
  123.0 2.7 %collective-permute-start.32 = (bf16[128,2048]{1,0:T(8,128)(2,1)S(1)}, bf16[128,2048]{1,0:T(8,128)(2,1)}, u32[]{:S(2)}, u32[]{:S(2)}) collective-permute-start(bf16[128,2048]{1,0:T(8,128)(2,1)S(1)} %collective-permute-done.28.refs_2_), channel_id=1, source_target_pairs={{0,4},{4,0},{1,5},{5,1},{2,6},{6,2},{3,7},{7,3},{8,12},{12,8},{9,1... | collective-permute-start | bytes 1572872 | tf_op jit(solution)/shard_map/ppermute | solution.py:542
  125.7 1.7 shard_map.156
  127.4 0.6 copy-done.8
  128.1 3.6 %collective-permute-start.34 = (bf16[256,1024]{1,0:T(8,128)(2,1)}, bf16[256,1024]{1,0:T(8,128)(2,1)S(1)}, u32[]{:S(2)}, u32[]{:S(2)}) collective-permute-start(bf16[256,1024]{1,0:T(8,128)(2,1)} %get-tuple-element.71.refs_0_), channel_id=1, source_target_pairs={{0,32},{4,12},{8,40},{12,20},{16,48},{20,28},{24,56},{28,4},{32,64... | collective-permute-start | bytes 1572872 | tf_op jit(solution)/shard_map/ppermute | solution.py:537
  131.7 0.8 copy-done.2
  132.5 2.4 %collective-permute-start.36 = (bf16[256,1024]{1,0:T(8,128)(2,1)}, bf16[256,1024]{1,0:T(8,128)(2,1)}, u32[]{:S(2)}, u32[]{:S(2)}) collective-permute-start(bf16[256,1024]{1,0:T(8,128)(2,1)} %get-tuple-element.71.refs_0_), channel_id=1, source_target_pairs={{0,96},{4,28},{8,104},{12,4},{16,112},{20,12},{24,120},{28,20},{32... | collective-permute-start | bytes 1572872 | tf_op jit(solution)/shard_map/ppermute | solution.py:537
  134.9 7.3 %all-to-all-start = ((bf16[128,24,128]{2,1,0:T(8,128)(2,1)}), bf16[128,24,128]{2,1,0:T(8,128)(2,1)}, u32[]{:S(2)}, u32[]{:S(2)}) async-start(bf16[128,24,128]{2,1,0:T(8,128)(2,1)} %get-tuple-element.68), calls=%async_computation | async-start | bytes 1572864 | tf_op jit(solution)/shard_map/all_to_all | solution.py:644
  142.2 1.2 collective-permute-start.33
  143.5 0.8 collective-permute-start.38
  144.3 0.8 collective-permute-done.35.refs_2_
  145.1 2.8 %collective-permute-start.40 = (bf16[256,1024]{1,0:T(8,128)(2,1)}, bf16[256,1024]{1,0:T(8,128)(2,1)S(1)}, u32[]{:S(2)}, u32[]{:S(2)}) collective-permute-start(bf16[256,1024]{1,0:T(8,128)(2,1)} %collective-permute-done.36.refs_3_), channel_id=1, source_target_pairs={{0,4},{4,0},{1,5},{5,1},{2,6},{6,2},{3,7},{7,3},{8,12},{12,8},{9,1... | collective-permute-start | bytes 1572872 | tf_op jit(solution)/shard_map/ppermute | solution.py:542
  147.9 1.0 copy-done.3
  148.9 1.5 shard_map.158.held_hbm
  150.4 2.0 %copy-done = bf16[1024,2048]{1,0:T(8,128)(2,1)} copy-done((bf16[1024,2048]{1,0:T(8,128)(2,1)}, bf16[1024,2048]{1,0:T(8,128)(2,1)S(1)}, u32[]{:S(2)}) %copy-start) | copy-done | bytes 4194328
  152.4 1.7 shard_map.159.grad_hbm
  154.1 2.0 %copy-done.1 = bf16[1024,2048]{1,0:T(8,128)(2,1)} copy-done((bf16[1024,2048]{1,0:T(8,128)(2,1)}, bf16[1024,2048]{1,0:T(8,128)(2,1)S(1)}, u32[]{:S(2)}) %copy-start.1) | copy-done | bytes 4194328
  156.1 2.5 %all-to-all-done.arrived_ref = bf16[128,24,128]{2,1,0:T(8,128)(2,1)} async-done(((bf16[128,24,128]{2,1,0:T(8,128)(2,1)}), bf16[128,24,128]{2,1,0:T(8,128)(2,1)}, u32[]{:S(2)}, u32[]{:S(2)}) %all-to-all-start) | async-done | bytes 786464 | tf_op jit(solution)/shard_map/all_to_all | solution.py:644
  158.6 11.7 %shard_map.160 = (f32[64,4096]{1,0:T(8,128)}, f32[1,4096]{1,0:T(1,128)}, bf16[1024,2048]{1,0:T(8,128)(2,1)}, f32[32,2048]{1,0:T(8,128)}) custom-call(bf16[128,24,128]{2,1,0:T(8,128)(2,1)} %all-to-all-done.arrived_ref, f32[32,2048]{1,0:T(8,128)} %rows_ref.1, f32[32,1024]{1,0:T(8,128)} %copy-done.8, f32[32,1024]{1,0:T(8,128)} %copy-done.19, ...), custom_call_target="tpu_custom_call" | custom-call | flops 8000000000 | bytes 2000000 | tf_op jit(solution)/shard_map/pallas_call | solution.py:282
  (79 shorter events, 1.5 us)
Async XLA Ops:
  0.6 1.0 copy-start.7
  1.7 0.7 copy-start.9
  2.4 0.7 copy-start.12
  3.0 11.5 %copy-start.18 = (bf16[2048]{0:T(1024)(128)(2,1)S(1)}, bf16[2048]{0:T(1024)(128)(2,1)}, u32[]{:S(2)}) copy-start(bf16[2048]{0:T(1024)(128)(2,1)} %param.20) | copy-start | bytes 12292
  3.0 11.6 %copy-start.6 = (bf16[1024,2048]{1,0:T(8,128)(2,1)S(1)}, bf16[1024,2048]{1,0:T(8,128)(2,1)}, u32[]{:S(2)}) copy-start(bf16[1024,2048]{1,0:T(8,128)(2,1)} %w_hbm.1) | copy-start | bytes 12582916
  3.1 11.6 %copy-start.11 = (f32[2048]{0:T(1024)S(1)}, f32[2048]{0:T(1024)}, u32[]{:S(2)}) copy-start(f32[2048]{0:T(1024)} %param.19) | copy-start | bytes 24580
  7.2 10.6 %collective-permute-start = (bf16[128,1024]{1,0:T(8,128)(2,1)S(1)}, bf16[128,1024]{1,0:T(8,128)(2,1)S(1)}, u32[]{:S(2)}, u32[]{:S(2)}) collective-permute-start(bf16[128,1024]{1,0:T(8,128)(2,1)S(1)} %get-tuple-element.40.refs_0_), channel_id=1, source_target_pairs={{0,1},{1,2},{2,3},{3,0},{4,5},{5,6},{6,7},{7,4},{8,9},{9,10},{10,1... | collective-permute-start | bytes 786440 | tf_op jit(solution)/shard_map/ppermute | solution.py:542
  9.7 8.1 %collective-permute-start.3 = (bf16[128,1024]{1,0:T(8,128)(2,1)S(1)}, bf16[128,1024]{1,0:T(8,128)(2,1)S(1)}, u32[]{:S(2)}, u32[]{:S(2)}) collective-permute-start(bf16[128,1024]{1,0:T(8,128)(2,1)S(1)} %get-tuple-element.41.refs_1_), channel_id=1, source_target_pairs={{0,3},{1,0},{2,1},{3,2},{4,7},{5,4},{6,5},{7,6},{8,11},{9,8},{10,9... | collective-permute-start | bytes 786440 | tf_op jit(solution)/shard_map/ppermute | solution.py:542
  11.9 11.5 %collective-permute-start.1 = (bf16[128,1024]{1,0:T(8,128)(2,1)S(1)}, bf16[128,1024]{1,0:T(8,128)(2,1)S(1)}, u32[]{:S(2)}, u32[]{:S(2)}) collective-permute-start(bf16[128,1024]{1,0:T(8,128)(2,1)S(1)} %get-tuple-element.41.refs_1_), channel_id=1, source_target_pairs={{0,1},{1,2},{2,3},{3,0},{4,5},{5,6},{6,7},{7,4},{8,9},{9,10},{10,1... | collective-permute-start | bytes 786440 | tf_op jit(solution)/shard_map/ppermute | solution.py:542
  11.9 11.5 %collective-permute-start.2 = (bf16[128,1024]{1,0:T(8,128)(2,1)S(1)}, bf16[128,1024]{1,0:T(8,128)(2,1)S(1)}, u32[]{:S(2)}, u32[]{:S(2)}) collective-permute-start(bf16[128,1024]{1,0:T(8,128)(2,1)S(1)} %get-tuple-element.40.refs_0_), channel_id=1, source_target_pairs={{0,3},{1,0},{2,1},{3,2},{4,7},{5,4},{6,5},{7,6},{8,11},{9,8},{10,9... | collective-permute-start | bytes 786440 | tf_op jit(solution)/shard_map/ppermute | solution.py:542
  17.8 11.2 %collective-permute-start.4 = (bf16[128,1024]{1,0:T(8,128)(2,1)S(1)}, bf16[128,1024]{1,0:T(8,128)(2,1)S(1)}, u32[]{:S(2)}, u32[]{:S(2)}) collective-permute-start(bf16[128,1024]{1,0:T(8,128)(2,1)S(1)} %collective-permute-done.refs_0_), channel_id=1, source_target_pairs={{0,1},{1,2},{2,3},{3,0},{4,5},{5,6},{6,7},{7,4},{8,9},{9,10},{10,1... | collective-permute-start | bytes 786440 | tf_op jit(solution)/shard_map/ppermute | solution.py:542
  17.8 11.2 %collective-permute-start.5 = (bf16[128,1024]{1,0:T(8,128)(2,1)S(1)}, bf16[128,1024]{1,0:T(8,128)(2,1)S(1)}, u32[]{:S(2)}, u32[]{:S(2)}) collective-permute-start(bf16[128,1024]{1,0:T(8,128)(2,1)S(1)} %collective-permute-done.3.refs_3_), channel_id=1, source_target_pairs={{0,3},{1,0},{2,1},{3,2},{4,7},{5,4},{6,5},{7,6},{8,11},{9,8},{10,9... | collective-permute-start | bytes 786440 | tf_op jit(solution)/shard_map/ppermute | solution.py:542
  27.4 10.0 %copy-start.4 = (s32[1024]{0:T(1024)S(1)}, s32[1024]{0:T(1024)}, u32[]{:S(2)}) copy-start(s32[1024]{0:T(1024)} %param.16) | copy-start | bytes 12292
  27.4 10.0 %copy-start.5 = (f32[1024]{0:T(1024)S(1)}, f32[1024]{0:T(1024)}, u32[]{:S(2)}) copy-start(f32[1024]{0:T(1024)} %param.17) | copy-start | bytes 12292
  30.9 3.3 %collective-permute-start.10 = (f32[4,256]{1,0:T(4,128)S(1)}, f32[4,256]{1,0:T(4,128)S(1)}, u32[]{:S(2)}, u32[]{:S(2)}) collective-permute-start(f32[4,256]{1,0:T(4,128)S(1)} %pad_maximum_fusion.refs_6_), channel_id=1, source_target_pairs={{0,3},{1,0},{2,1},{3,2},{4,7},{5,4},{6,5},{7,6},{8,11},{9,8},{10,9... | collective-permute-start | bytes 12296 | tf_op jit(solution)/shard_map/ppermute | solution.py:542
  33.5 4.0 %collective-permute-start.11 = (f32[4,256]{1,0:T(4,128)S(1)}, f32[4,256]{1,0:T(4,128)S(1)}, u32[]{:S(2)}, u32[]{:S(2)}) collective-permute-start(f32[4,256]{1,0:T(4,128)S(1)} %pad_maximum_fusion.refs_6_), channel_id=1, source_target_pairs={{0,2},{1,3},{2,0},{3,1},{4,6},{5,7},{6,4},{7,5},{8,10},{9,11},{10,... | collective-permute-start | bytes 12296 | tf_op jit(solution)/shard_map/ppermute | solution.py:542
  33.5 4.0 %collective-permute-start.9 = (f32[4,256]{1,0:T(4,128)S(1)}, f32[4,256]{1,0:T(4,128)S(1)}, u32[]{:S(2)}, u32[]{:S(2)}) collective-permute-start(f32[4,256]{1,0:T(4,128)S(1)} %pad_maximum_fusion.refs_6_), channel_id=1, source_target_pairs={{0,1},{1,2},{2,3},{3,0},{4,5},{5,6},{6,7},{7,4},{8,9},{9,10},{10,1... | collective-permute-start | bytes 12296 | tf_op jit(solution)/shard_map/ppermute | solution.py:542
  40.3 10.0 %collective-permute-start.12 = (bf16[1024,1024]{1,0:T(8,128)(2,1)S(1)}, bf16[1024,1024]{1,0:T(8,128)(2,1)S(1)}, u32[]{:S(2)}, u32[]{:S(2)}) collective-permute-start(bf16[1024,1024]{1,0:T(8,128)(2,1)S(1)} %get-tuple-element.55), channel_id=1, source_target_pairs={{0,4},{4,0},{1,5},{5,1},{2,6},{6,2},{3,7},{7,3},{8,12},{12,8},{9,1... | collective-permute-start | bytes 6291464 | tf_op jit(solution)/shard_map/ppermute | solution.py:542
  43.4 6.9 %collective-permute-start.7 = (bf16[1024,512]{1,0:T(8,128)(2,1)S(1)}, bf16[1024,512]{1,0:T(8,128)(2,1)S(1)}, u32[]{:S(2)}, u32[]{:S(2)}) collective-permute-start(bf16[1024,512]{1,0:T(8,128)(2,1)S(1)} %get-tuple-element.43.refs_1_), channel_id=1, source_target_pairs={{0,4},{4,0},{1,5},{5,1},{2,6},{6,2},{3,7},{7,3},{8,12},{12,8},{9,1... | collective-permute-start | bytes 3145736 | tf_op jit(solution)/shard_map/ppermute | solution.py:542
  43.5 5.9 %collective-permute-start.6 = (bf16[1024,256]{1,0:T(8,128)(2,1)S(1)}, bf16[1024,256]{1,0:T(8,128)(2,1)S(1)}, u32[]{:S(2)}, u32[]{:S(2)}) collective-permute-start(bf16[1024,256]{1,0:T(8,128)(2,1)S(1)} %get-tuple-element.42.refs_0_), channel_id=1, source_target_pairs={{0,4},{4,0},{1,5},{5,1},{2,6},{6,2},{3,7},{7,3},{8,12},{12,8},{9,1... | collective-permute-start | bytes 1572872 | tf_op jit(solution)/shard_map/ppermute | solution.py:542
  43.9 6.4 %collective-permute-start.8 = (bf16[1024,256]{1,0:T(8,128)(2,1)S(1)}, bf16[1024,256]{1,0:T(8,128)(2,1)S(1)}, u32[]{:S(2)}, u32[]{:S(2)}) collective-permute-start(bf16[1024,256]{1,0:T(8,128)(2,1)S(1)} %get-tuple-element.44.refs_2_), channel_id=1, source_target_pairs={{0,4},{4,0},{1,5},{5,1},{2,6},{6,2},{3,7},{7,3},{8,12},{12,8},{9,1... | collective-permute-start | bytes 1572872 | tf_op jit(solution)/shard_map/ppermute | solution.py:542
  44.0 6.3 %collective-permute-start.13 = (f32[16,1024]{1,0:T(8,128)S(1)}, f32[16,1024]{1,0:T(8,128)S(1)}, u32[]{:S(2)}, u32[]{:S(2)}) collective-permute-start(f32[16,1024]{1,0:T(8,128)S(1)} %get-tuple-element.57), channel_id=1, source_target_pairs={{0,4},{4,0},{1,5},{5,1},{2,6},{6,2},{3,7},{7,3},{8,12},{12,8},{9,1... | collective-permute-start | bytes 196616 | tf_op jit(solution)/shard_map/ppermute | solution.py:542
  52.6 21.2 %collective-permute-start.14 = (bf16[272,1024]{1,0:T(8,128)(2,1)S(1)}, bf16[272,1024]{1,0:T(8,128)(2,1)S(1)}, u32[]{:S(2)}, u32[]{:S(2)}) collective-permute-start(bf16[272,1024]{1,0:T(8,128)(2,1)S(1)} %get-tuple-element.59), channel_id=1, source_target_pairs={{0,32},{4,12},{8,40},{12,20},{16,48},{20,28},{24,56},{28,4},{32,64... | collective-permute-start | bytes 1671176 | tf_op jit(solution)/shard_map/ppermute | solution.py:537
  54.0 6.1 %copy-start.16 = (f32[32,2048]{1,0:T(8,128)S(1)}, f32[32,2048]{1,0:T(8,128)}, u32[]{:S(2)}) copy-start(f32[32,2048]{1,0:T(8,128)} %rows_ref.1) | copy-start | bytes 786436
  54.0 19.8 %collective-permute-start.16 = (bf16[272,1024]{1,0:T(8,128)(2,1)S(1)}, bf16[272,1024]{1,0:T(8,128)(2,1)S(1)}, u32[]{:S(2)}, u32[]{:S(2)}) collective-permute-start(bf16[272,1024]{1,0:T(8,128)(2,1)S(1)} %get-tuple-element.61), channel_id=1, source_target_pairs={{0,64},{4,20},{8,72},{12,28},{16,80},{20,4},{24,88},{28,12},{32,96... | collective-permute-start | bytes 1671176 | tf_op jit(solution)/shard_map/ppermute | solution.py:537
  59.0 14.8 %collective-permute-start.15 = (bf16[272,1024]{1,0:T(8,128)(2,1)S(1)}, bf16[272,1024]{1,0:T(8,128)(2,1)S(1)}, u32[]{:S(2)}, u32[]{:S(2)}) collective-permute-start(bf16[272,1024]{1,0:T(8,128)(2,1)S(1)} %get-tuple-element.60), channel_id=1, source_target_pairs={{0,96},{4,28},{8,104},{12,4},{16,112},{20,12},{24,120},{28,20},{32... | collective-permute-start | bytes 1671176 | tf_op jit(solution)/shard_map/ppermute | solution.py:537
  60.1 7.2 %collective-permute-start.24 = (bf16[32,2048]{1,0:T(8,128)(2,1)S(1)}, bf16[32,2048]{1,0:T(8,128)(2,1)S(1)}, u32[]{:S(2)}, u32[]{:S(2)}) collective-permute-start(bf16[32,2048]{1,0:T(8,128)(2,1)S(1)} %convert_element_type.3.refs_0_), channel_id=1, source_target_pairs={{0,8},{4,36},{8,16},{12,44},{16,24},{20,52},{24,0},{28,60},{32,40}... | collective-permute-start | bytes 393224 | tf_op jit(solution)/shard_map/ppermute | solution.py:537
  61.4 9.3 %collective-permute-start.25 = (bf16[32,2048]{1,0:T(8,128)(2,1)S(1)}, bf16[32,2048]{1,0:T(8,128)(2,1)S(1)}, u32[]{:S(2)}, u32[]{:S(2)}) collective-permute-start(bf16[32,2048]{1,0:T(8,128)(2,1)S(1)} %convert_element_type.3.refs_0_), channel_id=1, source_target_pairs={{0,16},{4,68},{8,24},{12,76},{16,0},{20,84},{24,8},{28,92},{32,48}... | collective-permute-start | bytes 393224 | tf_op jit(solution)/shard_map/ppermute | solution.py:537
  67.4 5.5 %collective-permute-start.26 = (bf16[32,2048]{1,0:T(8,128)(2,1)S(1)}, bf16[32,2048]{1,0:T(8,128)(2,1)S(1)}, u32[]{:S(2)}, u32[]{:S(2)}) collective-permute-start(bf16[32,2048]{1,0:T(8,128)(2,1)S(1)} %convert_element_type.3.refs_0_), channel_id=1, source_target_pairs={{0,24},{4,100},{8,0},{12,108},{16,8},{20,116},{24,16},{28,124},{32... | collective-permute-start | bytes 393224 | tf_op jit(solution)/shard_map/ppermute | solution.py:537
  72.9 17.0 %collective-permute-start.27 = (bf16[128,2048]{1,0:T(8,128)(2,1)S(1)}, bf16[128,2048]{1,0:T(8,128)(2,1)S(1)}, u32[]{:S(2)}, u32[]{:S(2)}) collective-permute-start(bf16[128,2048]{1,0:T(8,128)(2,1)S(1)} %shard_map.157.refs_0_), channel_id=1, source_target_pairs={{0,32},{4,12},{8,40},{12,20},{16,48},{20,28},{24,56},{28,4},{32,64... | collective-permute-start | bytes 1572872 | tf_op jit(solution)/shard_map/ppermute | solution.py:537
  73.0 18.7 %collective-permute-start.28 = (bf16[128,2048]{1,0:T(8,128)(2,1)S(1)}, bf16[128,2048]{1,0:T(8,128)(2,1)S(1)}, u32[]{:S(2)}, u32[]{:S(2)}) collective-permute-start(bf16[128,2048]{1,0:T(8,128)(2,1)S(1)} %shard_map.157.refs_0_), channel_id=1, source_target_pairs={{0,64},{4,20},{8,72},{12,28},{16,80},{20,4},{24,88},{28,12},{32,96... | collective-permute-start | bytes 1572872 | tf_op jit(solution)/shard_map/ppermute | solution.py:537
  74.0 17.6 %copy-start.17 = (s32[1,128,32]{1,2,0:T(8,128)S(1)}, s32[1,128,32]{1,2,0:T(8,128)}, u32[]{:S(2)}) copy-start(s32[1,128,32]{1,2,0:T(8,128)} %param.13) | copy-start | bytes 49156
  74.0 39.4 %copy-start.10 = (s32[256,16]{0,1:T(8,128)S(1)}, s32[256,16]{0,1:T(8,128)}, u32[]{:S(2)}) copy-start(s32[256,16]{0,1:T(8,128)} %param.15) | copy-start | bytes 49156
  74.1 39.4 %copy-start.13 = (s32[1,128]{1,0:T(1,128)S(1)}, s32[1,128]{1,0:T(1,128)}, u32[]{:S(2)}) copy-start(s32[1,128]{1,0:T(1,128)} %counts_ref.1) | copy-start | bytes 1540
  74.1 37.2 %collective-permute-start.17 = (bf16[272,1024]{1,0:T(8,128)(2,1)S(1)}, bf16[272,1024]{1,0:T(8,128)(2,1)S(1)}, u32[]{:S(2)}, u32[]{:S(2)}) collective-permute-start(bf16[272,1024]{1,0:T(8,128)(2,1)S(1)} %shard_map.153.own_ref), channel_id=1, source_target_pairs={{0,8},{4,36},{8,16},{12,44},{16,24},{20,52},{24,0},{28,60},{32,40}... | collective-permute-start | bytes 1671176 | tf_op jit(solution)/shard_map/ppermute | solution.py:537
  82.1 1.0 copy-start.14
  83.1 10.0 %collective-permute-start.20 = (bf16[256,1024]{1,0:T(8,128)(2,1)}, bf16[256,1024]{1,0:T(8,128)(2,1)}, u32[]{:S(2)}, u32[]{:S(2)}) collective-permute-start(bf16[256,1024]{1,0:T(8,128)(2,1)} %get-tuple-element.63), channel_id=1, source_target_pairs={{0,1},{1,2},{2,3},{3,0},{4,5},{5,6},{6,7},{7,4},{8,9},{9,10},{10,1... | collective-permute-start | bytes 1572872 | tf_op jit(solution)/shard_map/ppermute | solution.py:542
  83.1 27.1 %collective-permute-start.21 = (bf16[256,1024]{1,0:T(8,128)(2,1)}, bf16[256,1024]{1,0:T(8,128)(2,1)}, u32[]{:S(2)}, u32[]{:S(2)}) collective-permute-start(bf16[256,1024]{1,0:T(8,128)(2,1)} %get-tuple-element.64), channel_id=1, source_target_pairs={{0,3},{1,0},{2,1},{3,2},{4,7},{5,4},{6,5},{7,6},{8,11},{9,8},{10,9... | collective-permute-start | bytes 1572872 | tf_op jit(solution)/shard_map/ppermute | solution.py:542
  89.9 20.2 %collective-permute-start.22 = (bf16[256,1024]{1,0:T(8,128)(2,1)}, bf16[256,1024]{1,0:T(8,128)(2,1)}, u32[]{:S(2)}, u32[]{:S(2)}) collective-permute-start(bf16[256,1024]{1,0:T(8,128)(2,1)} %get-tuple-element.65), channel_id=1, source_target_pairs={{0,2},{1,3},{2,0},{3,1},{4,6},{5,7},{6,4},{7,5},{8,10},{9,11},{10,... | collective-permute-start | bytes 1572872 | tf_op jit(solution)/shard_map/ppermute | solution.py:542
  91.7 39.9 %collective-permute-start.29 = (bf16[128,2048]{1,0:T(8,128)(2,1)S(1)}, bf16[128,2048]{1,0:T(8,128)(2,1)S(1)}, u32[]{:S(2)}, u32[]{:S(2)}) collective-permute-start(bf16[128,2048]{1,0:T(8,128)(2,1)S(1)} %shard_map.157.refs_0_), channel_id=1, source_target_pairs={{0,96},{4,28},{8,104},{12,4},{16,112},{20,12},{24,120},{28,20},{32... | collective-permute-start | bytes 1572872 | tf_op jit(solution)/shard_map/ppermute | solution.py:537
  93.1 38.6 %collective-permute-start.30 = (bf16[128,2048]{1,0:T(8,128)(2,1)S(1)}, bf16[128,2048]{1,0:T(8,128)(2,1)S(1)}, u32[]{:S(2)}, u32[]{:S(2)}) collective-permute-start(bf16[128,2048]{1,0:T(8,128)(2,1)S(1)} %shard_map.157.refs_0_), channel_id=1, source_target_pairs={{0,4},{4,0},{1,5},{5,1},{2,6},{6,2},{3,7},{7,3},{8,12},{12,8},{9,1... | collective-permute-start | bytes 1572872 | tf_op jit(solution)/shard_map/ppermute | solution.py:542
  110.2 32.0 %collective-permute-start.31 = (bf16[128,2048]{1,0:T(8,128)(2,1)S(1)}, bf16[128,2048]{1,0:T(8,128)(2,1)}, u32[]{:S(2)}, u32[]{:S(2)}) collective-permute-start(bf16[128,2048]{1,0:T(8,128)(2,1)S(1)} %collective-permute-done.27.refs_1_), channel_id=1, source_target_pairs={{0,4},{4,0},{1,5},{5,1},{2,6},{6,2},{3,7},{7,3},{8,12},{12,8},{9,1... | collective-permute-start | bytes 1572872 | tf_op jit(solution)/shard_map/ppermute | solution.py:542
  110.2 12.8 %collective-permute-start.18 = (bf16[272,1024]{1,0:T(8,128)(2,1)S(1)}, bf16[272,1024]{1,0:T(8,128)(2,1)S(1)}, u32[]{:S(2)}, u32[]{:S(2)}) collective-permute-start(bf16[272,1024]{1,0:T(8,128)(2,1)S(1)} %shard_map.153.own_ref), channel_id=1, source_target_pairs={{0,24},{4,100},{8,0},{12,108},{16,8},{20,116},{24,16},{28,124},{32... | collective-permute-start | bytes 1671176 | tf_op jit(solution)/shard_map/ppermute | solution.py:537
  111.2 14.5 %collective-permute-start.19 = (bf16[272,1024]{1,0:T(8,128)(2,1)S(1)}, bf16[272,1024]{1,0:T(8,128)(2,1)S(1)}, u32[]{:S(2)}, u32[]{:S(2)}) collective-permute-start(bf16[272,1024]{1,0:T(8,128)(2,1)S(1)} %shard_map.153.own_ref), channel_id=1, source_target_pairs={{0,16},{4,68},{8,24},{12,76},{16,0},{20,84},{24,8},{28,92},{32,48}... | collective-permute-start | bytes 1671176 | tf_op jit(solution)/shard_map/ppermute | solution.py:537
  113.5 1.2 copy-start.15
  123.0 20.4 %collective-permute-start.32 = (bf16[128,2048]{1,0:T(8,128)(2,1)S(1)}, bf16[128,2048]{1,0:T(8,128)(2,1)}, u32[]{:S(2)}, u32[]{:S(2)}) collective-permute-start(bf16[128,2048]{1,0:T(8,128)(2,1)S(1)} %collective-permute-done.28.refs_2_), channel_id=1, source_target_pairs={{0,4},{4,0},{1,5},{5,1},{2,6},{6,2},{3,7},{7,3},{8,12},{12,8},{9,1... | collective-permute-start | bytes 1572872 | tf_op jit(solution)/shard_map/ppermute | solution.py:542
  127.4 0.6 copy-start.8
  128.1 15.4 %collective-permute-start.34 = (bf16[256,1024]{1,0:T(8,128)(2,1)}, bf16[256,1024]{1,0:T(8,128)(2,1)S(1)}, u32[]{:S(2)}, u32[]{:S(2)}) collective-permute-start(bf16[256,1024]{1,0:T(8,128)(2,1)} %get-tuple-element.71.refs_0_), channel_id=1, source_target_pairs={{0,32},{4,12},{8,40},{12,20},{16,48},{20,28},{24,56},{28,4},{32,64... | collective-permute-start | bytes 1572872 | tf_op jit(solution)/shard_map/ppermute | solution.py:537
  131.7 13.4 %collective-permute-start.35 = (bf16[256,1024]{1,0:T(8,128)(2,1)}, bf16[256,1024]{1,0:T(8,128)(2,1)}, u32[]{:S(2)}, u32[]{:S(2)}) collective-permute-start(bf16[256,1024]{1,0:T(8,128)(2,1)} %get-tuple-element.71.refs_0_), channel_id=1, source_target_pairs={{0,64},{4,20},{8,72},{12,28},{16,80},{20,4},{24,88},{28,12},{32,96... | collective-permute-start | bytes 1572872 | tf_op jit(solution)/shard_map/ppermute | solution.py:537
  131.7 0.8 copy-start.2
  132.5 12.6 %collective-permute-start.36 = (bf16[256,1024]{1,0:T(8,128)(2,1)}, bf16[256,1024]{1,0:T(8,128)(2,1)}, u32[]{:S(2)}, u32[]{:S(2)}) collective-permute-start(bf16[256,1024]{1,0:T(8,128)(2,1)} %get-tuple-element.71.refs_0_), channel_id=1, source_target_pairs={{0,96},{4,28},{8,104},{12,4},{16,112},{20,12},{24,120},{28,20},{32... | collective-permute-start | bytes 1572872 | tf_op jit(solution)/shard_map/ppermute | solution.py:537
  134.9 23.7 %all-to-all-start = ((bf16[128,24,128]{2,1,0:T(8,128)(2,1)}), bf16[128,24,128]{2,1,0:T(8,128)(2,1)}, u32[]{:S(2)}, u32[]{:S(2)}) async-start(bf16[128,24,128]{2,1,0:T(8,128)(2,1)} %get-tuple-element.68), calls=%async_computation | async-start | bytes 1572864 | tf_op jit(solution)/shard_map/all_to_all | solution.py:644
  142.2 5.7 %collective-permute-start.33 = (bf16[128,2048]{1,0:T(8,128)(2,1)S(1)}, bf16[128,2048]{1,0:T(8,128)(2,1)S(1)}, u32[]{:S(2)}, u32[]{:S(2)}) collective-permute-start(bf16[128,2048]{1,0:T(8,128)(2,1)S(1)} %collective-permute-done.29.refs_3_), channel_id=1, source_target_pairs={{0,4},{4,0},{1,5},{5,1},{2,6},{6,2},{3,7},{7,3},{8,12},{12,8},{9,1... | collective-permute-start | bytes 1572872 | tf_op jit(solution)/shard_map/ppermute | solution.py:542
  143.4 9.0 %collective-permute-start.37 = (bf16[256,1024]{1,0:T(8,128)(2,1)}, bf16[256,1024]{1,0:T(8,128)(2,1)S(1)}, u32[]{:S(2)}, u32[]{:S(2)}) collective-permute-start(bf16[256,1024]{1,0:T(8,128)(2,1)} %get-tuple-element.71.refs_0_), channel_id=1, source_target_pairs={{0,4},{4,0},{1,5},{5,1},{2,6},{6,2},{3,7},{7,3},{8,12},{12,8},{9,1... | collective-permute-start | bytes 1572872 | tf_op jit(solution)/shard_map/ppermute | solution.py:542
  143.5 8.9 %collective-permute-start.38 = (bf16[256,1024]{1,0:T(8,128)(2,1)S(1)}, bf16[256,1024]{1,0:T(8,128)(2,1)S(1)}, u32[]{:S(2)}, u32[]{:S(2)}) collective-permute-start(bf16[256,1024]{1,0:T(8,128)(2,1)S(1)} %collective-permute-done.34.refs_1_), channel_id=1, source_target_pairs={{0,4},{4,0},{1,5},{5,1},{2,6},{6,2},{3,7},{7,3},{8,12},{12,8},{9,1... | collective-permute-start | bytes 1572872 | tf_op jit(solution)/shard_map/ppermute | solution.py:542
  145.1 7.3 %collective-permute-start.39 = (bf16[256,1024]{1,0:T(8,128)(2,1)}, bf16[256,1024]{1,0:T(8,128)(2,1)S(1)}, u32[]{:S(2)}, u32[]{:S(2)}) collective-permute-start(bf16[256,1024]{1,0:T(8,128)(2,1)} %collective-permute-done.35.refs_2_), channel_id=1, source_target_pairs={{0,4},{4,0},{1,5},{5,1},{2,6},{6,2},{3,7},{7,3},{8,12},{12,8},{9,1... | collective-permute-start | bytes 1572872 | tf_op jit(solution)/shard_map/ppermute | solution.py:542
  145.1 7.3 %collective-permute-start.40 = (bf16[256,1024]{1,0:T(8,128)(2,1)}, bf16[256,1024]{1,0:T(8,128)(2,1)S(1)}, u32[]{:S(2)}, u32[]{:S(2)}) collective-permute-start(bf16[256,1024]{1,0:T(8,128)(2,1)} %collective-permute-done.36.refs_3_), channel_id=1, source_target_pairs={{0,4},{4,0},{1,5},{5,1},{2,6},{6,2},{3,7},{7,3},{8,12},{12,8},{9,1... | collective-permute-start | bytes 1572872 | tf_op jit(solution)/shard_map/ppermute | solution.py:542
  147.9 8.2 %collective-permute-start.23 = (f32[32,1024]{1,0:T(8,128)S(1)}, f32[32,1024]{1,0:T(8,128)S(1)}, u32[]{:S(2)}, u32[]{:S(2)}) collective-permute-start(f32[32,1024]{1,0:T(8,128)S(1)} %get-tuple-element.70), channel_id=1, source_target_pairs={{0,4},{4,0},{1,5},{5,1},{2,6},{6,2},{3,7},{7,3},{8,12},{12,8},{9,1... | collective-permute-start | bytes 393224 | tf_op jit(solution)/shard_map/ppermute | solution.py:542
  147.9 1.0 copy-start.3
  150.4 2.0 %copy-start = (bf16[1024,2048]{1,0:T(8,128)(2,1)}, bf16[1024,2048]{1,0:T(8,128)(2,1)S(1)}, u32[]{:S(2)}) copy-start(bf16[1024,2048]{1,0:T(8,128)(2,1)S(1)} %shard_map.158.held_hbm) | copy-start | bytes 12582916
  154.1 2.0 %copy-start.1 = (bf16[1024,2048]{1,0:T(8,128)(2,1)}, bf16[1024,2048]{1,0:T(8,128)(2,1)S(1)}, u32[]{:S(2)}) copy-start(bf16[1024,2048]{1,0:T(8,128)(2,1)S(1)} %shard_map.159.grad_hbm) | copy-start | bytes 12582916
  156.1 2.5 %copy-start.19 = (f32[32,1024]{1,0:T(8,128)}, f32[32,1024]{1,0:T(8,128)S(1)}, u32[]{:S(2)}) copy-start(f32[32,1024]{1,0:T(8,128)S(1)} %collective-permute-done.23.theirs_ref) | copy-start | bytes 393220

commit v4 on v3

--- a/solution.py
+++ b/solution.py
@@ -211,12 +211,12 @@
     rows = table_ref.shape[1]
     blocks = rows // 256
     every = sources * half
-    info = arrived_ref[:, half:, :].reshape(sources * 8, 128)
-    squares = jnp.sum(info.astype(F32)[:, 2 * capacity : 2 * capacity + 3], axis=0, keepdims=True)
-    total = jnp.sum(squares, axis=1, keepdims=True) * 0.125
+    info = jnp.sum(arrived_ref[:, half:, :].astype(F32), axis=1) * 0.125
+    squares = jnp.sum(info[:, 2 * capacity : 2 * capacity + 3], axis=0, keepdims=True)
+    total = jnp.sum(squares, axis=1, keepdims=True)
     scale = clip / jnp.maximum(jnp.sqrt(total), clip)
-    share = jnp.where(iota((sources * 8, every), 0) >> 3 == iota((sources * 8, every), 1) // half, 0.125, 0.0)
-    spread_info = dot_f32(info, share.astype(BF16), (((0,), (0,)), ((), ())))
+    share = jnp.where(iota((sources, every), 0) == iota((sources, every), 1) // half, 1.0, 0.0)
+    spread_info = dot_f32(info.astype(BF16), share.astype(BF16), (((0,), (0,)), ((), ())))
     slot = iota((capacity, every), 0)
     line = iota((capacity, every), 1) & (half - 1)
     inside_at = iota((256, every), 0).astype(F32)

time: 174 us -> 174 us (level)
  no operation moved by 1% of the time
where the time goes in v4:
time: 174 us; the launch traced here: 170 us
  starting transfers between devices  76 us (44%)
  Pallas kernels  49.9 us (29%)
  waiting for transfers between devices  32 us (18%)
  local copies, waits for them, and re-layouts  11.2 us (6%)
    ppermute x26, starting transfers between devices, send(): return lax.ppermute(x, axis, [(i, (i + shift) % n) for i in range(n)])  46.5 us
    pallas_call x14, Pallas kernels, call(): pl.pallas_call(kernel, out_shape=shapes, in_specs=[HBM if k in far else V...  45.8 us
    ppermute x15, starting transfers between devices, cross(): return lax.ppermute(x, DP, moves)  22.2 us
    ppermute x26, waiting for transfers between devices, send(): return lax.ppermute(x, axis, [(i, (i + shift) % n) for i in range(n)])  16.4 us
    ppermute x15, waiting for transfers between devices, cross(): return lax.ppermute(x, DP, moves)  13.1 us
    unnamed x41, local copies, waits for them, and re-layouts  11.2 us
    all_to_all x1, starting transfers between devices, inner(): arrived = lax.all_to_all(outgoing, DP_MP, 0, 0, tiled=True)  7.3 us
    pallas_call x1, Pallas kernels, gather_rows(): pl.pallas_call(gather_kernel, out_shape=(jax.ShapeDtypeStruct((batch // 2...  4.15 us
  transfers between devices with their start and end apart: 42, of which 14 were waited for; matrix products, arithmetic and copies ran while one was open for 0% of the time, Pallas kernels for 16%

profile of v4, /device:TPU:1, one launch (start us, length us, event | category | flops | bytes accessed | tf_op | source)
XLA Modules:
  0.0 170.2 jit_solution(796974927746396773)
XLA Ops:
  0.6 1.0 copy-done.7
  1.7 0.7 copy-done.9
  2.4 0.7 copy-done.12
  3.1 4.2 %gather_rows.1 = (bf16[128,1024]{1,0:T(8,128)(2,1)S(1)}, bf16[128,1024]{1,0:T(8,128)(2,1)S(1)}) custom-call(s32[1,128]{1,0:T(1,128)S(1)} %copy-done.12, s32[16,256]{1,0:T(8,128)S(1)} %bitcast.14, bf16[128,2048]{1,0:T(8,128)(2,1)S(1)} %bitcast.13), custom_call_target="tpu_custom_call" | custom-call | flops 6000000000 | bytes 2000000 | tf_op jit(solution)/shard_map/gather_rows/pallas_call | solution.py:95
  7.2 2.5 %collective-permute-start = (bf16[128,1024]{1,0:T(8,128)(2,1)S(1)}, bf16[128,1024]{1,0:T(8,128)(2,1)S(1)}, u32[]{:S(2)}, u32[]{:S(2)}) collective-permute-start(bf16[128,1024]{1,0:T(8,128)(2,1)S(1)} %get-tuple-element.40.refs_0_), channel_id=1, source_target_pairs={{0,1},{1,2},{2,3},{3,0},{4,5},{5,6},{6,7},{7,4},{8,9},{9,10},{10,1... | collective-permute-start | bytes 786440 | tf_op jit(solution)/shard_map/ppermute | solution.py:542
  9.7 2.2 %collective-permute-start.3 = (bf16[128,1024]{1,0:T(8,128)(2,1)S(1)}, bf16[128,1024]{1,0:T(8,128)(2,1)S(1)}, u32[]{:S(2)}, u32[]{:S(2)}) collective-permute-start(bf16[128,1024]{1,0:T(8,128)(2,1)S(1)} %get-tuple-element.41.refs_1_), channel_id=1, source_target_pairs={{0,3},{1,0},{2,1},{3,2},{4,7},{5,4},{6,5},{7,6},{8,11},{9,8},{10,9... | collective-permute-start | bytes 786440 | tf_op jit(solution)/shard_map/ppermute | solution.py:542
  11.9 2.7 %collective-permute-start.2 = (bf16[128,1024]{1,0:T(8,128)(2,1)S(1)}, bf16[128,1024]{1,0:T(8,128)(2,1)S(1)}, u32[]{:S(2)}, u32[]{:S(2)}) collective-permute-start(bf16[128,1024]{1,0:T(8,128)(2,1)S(1)} %get-tuple-element.40.refs_0_), channel_id=1, source_target_pairs={{0,3},{1,0},{2,1},{3,2},{4,7},{5,4},{6,5},{7,6},{8,11},{9,8},{10,9... | collective-permute-start | bytes 786440 | tf_op jit(solution)/shard_map/ppermute | solution.py:542
  14.6 1.9 %shard_map.147 = (f32[256,2048]{1,0:T(8,128)S(1)}, bf16[256,2048]{1,0:T(8,128)(2,1)S(1)}, f32[1,256]{1,0:T(1,128)S(1)}, bf16[1024,256]{1,0:T(8,128)(2,1)S(1)}) custom-call(bf16[128,1024]{1,0:T(8,128)(2,1)S(1)} %get-tuple-element.40.refs_0_, bf16[128,1024]{1,0:T(8,128)(2,1)S(1)} %get-tuple-element.41.refs_1_, bf16[1024,2048]{1,0:T(8,128)(2,1)S(1)} %copy-done.6, ...), custom_call_target="tpu_custom_call" | custom-call | flops 2560000000 | bytes 2000000 | tf_op jit(solution)/shard_map/pallas_call | solution.py:282
  16.5 1.3 collective-permute-done.refs_0_
  17.8 2.7 %collective-permute-start.5 = (bf16[128,1024]{1,0:T(8,128)(2,1)S(1)}, bf16[128,1024]{1,0:T(8,128)(2,1)S(1)}, u32[]{:S(2)}, u32[]{:S(2)}) collective-permute-start(bf16[128,1024]{1,0:T(8,128)(2,1)S(1)} %collective-permute-done.3.refs_3_), channel_id=1, source_target_pairs={{0,3},{1,0},{2,1},{3,2},{4,7},{5,4},{6,5},{7,6},{8,11},{9,8},{10,9... | collective-permute-start | bytes 786440 | tf_op jit(solution)/shard_map/ppermute | solution.py:542
  20.5 2.9 %collective-permute-done.1.refs_1_ = bf16[128,1024]{1,0:T(8,128)(2,1)S(1)} collective-permute-done((bf16[128,1024]{1,0:T(8,128)(2,1)S(1)}, bf16[128,1024]{1,0:T(8,128)(2,1)S(1)}, u32[]{:S(2)}, u32[]{:S(2)}) %collective-permute-start.1) | collective-permute-done | bytes 262176 | tf_op jit(solution)/shard_map/ppermute | solution.py:542
  23.5 3.9 %shard_map.148 = (f32[512,2048]{1,0:T(8,128)S(1)}, bf16[512,2048]{1,0:T(8,128)(2,1)S(1)}, f32[2,256]{1,0:T(2,128)S(1)}, bf16[1024,512]{1,0:T(8,128)(2,1)S(1)}) custom-call(bf16[128,1024]{1,0:T(8,128)(2,1)S(1)} %collective-permute-done.refs_0_, bf16[128,1024]{1,0:T(8,128)(2,1)S(1)} %collective-permute-done.1.refs_1_, ...), custom_call_target="tpu_custom_call" | custom-call | flops 5120000000 | bytes 2000000 | tf_op jit(solution)/shard_map/pallas_call | solution.py:282
  27.4 1.7 collective-permute-done.4.refs_0_
  29.1 1.8 %shard_map.149 = (f32[256,2048]{1,0:T(8,128)S(1)}, bf16[256,2048]{1,0:T(8,128)(2,1)S(1)}, f32[1,256]{1,0:T(1,128)S(1)}, bf16[1024,256]{1,0:T(8,128)(2,1)S(1)}) custom-call(bf16[128,1024]{1,0:T(8,128)(2,1)S(1)} %collective-permute-done.4.refs_0_, bf16[128,1024]{1,0:T(8,128)(2,1)S(1)} %collective-permute-done.5.refs_1_, bf16[1024,2048]{1,0:T(8,128)(2,1)S(1)} %copy-done.6, ...), custom_call_target="tpu_custom_call" | custom-call | flops 2560000000 | bytes 2000000 | tf_op jit(solution)/shard_map/pallas_call | solution.py:282
  30.9 2.5 %collective-permute-start.10 = (f32[4,256]{1,0:T(4,128)S(1)}, f32[4,256]{1,0:T(4,128)S(1)}, u32[]{:S(2)}, u32[]{:S(2)}) collective-permute-start(f32[4,256]{1,0:T(4,128)S(1)} %pad_maximum_fusion.refs_6_), channel_id=1, source_target_pairs={{0,3},{1,0},{2,1},{3,2},{4,7},{5,4},{6,5},{7,6},{8,11},{9,8},{10,9... | collective-permute-start | bytes 12296 | tf_op jit(solution)/shard_map/ppermute | solution.py:542
  33.5 0.7 collective-permute-start.9
  34.2 3.2 %collective-permute-done.11.refs_9_ = f32[4,256]{1,0:T(4,128)S(1)} collective-permute-done((f32[4,256]{1,0:T(4,128)S(1)}, f32[4,256]{1,0:T(4,128)S(1)}, u32[]{:S(2)}, u32[]{:S(2)}) %collective-permute-start.11) | collective-permute-done | bytes 4128 | tf_op jit(solution)/shard_map/ppermute | solution.py:542
  37.4 2.8 %shard_map.150 = (bf16[1024,2048]{1,0:T(8,128)(2,1)S(1)}, bf16[1024,1024]{1,0:T(8,128)(2,1)S(1)}, f32[16,1024]{1,0:T(8,128)S(1)}, f32[16,1024]{1,0:T(8,128)S(1)}) custom-call(f32[256,2048]{1,0:T(8,128)S(1)} %get-tuple-element.45.refs_0_, f32[512,2048]{1,0:T(8,128)S(1)} %get-tuple-element.46.refs_1_, f32[256,2048]{1,0:T(8,128)S(1)} %get-tuple-element.47.refs_2_, ...), custom_call_target="tpu_custom_call" | custom-call | flops 2000000000 | bytes 2000000 | tf_op jit(solution)/shard_map/pallas_call | solution.py:282
  40.3 3.1 %collective-permute-start.12 = (bf16[1024,1024]{1,0:T(8,128)(2,1)S(1)}, bf16[1024,1024]{1,0:T(8,128)(2,1)S(1)}, u32[]{:S(2)}, u32[]{:S(2)}) collective-permute-start(bf16[1024,1024]{1,0:T(8,128)(2,1)S(1)} %get-tuple-element.55), channel_id=1, source_target_pairs={{0,4},{4,0},{1,5},{5,1},{2,6},{6,2},{3,7},{7,3},{8,12},{12,8},{9,1... | collective-permute-start | bytes 6291464 | tf_op jit(solution)/shard_map/ppermute | solution.py:542
  44.0 0.4 collective-permute-start.13
  44.4 5.0 %collective-permute-done.6.refs_3_ = bf16[1024,256]{1,0:T(8,128)(2,1)S(1)} collective-permute-done((bf16[1024,256]{1,0:T(8,128)(2,1)S(1)}, bf16[1024,256]{1,0:T(8,128)(2,1)S(1)}, u32[]{:S(2)}, u32[]{:S(2)}) %collective-permute-start.6) | collective-permute-done | bytes 524320 | tf_op jit(solution)/shard_map/ppermute | solution.py:542
  49.4 0.8 collective-permute-done.13.refs_9_
  50.3 2.4 %shard_map.152 = (bf16[272,1024]{1,0:T(8,128)(2,1)S(1)}, bf16[272,1024]{1,0:T(8,128)(2,1)S(1)}) custom-call(bf16[1024,256]{1,0:T(8,128)(2,1)S(1)} %get-tuple-element.42.refs_0_, bf16[1024,512]{1,0:T(8,128)(2,1)S(1)} %get-tuple-element.43.refs_1_, bf16[1024,256]{1,0:T(8,128)(2,1)S(1)} %get-tuple-element.44.refs_2_, ...), custom_call_target="tpu_custom_call" | custom-call | flops 4000000000 | bytes 2000000 | tf_op jit(solution)/shard_map/pallas_call | solution.py:282
  52.6 1.4 collective-permute-start.14
  54.0 2.6 %collective-permute-start.16 = (bf16[272,1024]{1,0:T(8,128)(2,1)S(1)}, bf16[272,1024]{1,0:T(8,128)(2,1)S(1)}, u32[]{:S(2)}, u32[]{:S(2)}) collective-permute-start(bf16[272,1024]{1,0:T(8,128)(2,1)S(1)} %get-tuple-element.61), channel_id=1, source_target_pairs={{0,64},{4,20},{8,72},{12,28},{16,80},{20,4},{24,88},{28,12},{32,96... | collective-permute-start | bytes 1671176 | tf_op jit(solution)/shard_map/ppermute | solution.py:537
  56.6 2.4 %shard_map.151 = (bf16[272,1024]{1,0:T(8,128)(2,1)S(1)}, f32[272,1024]{1,0:T(8,128)S(1)}) custom-call(bf16[1024,256]{1,0:T(8,128)(2,1)S(1)} %get-tuple-element.42.refs_0_, bf16[1024,512]{1,0:T(8,128)(2,1)S(1)} %get-tuple-element.43.refs_1_, bf16[1024,256]{1,0:T(8,128)(2,1)S(1)} %get-tuple-element.44.refs_2_, ...), custom_call_target="tpu_custom_call" | custom-call | flops 4000000000 | bytes 2000000 | tf_op jit(solution)/shard_map/pallas_call | solution.py:282
  59.0 1.1 collective-permute-start.15
  60.1 1.3 collective-permute-start.24
  61.4 2.5 %collective-permute-start.25 = (bf16[32,2048]{1,0:T(8,128)(2,1)S(1)}, bf16[32,2048]{1,0:T(8,128)(2,1)S(1)}, u32[]{:S(2)}, u32[]{:S(2)}) collective-permute-start(bf16[32,2048]{1,0:T(8,128)(2,1)S(1)} %convert_element_type.3.refs_0_), channel_id=1, source_target_pairs={{0,16},{4,68},{8,24},{12,76},{16,0},{20,84},{24,8},{28,92},{32,48}... | collective-permute-start | bytes 393224 | tf_op jit(solution)/shard_map/ppermute | solution.py:537
  63.9 3.5 %collective-permute-done.24.refs_1_ = bf16[32,2048]{1,0:T(8,128)(2,1)S(1)} collective-permute-done((bf16[32,2048]{1,0:T(8,128)(2,1)S(1)}, bf16[32,2048]{1,0:T(8,128)(2,1)S(1)}, u32[]{:S(2)}, u32[]{:S(2)}) %collective-permute-start.24) | collective-permute-done | bytes 131104 | tf_op jit(solution)/shard_map/ppermute | solution.py:537
  67.4 0.8 collective-permute-start.26
  68.2 2.5 %collective-permute-done.25.refs_2_ = bf16[32,2048]{1,0:T(8,128)(2,1)S(1)} collective-permute-done((bf16[32,2048]{1,0:T(8,128)(2,1)S(1)}, bf16[32,2048]{1,0:T(8,128)(2,1)S(1)}, u32[]{:S(2)}, u32[]{:S(2)}) %collective-permute-start.25) | collective-permute-done | bytes 131104 | tf_op jit(solution)/shard_map/ppermute | solution.py:537
  70.7 2.1 %collective-permute-done.26.refs_3_ = bf16[32,2048]{1,0:T(8,128)(2,1)S(1)} collective-permute-done((bf16[32,2048]{1,0:T(8,128)(2,1)S(1)}, bf16[32,2048]{1,0:T(8,128)(2,1)S(1)}, u32[]{:S(2)}, u32[]{:S(2)}) %collective-permute-start.26) | collective-permute-done | bytes 131104 | tf_op jit(solution)/shard_map/ppermute | solution.py:537
  73.0 0.8 collective-permute-start.28
  74.1 2.3 %collective-permute-start.17 = (bf16[272,1024]{1,0:T(8,128)(2,1)S(1)}, bf16[272,1024]{1,0:T(8,128)(2,1)S(1)}, u32[]{:S(2)}, u32[]{:S(2)}) collective-permute-start(bf16[272,1024]{1,0:T(8,128)(2,1)S(1)} %shard_map.153.own_ref), channel_id=1, source_target_pairs={{0,8},{4,36},{8,16},{12,44},{16,24},{20,52},{24,0},{28,60},{32,40}... | collective-permute-start | bytes 1671176 | tf_op jit(solution)/shard_map/ppermute | solution.py:537
  76.4 5.7 %shard_map.154 = (f32[256,1024]{1,0:T(8,128)S(1)}, bf16[256,1024]{1,0:T(8,128)(2,1)}, bf16[256,1024]{1,0:T(8,128)(2,1)}, bf16[256,1024]{1,0:T(8,128)(2,1)}) custom-call(bf16[1024,2048]{1,0:T(8,128)(2,1)S(1)} %get-tuple-element.54.refs_6_.dact_ref, bf16[1024,2048]{1,0:T(8,128)(2,1)S(1)} %copy-done.6), custom_call_target="tpu_custom_call" | custom-call | flops 4000000000 | bytes 2000000 | tf_op jit(solution)/shard_map/pallas_call | solution.py:282
  82.1 1.0 copy-done.14
  83.1 2.7 %collective-permute-start.21 = (bf16[256,1024]{1,0:T(8,128)(2,1)}, bf16[256,1024]{1,0:T(8,128)(2,1)}, u32[]{:S(2)}, u32[]{:S(2)}) collective-permute-start(bf16[256,1024]{1,0:T(8,128)(2,1)} %get-tuple-element.64), channel_id=1, source_target_pairs={{0,3},{1,0},{2,1},{3,2},{4,7},{5,4},{6,5},{7,6},{8,11},{9,8},{10,9... | collective-permute-start | bytes 1572872 | tf_op jit(solution)/shard_map/ppermute | solution.py:542
  85.7 4.2 %collective-permute-done.27.refs_1_ = bf16[128,2048]{1,0:T(8,128)(2,1)S(1)} collective-permute-done((bf16[128,2048]{1,0:T(8,128)(2,1)S(1)}, bf16[128,2048]{1,0:T(8,128)(2,1)S(1)}, u32[]{:S(2)}, u32[]{:S(2)}) %collective-permute-start.27) | collective-permute-done | bytes 524320 | tf_op jit(solution)/shard_map/ppermute | solution.py:537
  89.9 1.7 %collective-permute-start.22 = (bf16[256,1024]{1,0:T(8,128)(2,1)}, bf16[256,1024]{1,0:T(8,128)(2,1)}, u32[]{:S(2)}, u32[]{:S(2)}) collective-permute-start(bf16[256,1024]{1,0:T(8,128)(2,1)} %get-tuple-element.65), channel_id=1, source_target_pairs={{0,2},{1,3},{2,0},{3,1},{4,6},{5,7},{6,4},{7,5},{8,10},{9,11},{10,... | collective-permute-start | bytes 1572872 | tf_op jit(solution)/shard_map/ppermute | solution.py:542
  91.8 1.2 collective-permute-done.20.a_ref
  93.1 17.1 %collective-permute-start.30 = (bf16[128,2048]{1,0:T(8,128)(2,1)S(1)}, bf16[128,2048]{1,0:T(8,128)(2,1)S(1)}, u32[]{:S(2)}, u32[]{:S(2)}) collective-permute-start(bf16[128,2048]{1,0:T(8,128)(2,1)S(1)} %shard_map.157.refs_0_), channel_id=1, source_target_pairs={{0,4},{4,0},{1,5},{5,1},{2,6},{6,2},{3,7},{7,3},{8,12},{12,8},{9,1... | collective-permute-start | bytes 1572872 | tf_op jit(solution)/shard_map/ppermute | solution.py:542
  110.2 1.1 collective-permute-start.18
  111.2 2.3 %collective-permute-start.19 = (bf16[272,1024]{1,0:T(8,128)(2,1)S(1)}, bf16[272,1024]{1,0:T(8,128)(2,1)S(1)}, u32[]{:S(2)}, u32[]{:S(2)}) collective-permute-start(bf16[272,1024]{1,0:T(8,128)(2,1)S(1)} %shard_map.153.own_ref), channel_id=1, source_target_pairs={{0,16},{4,68},{8,24},{12,76},{16,0},{20,84},{24,8},{28,92},{32,48}... | collective-permute-start | bytes 1671176 | tf_op jit(solution)/shard_map/ppermute | solution.py:537
  113.5 1.2 copy-done.15
  114.7 8.3 %shard_map.155 = (bf16[128,16,128]{2,1,0:T(8,128)(2,1)S(1)}, f32[8,128]{1,0:T(8,128)S(1)}) custom-call(s32[1,128]{1,0:T(1,128)S(1)} %copy-done.13, s32[16,256]{1,0:T(8,128)S(1)} %bitcast.15, f32[256,1024]{1,0:T(8,128)S(1)} %copy-done.15, bf16[256,1024]{1,0:T(8,128)(2,1)} %collective-permute-done.20.a_ref, bf16[256,1024]{1,0:T(8,128)(2,1)} %collective-permute-done.21.b_ref, ...), custom_call_target="tpu_custom_call" | custom-call | flops 8000000000 | bytes 2000000 | tf_op jit(solution)/shard_map/pallas_call | solution.py:282
  123.0 2.7 %collective-permute-start.32 = (bf16[128,2048]{1,0:T(8,128)(2,1)S(1)}, bf16[128,2048]{1,0:T(8,128)(2,1)}, u32[]{:S(2)}, u32[]{:S(2)}) collective-permute-start(bf16[128,2048]{1,0:T(8,128)(2,1)S(1)} %collective-permute-done.28.refs_2_), channel_id=1, source_target_pairs={{0,4},{4,0},{1,5},{5,1},{2,6},{6,2},{3,7},{7,3},{8,12},{12,8},{9,1... | collective-permute-start | bytes 1572872 | tf_op jit(solution)/shard_map/ppermute | solution.py:542
  125.7 1.7 shard_map.156
  127.4 0.6 copy-done.8
  128.1 3.6 %collective-permute-start.34 = (bf16[256,1024]{1,0:T(8,128)(2,1)}, bf16[256,1024]{1,0:T(8,128)(2,1)S(1)}, u32[]{:S(2)}, u32[]{:S(2)}) collective-permute-start(bf16[256,1024]{1,0:T(8,128)(2,1)} %get-tuple-element.71.refs_0_), channel_id=1, source_target_pairs={{0,32},{4,12},{8,40},{12,20},{16,48},{20,28},{24,56},{28,4},{32,64... | collective-permute-start | bytes 1572872 | tf_op jit(solution)/shard_map/ppermute | solution.py:537
  131.7 0.8 copy-done.2
  132.5 2.4 %collective-permute-start.36 = (bf16[256,1024]{1,0:T(8,128)(2,1)}, bf16[256,1024]{1,0:T(8,128)(2,1)}, u32[]{:S(2)}, u32[]{:S(2)}) collective-permute-start(bf16[256,1024]{1,0:T(8,128)(2,1)} %get-tuple-element.71.refs_0_), channel_id=1, source_target_pairs={{0,96},{4,28},{8,104},{12,4},{16,112},{20,12},{24,120},{28,20},{32... | collective-permute-start | bytes 1572872 | tf_op jit(solution)/shard_map/ppermute | solution.py:537
  134.9 7.3 %all-to-all-start = ((bf16[128,24,128]{2,1,0:T(8,128)(2,1)}), bf16[128,24,128]{2,1,0:T(8,128)(2,1)}, u32[]{:S(2)}, u32[]{:S(2)}) async-start(bf16[128,24,128]{2,1,0:T(8,128)(2,1)} %get-tuple-element.68), calls=%async_computation | async-start | bytes 1572864 | tf_op jit(solution)/shard_map/all_to_all | solution.py:644
  142.2 1.2 collective-permute-start.33
  143.5 0.8 collective-permute-start.38
  144.3 0.8 collective-permute-done.35.refs_2_
  145.1 2.8 %collective-permute-start.40 = (bf16[256,1024]{1,0:T(8,128)(2,1)}, bf16[256,1024]{1,0:T(8,128)(2,1)S(1)}, u32[]{:S(2)}, u32[]{:S(2)}) collective-permute-start(bf16[256,1024]{1,0:T(8,128)(2,1)} %collective-permute-done.36.refs_3_), channel_id=1, source_target_pairs={{0,4},{4,0},{1,5},{5,1},{2,6},{6,2},{3,7},{7,3},{8,12},{12,8},{9,1... | collective-permute-start | bytes 1572872 | tf_op jit(solution)/shard_map/ppermute | solution.py:542
  147.9 1.0 copy-done.3
  148.9 1.5 shard_map.158.held_hbm
  150.4 2.0 %copy-done = bf16[1024,2048]{1,0:T(8,128)(2,1)} copy-done((bf16[1024,2048]{1,0:T(8,128)(2,1)}, bf16[1024,2048]{1,0:T(8,128)(2,1)S(1)}, u32[]{:S(2)}) %copy-start) | copy-done | bytes 4194328
  152.4 1.7 shard_map.159.grad_hbm
  154.1 2.0 %copy-done.1 = bf16[1024,2048]{1,0:T(8,128)(2,1)} copy-done((bf16[1024,2048]{1,0:T(8,128)(2,1)}, bf16[1024,2048]{1,0:T(8,128)(2,1)S(1)}, u32[]{:S(2)}) %copy-start.1) | copy-done | bytes 4194328
  156.1 2.5 %all-to-all-done.arrived_ref = bf16[128,24,128]{2,1,0:T(8,128)(2,1)} async-done(((bf16[128,24,128]{2,1,0:T(8,128)(2,1)}), bf16[128,24,128]{2,1,0:T(8,128)(2,1)}, u32[]{:S(2)}, u32[]{:S(2)}) %all-to-all-start) | async-done | bytes 786464 | tf_op jit(solution)/shard_map/all_to_all | solution.py:644
  158.6 11.5 %shard_map.160 = (f32[64,4096]{1,0:T(8,128)}, f32[1,4096]{1,0:T(1,128)}, bf16[1024,2048]{1,0:T(8,128)(2,1)}, f32[32,2048]{1,0:T(8,128)}) custom-call(bf16[128,24,128]{2,1,0:T(8,128)(2,1)} %all-to-all-done.arrived_ref, f32[32,2048]{1,0:T(8,128)} %rows_ref.1, f32[32,1024]{1,0:T(8,128)} %copy-done.8, f32[32,1024]{1,0:T(8,128)} %copy-done.19, ...), custom_call_target="tpu_custom_call" | custom-call | flops 8000000000 | bytes 2000000 | tf_op jit(solution)/shard_map/pallas_call | solution.py:282
  (79 shorter events, 1.5 us)
Async XLA Ops:
  0.6 1.0 copy-start.7
  1.7 0.7 copy-start.9
  2.4 0.7 copy-start.12
  3.0 11.5 %copy-start.18 = (bf16[2048]{0:T(1024)(128)(2,1)S(1)}, bf16[2048]{0:T(1024)(128)(2,1)}, u32[]{:S(2)}) copy-start(bf16[2048]{0:T(1024)(128)(2,1)} %param.20) | copy-start | bytes 12292
  3.0 11.6 %copy-start.6 = (bf16[1024,2048]{1,0:T(8,128)(2,1)S(1)}, bf16[1024,2048]{1,0:T(8,128)(2,1)}, u32[]{:S(2)}) copy-start(bf16[1024,2048]{1,0:T(8,128)(2,1)} %w_hbm.1) | copy-start | bytes 12582916
  3.1 11.6 %copy-start.11 = (f32[2048]{0:T(1024)S(1)}, f32[2048]{0:T(1024)}, u32[]{:S(2)}) copy-start(f32[2048]{0:T(1024)} %param.19) | copy-start | bytes 24580
  7.2 10.6 %collective-permute-start = (bf16[128,1024]{1,0:T(8,128)(2,1)S(1)}, bf16[128,1024]{1,0:T(8,128)(2,1)S(1)}, u32[]{:S(2)}, u32[]{:S(2)}) collective-permute-start(bf16[128,1024]{1,0:T(8,128)(2,1)S(1)} %get-tuple-element.40.refs_0_), channel_id=1, source_target_pairs={{0,1},{1,2},{2,3},{3,0},{4,5},{5,6},{6,7},{7,4},{8,9},{9,10},{10,1... | collective-permute-start | bytes 786440 | tf_op jit(solution)/shard_map/ppermute | solution.py:542
  9.7 8.1 %collective-permute-start.3 = (bf16[128,1024]{1,0:T(8,128)(2,1)S(1)}, bf16[128,1024]{1,0:T(8,128)(2,1)S(1)}, u32[]{:S(2)}, u32[]{:S(2)}) collective-permute-start(bf16[128,1024]{1,0:T(8,128)(2,1)S(1)} %get-tuple-element.41.refs_1_), channel_id=1, source_target_pairs={{0,3},{1,0},{2,1},{3,2},{4,7},{5,4},{6,5},{7,6},{8,11},{9,8},{10,9... | collective-permute-start | bytes 786440 | tf_op jit(solution)/shard_map/ppermute | solution.py:542
  11.9 11.5 %collective-permute-start.1 = (bf16[128,1024]{1,0:T(8,128)(2,1)S(1)}, bf16[128,1024]{1,0:T(8,128)(2,1)S(1)}, u32[]{:S(2)}, u32[]{:S(2)}) collective-permute-start(bf16[128,1024]{1,0:T(8,128)(2,1)S(1)} %get-tuple-element.41.refs_1_), channel_id=1, source_target_pairs={{0,1},{1,2},{2,3},{3,0},{4,5},{5,6},{6,7},{7,4},{8,9},{9,10},{10,1... | collective-permute-start | bytes 786440 | tf_op jit(solution)/shard_map/ppermute | solution.py:542
  11.9 11.5 %collective-permute-start.2 = (bf16[128,1024]{1,0:T(8,128)(2,1)S(1)}, bf16[128,1024]{1,0:T(8,128)(2,1)S(1)}, u32[]{:S(2)}, u32[]{:S(2)}) collective-permute-start(bf16[128,1024]{1,0:T(8,128)(2,1)S(1)} %get-tuple-element.40.refs_0_), channel_id=1, source_target_pairs={{0,3},{1,0},{2,1},{3,2},{4,7},{5,4},{6,5},{7,6},{8,11},{9,8},{10,9... | collective-permute-start | bytes 786440 | tf_op jit(solution)/shard_map/ppermute | solution.py:542
  17.8 11.2 %collective-permute-start.4 = (bf16[128,1024]{1,0:T(8,128)(2,1)S(1)}, bf16[128,1024]{1,0:T(8,128)(2,1)S(1)}, u32[]{:S(2)}, u32[]{:S(2)}) collective-permute-start(bf16[128,1024]{1,0:T(8,128)(2,1)S(1)} %collective-permute-done.refs_0_), channel_id=1, source_target_pairs={{0,1},{1,2},{2,3},{3,0},{4,5},{5,6},{6,7},{7,4},{8,9},{9,10},{10,1... | collective-permute-start | bytes 786440 | tf_op jit(solution)/shard_map/ppermute | solution.py:542
  17.8 11.2 %collective-permute-start.5 = (bf16[128,1024]{1,0:T(8,128)(2,1)S(1)}, bf16[128,1024]{1,0:T(8,128)(2,1)S(1)}, u32[]{:S(2)}, u32[]{:S(2)}) collective-permute-start(bf16[128,1024]{1,0:T(8,128)(2,1)S(1)} %collective-permute-done.3.refs_3_), channel_id=1, source_target_pairs={{0,3},{1,0},{2,1},{3,2},{4,7},{5,4},{6,5},{7,6},{8,11},{9,8},{10,9... | collective-permute-start | bytes 786440 | tf_op jit(solution)/shard_map/ppermute | solution.py:542
  27.4 10.0 %copy-start.4 = (s32[1024]{0:T(1024)S(1)}, s32[1024]{0:T(1024)}, u32[]{:S(2)}) copy-start(s32[1024]{0:T(1024)} %param.16) | copy-start | bytes 12292
  27.4 10.0 %copy-start.5 = (f32[1024]{0:T(1024)S(1)}, f32[1024]{0:T(1024)}, u32[]{:S(2)}) copy-start(f32[1024]{0:T(1024)} %param.17) | copy-start | bytes 12292
  30.9 3.3 %collective-permute-start.10 = (f32[4,256]{1,0:T(4,128)S(1)}, f32[4,256]{1,0:T(4,128)S(1)}, u32[]{:S(2)}, u32[]{:S(2)}) collective-permute-start(f32[4,256]{1,0:T(4,128)S(1)} %pad_maximum_fusion.refs_6_), channel_id=1, source_target_pairs={{0,3},{1,0},{2,1},{3,2},{4,7},{5,4},{6,5},{7,6},{8,11},{9,8},{10,9... | collective-permute-start | bytes 12296 | tf_op jit(solution)/shard_map/ppermute | solution.py:542
  33.5 4.0 %collective-permute-start.11 = (f32[4,256]{1,0:T(4,128)S(1)}, f32[4,256]{1,0:T(4,128)S(1)}, u32[]{:S(2)}, u32[]{:S(2)}) collective-permute-start(f32[4,256]{1,0:T(4,128)S(1)} %pad_maximum_fusion.refs_6_), channel_id=1, source_target_pairs={{0,2},{1,3},{2,0},{3,1},{4,6},{5,7},{6,4},{7,5},{8,10},{9,11},{10,... | collective-permute-start | bytes 12296 | tf_op jit(solution)/shard_map/ppermute | solution.py:542
  33.5 4.0 %collective-permute-start.9 = (f32[4,256]{1,0:T(4,128)S(1)}, f32[4,256]{1,0:T(4,128)S(1)}, u32[]{:S(2)}, u32[]{:S(2)}) collective-permute-start(f32[4,256]{1,0:T(4,128)S(1)} %pad_maximum_fusion.refs_6_), channel_id=1, source_target_pairs={{0,1},{1,2},{2,3},{3,0},{4,5},{5,6},{6,7},{7,4},{8,9},{9,10},{10,1... | collective-permute-start | bytes 12296 | tf_op jit(solution)/shard_map/ppermute | solution.py:542
  40.3 10.0 %collective-permute-start.12 = (bf16[1024,1024]{1,0:T(8,128)(2,1)S(1)}, bf16[1024,1024]{1,0:T(8,128)(2,1)S(1)}, u32[]{:S(2)}, u32[]{:S(2)}) collective-permute-start(bf16[1024,1024]{1,0:T(8,128)(2,1)S(1)} %get-tuple-element.55), channel_id=1, source_target_pairs={{0,4},{4,0},{1,5},{5,1},{2,6},{6,2},{3,7},{7,3},{8,12},{12,8},{9,1... | collective-permute-start | bytes 6291464 | tf_op jit(solution)/shard_map/ppermute | solution.py:542
  43.4 6.9 %collective-permute-start.7 = (bf16[1024,512]{1,0:T(8,128)(2,1)S(1)}, bf16[1024,512]{1,0:T(8,128)(2,1)S(1)}, u32[]{:S(2)}, u32[]{:S(2)}) collective-permute-start(bf16[1024,512]{1,0:T(8,128)(2,1)S(1)} %get-tuple-element.43.refs_1_), channel_id=1, source_target_pairs={{0,4},{4,0},{1,5},{5,1},{2,6},{6,2},{3,7},{7,3},{8,12},{12,8},{9,1... | collective-permute-start | bytes 3145736 | tf_op jit(solution)/shard_map/ppermute | solution.py:542
  43.5 5.9 %collective-permute-start.6 = (bf16[1024,256]{1,0:T(8,128)(2,1)S(1)}, bf16[1024,256]{1,0:T(8,128)(2,1)S(1)}, u32[]{:S(2)}, u32[]{:S(2)}) collective-permute-start(bf16[1024,256]{1,0:T(8,128)(2,1)S(1)} %get-tuple-element.42.refs_0_), channel_id=1, source_target_pairs={{0,4},{4,0},{1,5},{5,1},{2,6},{6,2},{3,7},{7,3},{8,12},{12,8},{9,1... | collective-permute-start | bytes 1572872 | tf_op jit(solution)/shard_map/ppermute | solution.py:542
  43.9 6.4 %collective-permute-start.8 = (bf16[1024,256]{1,0:T(8,128)(2,1)S(1)}, bf16[1024,256]{1,0:T(8,128)(2,1)S(1)}, u32[]{:S(2)}, u32[]{:S(2)}) collective-permute-start(bf16[1024,256]{1,0:T(8,128)(2,1)S(1)} %get-tuple-element.44.refs_2_), channel_id=1, source_target_pairs={{0,4},{4,0},{1,5},{5,1},{2,6},{6,2},{3,7},{7,3},{8,12},{12,8},{9,1... | collective-permute-start | bytes 1572872 | tf_op jit(solution)/shard_map/ppermute | solution.py:542
  44.0 6.3 %collective-permute-start.13 = (f32[16,1024]{1,0:T(8,128)S(1)}, f32[16,1024]{1,0:T(8,128)S(1)}, u32[]{:S(2)}, u32[]{:S(2)}) collective-permute-start(f32[16,1024]{1,0:T(8,128)S(1)} %get-tuple-element.57), channel_id=1, source_target_pairs={{0,4},{4,0},{1,5},{5,1},{2,6},{6,2},{3,7},{7,3},{8,12},{12,8},{9,1... | collective-permute-start | bytes 196616 | tf_op jit(solution)/shard_map/ppermute | solution.py:542
  52.6 21.2 %collective-permute-start.14 = (bf16[272,1024]{1,0:T(8,128)(2,1)S(1)}, bf16[272,1024]{1,0:T(8,128)(2,1)S(1)}, u32[]{:S(2)}, u32[]{:S(2)}) collective-permute-start(bf16[272,1024]{1,0:T(8,128)(2,1)S(1)} %get-tuple-element.59), channel_id=1, source_target_pairs={{0,32},{4,12},{8,40},{12,20},{16,48},{20,28},{24,56},{28,4},{32,64... | collective-permute-start | bytes 1671176 | tf_op jit(solution)/shard_map/ppermute | solution.py:537
  54.0 6.1 %copy-start.16 = (f32[32,2048]{1,0:T(8,128)S(1)}, f32[32,2048]{1,0:T(8,128)}, u32[]{:S(2)}) copy-start(f32[32,2048]{1,0:T(8,128)} %rows_ref.1) | copy-start | bytes 786436
  54.0 19.8 %collective-permute-start.16 = (bf16[272,1024]{1,0:T(8,128)(2,1)S(1)}, bf16[272,1024]{1,0:T(8,128)(2,1)S(1)}, u32[]{:S(2)}, u32[]{:S(2)}) collective-permute-start(bf16[272,1024]{1,0:T(8,128)(2,1)S(1)} %get-tuple-element.61), channel_id=1, source_target_pairs={{0,64},{4,20},{8,72},{12,28},{16,80},{20,4},{24,88},{28,12},{32,96... | collective-permute-start | bytes 1671176 | tf_op jit(solution)/shard_map/ppermute | solution.py:537
  59.0 14.8 %collective-permute-start.15 = (bf16[272,1024]{1,0:T(8,128)(2,1)S(1)}, bf16[272,1024]{1,0:T(8,128)(2,1)S(1)}, u32[]{:S(2)}, u32[]{:S(2)}) collective-permute-start(bf16[272,1024]{1,0:T(8,128)(2,1)S(1)} %get-tuple-element.60), channel_id=1, source_target_pairs={{0,96},{4,28},{8,104},{12,4},{16,112},{20,12},{24,120},{28,20},{32... | collective-permute-start | bytes 1671176 | tf_op jit(solution)/shard_map/ppermute | solution.py:537
  60.1 7.2 %collective-permute-start.24 = (bf16[32,2048]{1,0:T(8,128)(2,1)S(1)}, bf16[32,2048]{1,0:T(8,128)(2,1)S(1)}, u32[]{:S(2)}, u32[]{:S(2)}) collective-permute-start(bf16[32,2048]{1,0:T(8,128)(2,1)S(1)} %convert_element_type.3.refs_0_), channel_id=1, source_target_pairs={{0,8},{4,36},{8,16},{12,44},{16,24},{20,52},{24,0},{28,60},{32,40}... | collective-permute-start | bytes 393224 | tf_op jit(solution)/shard_map/ppermute | solution.py:537
  61.4 9.3 %collective-permute-start.25 = (bf16[32,2048]{1,0:T(8,128)(2,1)S(1)}, bf16[32,2048]{1,0:T(8,128)(2,1)S(1)}, u32[]{:S(2)}, u32[]{:S(2)}) collective-permute-start(bf16[32,2048]{1,0:T(8,128)(2,1)S(1)} %convert_element_type.3.refs_0_), channel_id=1, source_target_pairs={{0,16},{4,68},{8,24},{12,76},{16,0},{20,84},{24,8},{28,92},{32,48}... | collective-permute-start | bytes 393224 | tf_op jit(solution)/shard_map/ppermute | solution.py:537
  67.4 5.5 %collective-permute-start.26 = (bf16[32,2048]{1,0:T(8,128)(2,1)S(1)}, bf16[32,2048]{1,0:T(8,128)(2,1)S(1)}, u32[]{:S(2)}, u32[]{:S(2)}) collective-permute-start(bf16[32,2048]{1,0:T(8,128)(2,1)S(1)} %convert_element_type.3.refs_0_), channel_id=1, source_target_pairs={{0,24},{4,100},{8,0},{12,108},{16,8},{20,116},{24,16},{28,124},{32... | collective-permute-start | bytes 393224 | tf_op jit(solution)/shard_map/ppermute | solution.py:537
  72.9 17.0 %collective-permute-start.27 = (bf16[128,2048]{1,0:T(8,128)(2,1)S(1)}, bf16[128,2048]{1,0:T(8,128)(2,1)S(1)}, u32[]{:S(2)}, u32[]{:S(2)}) collective-permute-start(bf16[128,2048]{1,0:T(8,128)(2,1)S(1)} %shard_map.157.refs_0_), channel_id=1, source_target_pairs={{0,32},{4,12},{8,40},{12,20},{16,48},{20,28},{24,56},{28,4},{32,64... | collective-permute-start | bytes 1572872 | tf_op jit(solution)/shard_map/ppermute | solution.py:537
  73.0 18.7 %collective-permute-start.28 = (bf16[128,2048]{1,0:T(8,128)(2,1)S(1)}, bf16[128,2048]{1,0:T(8,128)(2,1)S(1)}, u32[]{:S(2)}, u32[]{:S(2)}) collective-permute-start(bf16[128,2048]{1,0:T(8,128)(2,1)S(1)} %shard_map.157.refs_0_), channel_id=1, source_target_pairs={{0,64},{4,20},{8,72},{12,28},{16,80},{20,4},{24,88},{28,12},{32,96... | collective-permute-start | bytes 1572872 | tf_op jit(solution)/shard_map/ppermute | solution.py:537
  74.0 17.6 %copy-start.17 = (s32[1,128,32]{1,2,0:T(8,128)S(1)}, s32[1,128,32]{1,2,0:T(8,128)}, u32[]{:S(2)}) copy-start(s32[1,128,32]{1,2,0:T(8,128)} %param.13) | copy-start | bytes 49156
  74.0 39.4 %copy-start.10 = (s32[256,16]{0,1:T(8,128)S(1)}, s32[256,16]{0,1:T(8,128)}, u32[]{:S(2)}) copy-start(s32[256,16]{0,1:T(8,128)} %param.15) | copy-start | bytes 49156
  74.1 39.4 %copy-start.13 = (s32[1,128]{1,0:T(1,128)S(1)}, s32[1,128]{1,0:T(1,128)}, u32[]{:S(2)}) copy-start(s32[1,128]{1,0:T(1,128)} %counts_ref.1) | copy-start | bytes 1540
  74.1 37.2 %collective-permute-start.17 = (bf16[272,1024]{1,0:T(8,128)(2,1)S(1)}, bf16[272,1024]{1,0:T(8,128)(2,1)S(1)}, u32[]{:S(2)}, u32[]{:S(2)}) collective-permute-start(bf16[272,1024]{1,0:T(8,128)(2,1)S(1)} %shard_map.153.own_ref), channel_id=1, source_target_pairs={{0,8},{4,36},{8,16},{12,44},{16,24},{20,52},{24,0},{28,60},{32,40}... | collective-permute-start | bytes 1671176 | tf_op jit(solution)/shard_map/ppermute | solution.py:537
  82.1 1.0 copy-start.14
  83.1 10.0 %collective-permute-start.20 = (bf16[256,1024]{1,0:T(8,128)(2,1)}, bf16[256,1024]{1,0:T(8,128)(2,1)}, u32[]{:S(2)}, u32[]{:S(2)}) collective-permute-start(bf16[256,1024]{1,0:T(8,128)(2,1)} %get-tuple-element.63), channel_id=1, source_target_pairs={{0,1},{1,2},{2,3},{3,0},{4,5},{5,6},{6,7},{7,4},{8,9},{9,10},{10,1... | collective-permute-start | bytes 1572872 | tf_op jit(solution)/shard_map/ppermute | solution.py:542
  83.1 27.1 %collective-permute-start.21 = (bf16[256,1024]{1,0:T(8,128)(2,1)}, bf16[256,1024]{1,0:T(8,128)(2,1)}, u32[]{:S(2)}, u32[]{:S(2)}) collective-permute-start(bf16[256,1024]{1,0:T(8,128)(2,1)} %get-tuple-element.64), channel_id=1, source_target_pairs={{0,3},{1,0},{2,1},{3,2},{4,7},{5,4},{6,5},{7,6},{8,11},{9,8},{10,9... | collective-permute-start | bytes 1572872 | tf_op jit(solution)/shard_map/ppermute | solution.py:542
  89.9 20.2 %collective-permute-start.22 = (bf16[256,1024]{1,0:T(8,128)(2,1)}, bf16[256,1024]{1,0:T(8,128)(2,1)}, u32[]{:S(2)}, u32[]{:S(2)}) collective-permute-start(bf16[256,1024]{1,0:T(8,128)(2,1)} %get-tuple-element.65), channel_id=1, source_target_pairs={{0,2},{1,3},{2,0},{3,1},{4,6},{5,7},{6,4},{7,5},{8,10},{9,11},{10,... | collective-permute-start | bytes 1572872 | tf_op jit(solution)/shard_map/ppermute | solution.py:542
  91.7 39.9 %collective-permute-start.29 = (bf16[128,2048]{1,0:T(8,128)(2,1)S(1)}, bf16[128,2048]{1,0:T(8,128)(2,1)S(1)}, u32[]{:S(2)}, u32[]{:S(2)}) collective-permute-start(bf16[128,2048]{1,0:T(8,128)(2,1)S(1)} %shard_map.157.refs_0_), channel_id=1, source_target_pairs={{0,96},{4,28},{8,104},{12,4},{16,112},{20,12},{24,120},{28,20},{32... | collective-permute-start | bytes 1572872 | tf_op jit(solution)/shard_map/ppermute | solution.py:537
  93.1 38.6 %collective-permute-start.30 = (bf16[128,2048]{1,0:T(8,128)(2,1)S(1)}, bf16[128,2048]{1,0:T(8,128)(2,1)S(1)}, u32[]{:S(2)}, u32[]{:S(2)}) collective-permute-start(bf16[128,2048]{1,0:T(8,128)(2,1)S(1)} %shard_map.157.refs_0_), channel_id=1, source_target_pairs={{0,4},{4,0},{1,5},{5,1},{2,6},{6,2},{3,7},{7,3},{8,12},{12,8},{9,1... | collective-permute-start | bytes 1572872 | tf_op jit(solution)/shard_map/ppermute | solution.py:542
  110.2 32.0 %collective-permute-start.31 = (bf16[128,2048]{1,0:T(8,128)(2,1)S(1)}, bf16[128,2048]{1,0:T(8,128)(2,1)}, u32[]{:S(2)}, u32[]{:S(2)}) collective-permute-start(bf16[128,2048]{1,0:T(8,128)(2,1)S(1)} %collective-permute-done.27.refs_1_), channel_id=1, source_target_pairs={{0,4},{4,0},{1,5},{5,1},{2,6},{6,2},{3,7},{7,3},{8,12},{12,8},{9,1... | collective-permute-start | bytes 1572872 | tf_op jit(solution)/shard_map/ppermute | solution.py:542
  110.2 12.8 %collective-permute-start.18 = (bf16[272,1024]{1,0:T(8,128)(2,1)S(1)}, bf16[272,1024]{1,0:T(8,128)(2,1)S(1)}, u32[]{:S(2)}, u32[]{:S(2)}) collective-permute-start(bf16[272,1024]{1,0:T(8,128)(2,1)S(1)} %shard_map.153.own_ref), channel_id=1, source_target_pairs={{0,24},{4,100},{8,0},{12,108},{16,8},{20,116},{24,16},{28,124},{32... | collective-permute-start | bytes 1671176 | tf_op jit(solution)/shard_map/ppermute | solution.py:537
  111.2 14.5 %collective-permute-start.19 = (bf16[272,1024]{1,0:T(8,128)(2,1)S(1)}, bf16[272,1024]{1,0:T(8,128)(2,1)S(1)}, u32[]{:S(2)}, u32[]{:S(2)}) collective-permute-start(bf16[272,1024]{1,0:T(8,128)(2,1)S(1)} %shard_map.153.own_ref), channel_id=1, source_target_pairs={{0,16},{4,68},{8,24},{12,76},{16,0},{20,84},{24,8},{28,92},{32,48}... | collective-permute-start | bytes 1671176 | tf_op jit(solution)/shard_map/ppermute | solution.py:537
  113.5 1.2 copy-start.15
  123.0 20.4 %collective-permute-start.32 = (bf16[128,2048]{1,0:T(8,128)(2,1)S(1)}, bf16[128,2048]{1,0:T(8,128)(2,1)}, u32[]{:S(2)}, u32[]{:S(2)}) collective-permute-start(bf16[128,2048]{1,0:T(8,128)(2,1)S(1)} %collective-permute-done.28.refs_2_), channel_id=1, source_target_pairs={{0,4},{4,0},{1,5},{5,1},{2,6},{6,2},{3,7},{7,3},{8,12},{12,8},{9,1... | collective-permute-start | bytes 1572872 | tf_op jit(solution)/shard_map/ppermute | solution.py:542
  127.4 0.6 copy-start.8
  128.1 15.4 %collective-permute-start.34 = (bf16[256,1024]{1,0:T(8,128)(2,1)}, bf16[256,1024]{1,0:T(8,128)(2,1)S(1)}, u32[]{:S(2)}, u32[]{:S(2)}) collective-permute-start(bf16[256,1024]{1,0:T(8,128)(2,1)} %get-tuple-element.71.refs_0_), channel_id=1, source_target_pairs={{0,32},{4,12},{8,40},{12,20},{16,48},{20,28},{24,56},{28,4},{32,64... | collective-permute-start | bytes 1572872 | tf_op jit(solution)/shard_map/ppermute | solution.py:537
  131.7 13.4 %collective-permute-start.35 = (bf16[256,1024]{1,0:T(8,128)(2,1)}, bf16[256,1024]{1,0:T(8,128)(2,1)}, u32[]{:S(2)}, u32[]{:S(2)}) collective-permute-start(bf16[256,1024]{1,0:T(8,128)(2,1)} %get-tuple-element.71.refs_0_), channel_id=1, source_target_pairs={{0,64},{4,20},{8,72},{12,28},{16,80},{20,4},{24,88},{28,12},{32,96... | collective-permute-start | bytes 1572872 | tf_op jit(solution)/shard_map/ppermute | solution.py:537
  131.7 0.8 copy-start.2
  132.5 12.6 %collective-permute-start.36 = (bf16[256,1024]{1,0:T(8,128)(2,1)}, bf16[256,1024]{1,0:T(8,128)(2,1)}, u32[]{:S(2)}, u32[]{:S(2)}) collective-permute-start(bf16[256,1024]{1,0:T(8,128)(2,1)} %get-tuple-element.71.refs_0_), channel_id=1, source_target_pairs={{0,96},{4,28},{8,104},{12,4},{16,112},{20,12},{24,120},{28,20},{32... | collective-permute-start | bytes 1572872 | tf_op jit(solution)/shard_map/ppermute | solution.py:537
  134.9 23.7 %all-to-all-start = ((bf16[128,24,128]{2,1,0:T(8,128)(2,1)}), bf16[128,24,128]{2,1,0:T(8,128)(2,1)}, u32[]{:S(2)}, u32[]{:S(2)}) async-start(bf16[128,24,128]{2,1,0:T(8,128)(2,1)} %get-tuple-element.68), calls=%async_computation | async-start | bytes 1572864 | tf_op jit(solution)/shard_map/all_to_all | solution.py:644
  142.2 5.7 %collective-permute-start.33 = (bf16[128,2048]{1,0:T(8,128)(2,1)S(1)}, bf16[128,2048]{1,0:T(8,128)(2,1)S(1)}, u32[]{:S(2)}, u32[]{:S(2)}) collective-permute-start(bf16[128,2048]{1,0:T(8,128)(2,1)S(1)} %collective-permute-done.29.refs_3_), channel_id=1, source_target_pairs={{0,4},{4,0},{1,5},{5,1},{2,6},{6,2},{3,7},{7,3},{8,12},{12,8},{9,1... | collective-permute-start | bytes 1572872 | tf_op jit(solution)/shard_map/ppermute | solution.py:542
  143.4 9.0 %collective-permute-start.37 = (bf16[256,1024]{1,0:T(8,128)(2,1)}, bf16[256,1024]{1,0:T(8,128)(2,1)S(1)}, u32[]{:S(2)}, u32[]{:S(2)}) collective-permute-start(bf16[256,1024]{1,0:T(8,128)(2,1)} %get-tuple-element.71.refs_0_), channel_id=1, source_target_pairs={{0,4},{4,0},{1,5},{5,1},{2,6},{6,2},{3,7},{7,3},{8,12},{12,8},{9,1... | collective-permute-start | bytes 1572872 | tf_op jit(solution)/shard_map/ppermute | solution.py:542
  143.5 8.9 %collective-permute-start.38 = (bf16[256,1024]{1,0:T(8,128)(2,1)S(1)}, bf16[256,1024]{1,0:T(8,128)(2,1)S(1)}, u32[]{:S(2)}, u32[]{:S(2)}) collective-permute-start(bf16[256,1024]{1,0:T(8,128)(2,1)S(1)} %collective-permute-done.34.refs_1_), channel_id=1, source_target_pairs={{0,4},{4,0},{1,5},{5,1},{2,6},{6,2},{3,7},{7,3},{8,12},{12,8},{9,1... | collective-permute-start | bytes 1572872 | tf_op jit(solution)/shard_map/ppermute | solution.py:542
  145.1 7.3 %collective-permute-start.39 = (bf16[256,1024]{1,0:T(8,128)(2,1)}, bf16[256,1024]{1,0:T(8,128)(2,1)S(1)}, u32[]{:S(2)}, u32[]{:S(2)}) collective-permute-start(bf16[256,1024]{1,0:T(8,128)(2,1)} %collective-permute-done.35.refs_2_), channel_id=1, source_target_pairs={{0,4},{4,0},{1,5},{5,1},{2,6},{6,2},{3,7},{7,3},{8,12},{12,8},{9,1... | collective-permute-start | bytes 1572872 | tf_op jit(solution)/shard_map/ppermute | solution.py:542
  145.1 7.3 %collective-permute-start.40 = (bf16[256,1024]{1,0:T(8,128)(2,1)}, bf16[256,1024]{1,0:T(8,128)(2,1)S(1)}, u32[]{:S(2)}, u32[]{:S(2)}) collective-permute-start(bf16[256,1024]{1,0:T(8,128)(2,1)} %collective-permute-done.36.refs_3_), channel_id=1, source_target_pairs={{0,4},{4,0},{1,5},{5,1},{2,6},{6,2},{3,7},{7,3},{8,12},{12,8},{9,1... | collective-permute-start | bytes 1572872 | tf_op jit(solution)/shard_map/ppermute | solution.py:542
  147.9 8.2 %collective-permute-start.23 = (f32[32,1024]{1,0:T(8,128)S(1)}, f32[32,1024]{1,0:T(8,128)S(1)}, u32[]{:S(2)}, u32[]{:S(2)}) collective-permute-start(f32[32,1024]{1,0:T(8,128)S(1)} %get-tuple-element.70), channel_id=1, source_target_pairs={{0,4},{4,0},{1,5},{5,1},{2,6},{6,2},{3,7},{7,3},{8,12},{12,8},{9,1... | collective-permute-start | bytes 393224 | tf_op jit(solution)/shard_map/ppermute | solution.py:542
  147.9 1.0 copy-start.3
  150.4 2.0 %copy-start = (bf16[1024,2048]{1,0:T(8,128)(2,1)}, bf16[1024,2048]{1,0:T(8,128)(2,1)S(1)}, u32[]{:S(2)}) copy-start(bf16[1024,2048]{1,0:T(8,128)(2,1)S(1)} %shard_map.158.held_hbm) | copy-start | bytes 12582916
  154.1 2.0 %copy-start.1 = (bf16[1024,2048]{1,0:T(8,128)(2,1)}, bf16[1024,2048]{1,0:T(8,128)(2,1)S(1)}, u32[]{:S(2)}) copy-start(bf16[1024,2048]{1,0:T(8,128)(2,1)S(1)} %shard_map.159.grad_hbm) | copy-start | bytes 12582916
  156.1 2.5 %copy-start.19 = (f32[32,1024]{1,0:T(8,128)}, f32[32,1024]{1,0:T(8,128)S(1)}, u32[]{:S(2)}) copy-start(f32[32,1024]{1,0:T(8,128)S(1)} %collective-permute-done.23.theirs_ref) | copy-start | bytes 393220
